TPU v7x, 256 devices: a whole 4x4x8 slice. The times are simulated.
256 devices in a mesh: cols: 32 (over x, z_hi, y), params: 8 (over z_lo, core).
Axes of the slice: x: 4, y: 4, z: 8 (z_hi: 2, z_lo: 4; z = z_hi * 4 + z_lo), core: 2. Of those that a mesh axis runs over, the one named last changes fastest.
Arguments:
- concentration: float32 [128, 32768], P(None, ('cols', 'params')), may hold values from 0.2 to 5
- emissions: float32 [128, 32768], P(None, ('cols', 'params')), may hold values from 0 to 1
- rate_table: float32 [8, 16, 16], replicated, may hold values from 0.01 to 0.3
- species_order: int32 [128], replicated, may hold values from 0 to 127, each once
- sensitivity: float32 [16, 128, 64, 4, 128], P('params', None, 'cols'), may hold values from -6 to 6
- source_terms: bfloat16 [16, 128, 64, 4, 128], P('params', None, 'cols'), may hold values from 0 to 2
- courant_x: float32 [64, 4, 128], P('cols'), may hold values from 0.05 to 0.24
- upwind_x: int32 [64, 4, 128], P('cols'), may hold values from 0 to 1
- courant_y: float32 [64, 4, 128], P('cols'), may hold values from 0.05 to 0.24
- upwind_y: int32 [64, 4, 128], P('cols'), may hold values from 0 to 1
Outputs:
- new_concentration: float32 [128, 32768], P(None, ('cols', 'params'))
- new_sensitivity: float32 [16, 128, 64, 4, 128], P('params', None, 'cols')
- sensitivity_burden: float32 [16, 128], P('params')
- species_burden: float32 [128], replicated
Inputs may be any that keep to these rules, and one draw needn't show every extreme that they name: `species_order`: each species appears exactly once. `upwind_x`: 1 means the wind blows toward higher indices through the face. `upwind_y`: 1 means the wind blows toward higher indices through the face.
All inputs are finite; a program needn't handle non-finite values.
Results may differ from a plain program's by a relative error of at most 0.0016.
Values may be sent and summed in bfloat16 or wider, within the bound.
No kernel may reach another device: no remote copies, remote signals or barrier semaphores. Data moves between devices by JAX's collectives and lax.ppermute only.
A program may use at most 128 MiB of HBM per device.

v0:
```python
import jax
import jax.numpy as jnp
from jax import lax
from jax.sharding import Mesh
from jax.sharding import PartitionSpec as P

SUBSTEPS = 2
COLS = ("cols_0", "cols_1", "cols_2")
PARAMS = ("params_0", "params_1")
COLS_PARAMS = ("cols_0", "cols_1", "cols_2", "params_0", "params_1")


def for_sending(value):

    def short(part):
        return part.astype(jnp.bfloat16) if part.dtype == jnp.float32 else part

    return jax.tree.map(short, value)


def passed_along(value, axis, by):
    devices = lax.axis_size(axis)
    pairs = [(i, i + by) for i in range(devices) if 0 <= i + by < devices]
    return lax.ppermute(value, axis, pairs)


def from_everyone(value, axis):
    devices = lax.axis_size(axis)
    return lax.all_to_all(
        jnp.broadcast_to(value[None], (devices, *value.shape)), axis, 0, 0, tiled=True
    )


def over_copies(value, axis):
    everything = from_everyone(value, axis)
    return jnp.sum(everything, axis=0)


def one_axis_at_a_time(value, axes):
    for axis in axes:
        value = lax.psum(value, axis)
    return value


def invert_blocks(matrix):
    size = matrix.shape[1]
    positions = jnp.arange(size)

    def eliminate(pivot_index, current):
        pivot = 1.0 / current[:, pivot_index, pivot_index, :]
        pivot_row = current[:, pivot_index, :, :] * pivot[:, None, :]
        pivot_row = jnp.where(
            (positions == pivot_index)[None, :, None], pivot[:, None, :], pivot_row
        )
        column = current[:, :, pivot_index, :]
        updated = current - column[:, :, None, :] * pivot_row[:, None, :, :]
        updated = jnp.where(
            (positions == pivot_index)[None, None, :, None],
            -column[:, :, None, :] * pivot[:, None, None, :],
            updated,
        )
        updated = jnp.where(
            (positions == pivot_index)[None, :, None, None], pivot_row[:, None, :, :], updated
        )
        return updated

    return lax.fori_loop(0, size, eliminate, matrix)


def build_factors(conc_cells, species_order, rate_table):
    block_count, block_width = (rate_table.shape[0], rate_table.shape[1])
    ordered = jnp.take(conc_cells, species_order, axis=0).reshape(block_count, block_width, -1)
    coupling = rate_table[:, :, :, None] * ordered[:, None, :, :]
    row_total = jnp.sum(coupling, axis=2)
    positions = jnp.arange(block_width)
    identity = (positions[:, None] == positions[None, :]).astype(jnp.float32)
    system = identity[None, :, :, None] * (1.0 + row_total)[:, :, None, :] - coupling
    return invert_blocks(system).astype(jnp.bfloat16)


def apply_blocks(factors, values):
    result = jnp.zeros(values.shape, jnp.float32)
    for column_index in range(factors.shape[2]):
        result = (
            result
            + factors[:, :, column_index, :].astype(jnp.float32)[None]
            * values[:, :, column_index, :][:, :, None, :]
        )
    return result


def across_flux(tracer, courant_y, upwind_y):
    before_y = jnp.concatenate([jnp.zeros_like(tracer[..., :1]), tracer[..., :-1]], axis=4)
    lower_y = courant_y * jnp.where(upwind_y == 1, before_y, -tracer)
    upper_y = jnp.concatenate([lower_y[..., 1:], jnp.zeros_like(lower_y[..., :1])], axis=4)
    return lower_y - upper_y


def advect_paired(tracer, weight_up, weight_down, courant_x, upwind_x, courant_y, upwind_y):
    groups, species, planes, layers, across = tracer.shape
    stacked = groups * species
    outgoing = jnp.concatenate(
        [
            tracer[:, :, :1].reshape(stacked, 1, layers, across),
            weight_up[None, :1],
            weight_down[None, :1],
        ],
        axis=0,
    )
    left_plane = passed_along(for_sending(tracer[:, :, -1:]), COLS, 1)
    incoming = passed_along(for_sending(outgoing), COLS, -1).astype(outgoing.dtype)
    next_first = incoming[:stacked].reshape(groups, species, 1, layers, across)
    right_plane = (
        incoming[stacked : stacked + 1] * tracer[:, :, -1:]
        - incoming[stacked + 1 : stacked + 2] * next_first
    )
    before_x = jnp.concatenate([left_plane, tracer[:, :, :-1]], axis=2)
    lower_x = courant_x * jnp.where(upwind_x == 1, before_x, -tracer)
    upper_x = jnp.concatenate([lower_x[:, :, 1:], right_plane], axis=2)
    return tracer + lower_x - upper_x + across_flux(tracer, courant_y, upwind_y)


def shards(
    concentration,
    emissions,
    rate_table,
    species_order,
    sensitivity,
    source_terms,
    courant_x,
    upwind_x,
    courant_y,
    upwind_y,
):
    block_count, block_width = (rate_table.shape[0], rate_table.shape[1])
    groups, species = (sensitivity.shape[0], sensitivity.shape[1])
    planes, layers, across = (sensitivity.shape[2], sensitivity.shape[3], sensitivity.shape[4])
    cell_count = planes * layers * across
    inverse = jnp.argsort(species_order)
    own_factors = build_factors(concentration, species_order, rate_table)
    base_side = jnp.take(concentration + emissions, species_order, axis=0).reshape(
        block_count, block_width, -1
    )
    new_base = apply_blocks(own_factors, base_side[None])[0].reshape(species, -1)
    new_concentration = jnp.take(new_base, inverse, axis=0)
    tracer = sensitivity
    weight_up = jnp.where(upwind_x == 1, courant_x, 0.0)
    weight_down = jnp.where(upwind_x == 1, 0.0, courant_x)
    for substep in range(SUBSTEPS):
        tracer = advect_paired(
            tracer, weight_up, weight_down, courant_x, upwind_x, courant_y, upwind_y
        )
    right_side = jnp.take(tracer + source_terms.astype(jnp.float32), species_order, axis=1)
    right_side = right_side.reshape(groups, block_count, block_width, cell_count)
    result = apply_blocks(lax.all_gather(own_factors, PARAMS, axis=3, tiled=True), right_side)
    new_sensitivity = jnp.take(
        result.reshape(groups, species, planes, layers, across), inverse, axis=1
    )
    partial_sens = jnp.sum(new_sensitivity, axis=(2, 3, 4))
    partial_conc = jnp.sum(new_concentration, axis=1)
    total_cells = cell_count * lax.axis_size(COLS)
    sens_total = over_copies(partial_sens, COLS)
    conc_total = one_axis_at_a_time(partial_conc, COLS_PARAMS)
    return (new_concentration, new_sensitivity, sens_total / total_cells, conc_total / total_cells)


def solution(mesh):
    split = Mesh(
        mesh.devices.reshape(4, 2, 4, 4, 2), ("cols_0", "cols_1", "cols_2", "params_0", "params_1")
    )
    in_specs = (
        P(None, COLS_PARAMS),
        P(None, COLS_PARAMS),
        P(),
        P(),
        P(PARAMS, None, COLS, None, None),
        P(PARAMS, None, COLS, None, None),
        P(COLS, None, None),
        P(COLS, None, None),
        P(COLS, None, None),
        P(COLS, None, None),
    )
    out_specs = (P(None, COLS_PARAMS), P(PARAMS, None, COLS, None, None), P(PARAMS, None), P())
    return jax.shard_map(
        shards, mesh=split, in_specs=in_specs, out_specs=out_specs, check_vma=False
    )
```

profile of v0, /device:TPU:1, one launch (start us, length us, event | category | flops | bytes accessed | tf_op | source)
XLA Modules:
  0.0 210.1 jit_solution(7079474087047705380)
XLA Ops:
  8.5 1.5 gather_fusion
  14.2 8.4 %while.14 = (s32[]{:T(128)}, f32[8,16,16,128]{3,2,1,0:T(8,128)S(1)}, s32[]{:T(128)}) while((s32[]{:T(128)}, f32[8,16,16,128]{3,2,1,0:T(8,128)S(1)}, s32[]{:T(128)}) %tuple.117), condition=%wide.region_2.4_spmd.clone, body=%wide.region_1.3_spmd.clone.sunk | while | flops 1115154 | bytes 2637941 | solution.py:67
  23.8 4.0 %collective-permute-start = (bf16[2,128,1,4,128]{4,3,2,1,0:T(4,128)(2,1)S(1)}, bf16[2,128,1,4,128]{4,3,2,1,0:T(4,128)(2,1)S(1)}, u32[]{:S(2)}, u32[]{:S(2)}) collective-permute-start(bf16[2,128,1,4,128]{4,3,2,1,0:T(4,128)(2,1)S(1)} %get-tuple-element.145), channel_id=1, source_target_pairs={{0,8},{8,16},{16,24},{24,32},{32,40},{40,48},{48,56},{56,64},{64,7... | collective-permute-start | bytes 786440 | tf_op jit(solution)/shard_map/ppermute | solution.py:24
  29.4 2.5 %sort.17 = (s32[128]{0:T(128)}, s32[128]{0:T(128)S(1)}) sort(s32[128]{0:T(128)S(1)} %copy-done.15, s32[128]{0:T(128)S(1)} %iota.23), dimensions={0}, to_apply=%region_3.5 | sort | flops 896 | bytes 2048 | tf_op jit(solution)/shard_map/jit(argsort)/sort | solution.py:139
  31.9 4.0 %slice_convert_fusion.33 = (f32[8,16,1,128]{3,2,1,0:T(1,128)S(1)}, f32[8,16,1,128]{3,2,1,0:T(1,128)S(1)}, f32[8,16,1,128]{3,2,1,0:T(1,128)S(1)}, f32[8,16,1,128]...) fusion(bf16[8,16,16,128]{3,2,1,0:T(8,128)(2,1)} %convert_elemen, ...), kind=kLoop, calls=%fused_computation.83 | loop fusion | flops 262144 | bytes 1572864 | tf_op jit(solution)/shard_map/convert_element_type | solution.py:86
  39.9 3.2 %collective-permute-start.2 = (bf16[2,128,1,4,128]{4,3,2,1,0:T(4,128)(2,1)S(1)}, bf16[2,128,1,4,128]{4,3,2,1,0:T(4,128)(2,1)S(1)}, u32[]{:S(2)}, u32[]{:S(2)}) collective-permute-start(bf16[2,128,1,4,128]{4,3,2,1,0:T(4,128)(2,1)S(1)} %get-tuple-element.139), channel_id=1, source_target_pairs={{0,8},{8,16},{16,24},{24,32},{32,40},{40,48},{48,56},{56,64},{64,7... | collective-permute-start | bytes 786440 | tf_op jit(solution)/shard_map/ppermute | solution.py:24
  46.1 33.6 %psum.35 = f32[128]{0:T(128)S(1)} all-reduce(f32[128]{0:T(128)S(1)} %get-tuple-element.101), channel_id=1, replica_groups=mesh['cols_0'=4,'cols_1'=2,'cols_2'=4,'params_0'=4,'params_1'=2] {'cols_0'}, use_global_device_ids=true, to_apply=%region_7.10 | all-reduce | flops 128 | bytes 1024 | tf_op jit(solution)/shard_map/psum | solution.py:41
  79.8 7.8 %psum.36 = f32[128]{0:T(128)S(1)} all-reduce(f32[128]{0:T(128)S(1)} %psum.35), channel_id=1, replica_groups=mesh['cols_0'=4,'cols_1'=2,'cols_2'=4,'params_0'=4,'params_1'=2] {'cols_1'}, use_global_device_ids=true, to_apply=%region_8.11 | all-reduce | flops 128 | bytes 1024 | tf_op jit(solution)/shard_map/psum | solution.py:41
  87.6 6.5 %psum.37 = f32[128]{0:T(128)S(1)} all-reduce(f32[128]{0:T(128)S(1)} %psum.36), channel_id=1, replica_groups=mesh['cols_0'=4,'cols_1'=2,'cols_2'=4,'params_0'=4,'params_1'=2] {'cols_2'}, use_global_device_ids=true, to_apply=%region_9.12 | all-reduce | flops 128 | bytes 1024 | tf_op jit(solution)/shard_map/psum | solution.py:41
  94.1 16.4 %psum.38 = f32[128]{0:T(128)S(1)} all-reduce(f32[128]{0:T(128)S(1)} %psum.37), channel_id=1, replica_groups=mesh['cols_0'=4,'cols_1'=2,'cols_2'=4,'params_0'=4,'params_1'=2] {'param..., use_global_device_ids=true, to_apply=%region_10.13 | all-reduce | flops 128 | bytes 1024 | tf_op jit(solution)/shard_map/psum | solution.py:41
  110.5 7.2 %psum.39 = f32[128]{0:T(128)S(1)} all-reduce(f32[128]{0:T(128)S(1)} %psum.38), channel_id=1, replica_groups=mesh['cols_0'=4,'cols_1'=2,'cols_2'=4,'params_0'=4,'params_1'=2] {'param..., use_global_device_ids=true, to_apply=%region_11.14 | all-reduce | flops 128 | bytes 1024 | tf_op jit(solution)/shard_map/psum | solution.py:41
  134.6 1.5 mul.810
  137.0 1.5 mul.815
  139.4 1.5 mul.820
  141.9 1.5 mul.825
  149.2 1.5 mul.840
  150.7 1.5 mul.845
  152.3 1.7 mul.850
  154.2 1.5 mul.855
  155.8 1.5 mul.860
  160.4 18.7 %slice_convert_fusion.15 = (f32[8,16,1,1024]{3,2,1,0:T(1,128)}, f32[8,16,1,1024]{3,2,1,0:T(1,128)}, f32[8,16,1,1024]{3,2,1,0:T(1,128)}, f32[8,16,1,1024]{3,2,1,0...) fusion(bf16[8,16,16,1024]{3,2,1,0:T(8,128)(2,1)} %all-gather.2., ...), kind=kLoop, calls=%fused_computation.43 | loop fusion | flops 2097152 | bytes 12582912 | tf_op jit(solution)/shard_map/convert_element_type | solution.py:86
  179.2 5.6 %multiply_add_fusion = f32[2,128,1,8,128]{4,3,2,1,0:T(8,128)S(1)} fusion(f32[2,128,1,8,128]{4,3,2,1,0:T(8,128)} %bitcast.300, f32[2,128,1,8,128]{4,3,2,1,0:T(8,128)} %bitcast.299, f32[2,128,1,8,128]{4,3,2,1,0:T(8,128)} %bitcast.298, f32[2,128,1,8,128]{4,3,2,1,0:T(8,128)} %bitcast.297, f32[2,128,1,8,128]{4,3,2,1,0:T(8,128)S(1)} %bitcast.296, ...), kind=kLoop, calls=%fused_computation.25 | loop fusion | flops 8126464 | bytes 26214400 | tf_op jit(solution)/shard_map/add | solution.py:85
  187.5 4.0 %all-to-all-start = ((f32[32,2,128]{2,1,0:T(2,128)}), f32[32,2,128]{2,1,0:T(2,128)S(1)}, u32[]{:S(2)}, u32[]{:S(2)}) async-start(f32[32,2,128]{2,1,0:T(2,128)} %broadcast_in_dim.219), calls=%async_computation | async-start | bytes 65536 | tf_op jit(solution)/shard_map/all_to_all | solution.py:29
  193.2 9.5 %all-to-all-done = f32[32,2,128]{2,1,0:T(2,128)S(1)} async-done(((f32[32,2,128]{2,1,0:T(2,128)}), f32[32,2,128]{2,1,0:T(2,128)S(1)}, u32[]{:S(2)}, u32[]{:S(2)}) %all-to-all-start) | async-done | bytes 32800 | tf_op jit(solution)/shard_map/all_to_all | solution.py:29
  (215 shorter events, 56.5 us)
Async XLA Ops:
  7.2 153.2 %all-gather.2.cloned.1.call-start = ((), (), s32[]{:S(2)}) async-start(), calls=%async_computation.1 | async-start | bytes 4718592 | tf_op jit(solution)/shard_map/all_gather | solution.py:155
  14.2 9.4 %copy-start = (f32[2,128,2,4,128]{4,3,2,1,0:T(4,128)S(1)}, f32[2,128,2,4,128]{4,3,2,1,0:T(4,128)}, u32[]{:S(2)}) copy-start(f32[2,128,2,4,128]{4,3,2,1,0:T(4,128)} %param.20) | copy-start | bytes 3145732
  14.2 13.6 %copy-start.13 = (s32[2,4,128]{2,1,0:T(4,128)S(1)}, s32[2,4,128]{2,1,0:T(4,128)}, u32[]{:S(2)}) copy-start(s32[2,4,128]{2,1,0:T(4,128)} %param.25) | copy-start | bytes 12292
  14.2 13.6 %copy-start.14 = (s32[2,4,128]{2,1,0:T(4,128)S(1)}, s32[2,4,128]{2,1,0:T(4,128)}, u32[]{:S(2)}) copy-start(s32[2,4,128]{2,1,0:T(4,128)} %param.23) | copy-start | bytes 12292
  14.2 13.6 %copy-start.11 = (f32[2,4,128]{2,1,0:T(4,128)S(1)}, f32[2,4,128]{2,1,0:T(4,128)}, u32[]{:S(2)}) copy-start(f32[2,4,128]{2,1,0:T(4,128)} %param.22) | copy-start | bytes 12292
  14.2 15.2 %copy-start.15 = (s32[128]{0:T(128)S(1)}, s32[128]{0:T(128)}, u32[]{:S(2)}) copy-start(s32[128]{0:T(128)} %param.19) | copy-start | bytes 1540
  23.7 13.6 %copy-start.12 = (f32[2,4,128]{2,1,0:T(4,128)S(1)}, f32[2,4,128]{2,1,0:T(4,128)}, u32[]{:S(2)}) copy-start(f32[2,4,128]{2,1,0:T(4,128)} %param.24) | copy-start | bytes 12292
  23.8 12.2 %collective-permute-start = (bf16[2,128,1,4,128]{4,3,2,1,0:T(4,128)(2,1)S(1)}, bf16[2,128,1,4,128]{4,3,2,1,0:T(4,128)(2,1)S(1)}, u32[]{:S(2)}, u32[]{:S(2)}) collective-permute-start(bf16[2,128,1,4,128]{4,3,2,1,0:T(4,128)(2,1)S(1)} %get-tuple-element.145), channel_id=1, source_target_pairs={{0,8},{8,16},{16,24},{24,32},{32,40},{40,48},{48,56},{56,64},{64,7... | collective-permute-start | bytes 786440 | tf_op jit(solution)/shard_map/ppermute | solution.py:24
  28.1 8.8 %collective-permute-start.1 = (bf16[258,1,4,128]{3,2,0,1:T(4,128)(2,1)S(1)}, bf16[258,1,4,128]{3,2,0,1:T(4,128)(2,1)S(1)}, u32[]{:S(2)}, u32[]{:S(2)}) collective-permute-start(bf16[258,1,4,128]{3,2,0,1:T(4,128)(2,1)S(1)} %pad_maximum_fusion.1), channel_id=1, source_target_pairs={{8,0},{16,8},{24,16},{32,24},{40,32},{48,40},{56,48},{64,56},{72,6... | collective-permute-start | bytes 792584 | tf_op jit(solution)/shard_map/ppermute | solution.py:24
  39.9 77.8 %collective-permute-start.2 = (bf16[2,128,1,4,128]{4,3,2,1,0:T(4,128)(2,1)S(1)}, bf16[2,128,1,4,128]{4,3,2,1,0:T(4,128)(2,1)S(1)}, u32[]{:S(2)}, u32[]{:S(2)}) collective-permute-start(bf16[2,128,1,4,128]{4,3,2,1,0:T(4,128)(2,1)S(1)} %get-tuple-element.139), channel_id=1, source_target_pairs={{0,8},{8,16},{16,24},{24,32},{32,40},{40,48},{48,56},{56,64},{64,7... | collective-permute-start | bytes 786440 | tf_op jit(solution)/shard_map/ppermute | solution.py:24
  43.3 74.5 %collective-permute-start.3 = (bf16[258,1,4,128]{3,2,0,1:T(4,128)(2,1)S(1)}, bf16[258,1,4,128]{3,2,0,1:T(4,128)(2,1)S(1)}, u32[]{:S(2)}, u32[]{:S(2)}) collective-permute-start(bf16[258,1,4,128]{3,2,0,1:T(4,128)(2,1)S(1)} %pad_maximum_fusion), channel_id=1, source_target_pairs={{8,0},{16,8},{24,16},{32,24},{40,32},{48,40},{56,48},{64,56},{72,6... | collective-permute-start | bytes 792584 | tf_op jit(solution)/shard_map/ppermute | solution.py:24
  118.2 1.6 copy-start.10
  160.3 18.7 %copy-start.1 = (f32[2,128,2,4,128]{4,3,2,1,0:T(4,128)S(1)}, f32[2,128,2,4,128]{4,3,2,1,0:T(4,128)}, u32[]{:S(2)}) copy-start(f32[2,128,2,4,128]{4,3,2,1,0:T(4,128)} %mul.805) | copy-start | bytes 3145732
  160.3 18.8 %copy-start.2 = (f32[2,128,2,4,128]{4,3,2,1,0:T(4,128)S(1)}, f32[2,128,2,4,128]{4,3,2,1,0:T(4,128)}, u32[]{:S(2)}) copy-start(f32[2,128,2,4,128]{4,3,2,1,0:T(4,128)} %mul.810) | copy-start | bytes 3145732
  160.3 18.8 %copy-start.3 = (f32[2,128,2,4,128]{4,3,2,1,0:T(4,128)S(1)}, f32[2,128,2,4,128]{4,3,2,1,0:T(4,128)}, u32[]{:S(2)}) copy-start(f32[2,128,2,4,128]{4,3,2,1,0:T(4,128)} %mul.815) | copy-start | bytes 3145732
  160.3 18.8 %copy-start.4 = (f32[2,128,2,4,128]{4,3,2,1,0:T(4,128)S(1)}, f32[2,128,2,4,128]{4,3,2,1,0:T(4,128)}, u32[]{:S(2)}) copy-start(f32[2,128,2,4,128]{4,3,2,1,0:T(4,128)} %mul.820) | copy-start | bytes 3145732
  160.4 18.8 %copy-start.5 = (f32[2,128,2,4,128]{4,3,2,1,0:T(4,128)S(1)}, f32[2,128,2,4,128]{4,3,2,1,0:T(4,128)}, u32[]{:S(2)}) copy-start(f32[2,128,2,4,128]{4,3,2,1,0:T(4,128)} %mul.825) | copy-start | bytes 3145732
  160.4 18.8 %copy-start.6 = (f32[2,128,2,4,128]{4,3,2,1,0:T(4,128)S(1)}, f32[2,128,2,4,128]{4,3,2,1,0:T(4,128)}, u32[]{:S(2)}) copy-start(f32[2,128,2,4,128]{4,3,2,1,0:T(4,128)} %mul.830) | copy-start | bytes 3145732
  160.4 18.8 %copy-start.7 = (f32[2,128,2,4,128]{4,3,2,1,0:T(4,128)S(1)}, f32[2,128,2,4,128]{4,3,2,1,0:T(4,128)}, u32[]{:S(2)}) copy-start(f32[2,128,2,4,128]{4,3,2,1,0:T(4,128)} %mul.835) | copy-start | bytes 3145732
  160.4 18.8 %copy-start.8 = (f32[2,128,2,4,128]{4,3,2,1,0:T(4,128)S(1)}, f32[2,128,2,4,128]{4,3,2,1,0:T(4,128)}, u32[]{:S(2)}) copy-start(f32[2,128,2,4,128]{4,3,2,1,0:T(4,128)} %mul.840) | copy-start | bytes 3145732
  160.4 18.8 %copy-start.9 = (f32[2,128,2,4,128]{4,3,2,1,0:T(4,128)S(1)}, f32[2,128,2,4,128]{4,3,2,1,0:T(4,128)}, u32[]{:S(2)}) copy-start(f32[2,128,2,4,128]{4,3,2,1,0:T(4,128)} %mul.845) | copy-start | bytes 3145732
  187.5 15.2 %all-to-all-start = ((f32[32,2,128]{2,1,0:T(2,128)}), f32[32,2,128]{2,1,0:T(2,128)S(1)}, u32[]{:S(2)}, u32[]{:S(2)}) async-start(f32[32,2,128]{2,1,0:T(2,128)} %broadcast_in_dim.219), calls=%async_computation | async-start | bytes 65536 | tf_op jit(solution)/shard_map/all_to_all | solution.py:29
Sparse Core Ops, SparseCore 0:
  23.7 64.5 all-gather.1
where the time goes:
time: 211 us; the launch traced here: 210 us
  blocking collectives  71.6 us (34%)
  other arithmetic  51.9 us (25%)
  local copies, waits for them, and re-layouts  46.9 us (22%)
  between operations  14.8 us (7%)
  starting transfers between devices  13.9 us (7%)
  waiting for transfers between devices  10.4 us (5%)
    psum x5, blocking collectives, one_axis_at_a_time(): value = lax.psum(value, axis)  71.6 us
    mul x49, local copies, waits for them, and re-layouts, apply_blocks(): factors[:, :, column_index, :].astype(jnp.float32)[None]  37.1 us
    convert_element_type x2, other arithmetic, apply_blocks(): factors[:, :, column_index, :].astype(jnp.float32)[None]  22.7 us
    ppermute x4, starting transfers between devices, passed_along(): return lax.ppermute(value, axis, pairs)  9.82 us
    all_to_all x1, waiting for transfers between devices, from_everyone(): lax.all_to_all(jnp.broadcast_to(value[None], (devices, *value.shape)), ax...  9.46 us
    add x2, other arithmetic, apply_blocks(): result + factors[:, :, column_index, :].astype(jnp.float32)[None] * value...  5.73 us
    select_n x16, other arithmetic, eliminate(): jnp.where((positions == pivot_index)[None, :, None, None], pivot_row[:, N...  4.62 us
  transfers between devices with their start and end apart: 6, of which 2 were waited for; matrix products, arithmetic and copies ran while one was open for 26% of the time, Pallas kernels for 0%

commit v1 on v0

v1 whole, which is shorter than its diff:
```python
import functools

import jax
import jax.numpy as jnp
from jax import lax
from jax.experimental import pallas as pl
from jax.experimental.pallas import tpu as pltpu
from jax.sharding import PartitionSpec as P

ROWS, LANES = 8, 128
HIGHEST = lax.Precision.HIGHEST


def shifted(value, by, axis):
    return pltpu.roll(value, by % value.shape[axis], axis)


def coefficients(cx, ux, cy, uy, upper):
    half = ROWS // 2
    row = lax.broadcasted_iota(jnp.int32, (ROWS, LANES), 0)
    lane = lax.broadcasted_iota(jnp.int32, (ROWS, LANES), 1)
    first = row < half
    up_x = jnp.where(ux == 1, cx, 0.0)
    down_x = jnp.where(ux == 1, 0.0, cx)
    up_y = jnp.where(uy == 1, cy, 0.0)
    down_y = jnp.where(uy == 1, 0.0, cy)
    before = jnp.where(lane == 0, 0.0, up_y)
    leave = jnp.where(lane == LANES - 1, 0.0, shifted(up_y, -1, 1))
    after = jnp.where(lane == LANES - 1, 0.0, shifted(down_y, -1, 1))
    other = jnp.where(first, shifted(down_x, half, 0), up_x)
    leave_x = jnp.where(first, shifted(up_x, half, 0), upper)
    own = 1.0 - down_y - leave - down_x - leave_x
    return first, up_x, down_x, own, other, before, after


def moved(s, own, other, before, after):
    return (
        own * s
        + other * shifted(s, ROWS // 2, 0)
        + before * shifted(s, 1, 1)
        + after * shifted(s, -1, 1)
    )


def message_kernel(cx, ux, cy, uy, s_ref, right_ref, left_ref):
    half = ROWS // 2
    species = right_ref.shape[0]
    first, up_x, down_x, own, other, before, after = coefficients(
        cx[...], ux[...], cy[...], uy[...], 0.0
    )
    down = jnp.where(first, down_x, 0.0)

    def one(k, carry):
        rights, lefts = [], []
        for g in range(2):
            s = s_ref[g, k]
            t = moved(s, own, other, before, after)
            rights.append(jnp.where(first, shifted(s, half, 0), t))
            lefts.append(jnp.where(first, down * s, shifted(down * t, half, 0)))
        right_ref[k] = jnp.concatenate(rights, 0).astype(jnp.bfloat16)
        left_ref[k] = jnp.concatenate(lefts, 0).astype(jnp.bfloat16)
        return carry

    lax.fori_loop(0, species, one, 0, unroll=8)
    high = up_x.astype(jnp.bfloat16).astype(jnp.float32)
    low = up_x - high
    both = jnp.where(first, high, shifted(low, half, 0))
    left_ref[species] = jnp.concatenate([both, jnp.zeros_like(both)], 0).astype(jnp.bfloat16)


def factor_kernel(place_ref, order_ref, rate_ref, cells_ref, factor_ref, conc_ref, part_ref, m_ref, all_ref):
    n = 16
    block = pl.program_id(0)
    stride = cells_ref.shape[0] // ROWS
    species = stride // 2
    where_ = [order_ref[block * n + j] for j in range(n)]
    conc = [cells_ref[pl.ds(where_[j], ROWS, stride=stride), :] for j in range(n)]
    for i in range(n):
        total = None
        row = []
        for j in range(n):
            c = rate_ref[(block * n + i) * n + j] * conc[j]
            row.append(c)
            total = c if total is None else total + c
        for j in range(n):
            m_ref[i * n + j] = (1.0 + total) - row[j] if i == j else -row[j]

    for k in range(0, n, 2):
        x = [m_ref[k * n + j] for j in range(n)]
        y = [m_ref[(k + 1) * n + j] for j in range(n)]
        p = 1.0 / x[k]
        x = [p if j == k else x[j] * p for j in range(n)]
        e = y[k]
        y = [-(e * x[j]) if j == k else y[j] - e * x[j] for j in range(n)]
        p = 1.0 / y[k + 1]
        y = [p if j == k + 1 else y[j] * p for j in range(n)]
        e = x[k + 1]
        x = [-(e * y[j]) if j == k + 1 else x[j] - e * y[j] for j in range(n)]
        for i in range(n):
            if i in (k, k + 1):
                continue
            a = m_ref[i * n + k]
            b = m_ref[i * n + k + 1]
            for j in range(n):
                step = a * x[j] + b * y[j]
                m_ref[i * n + j] = -step if j in (k, k + 1) else m_ref[i * n + j] - step
        for j in range(n):
            m_ref[k * n + j] = x[j]
            m_ref[(k + 1) * n + j] = y[j]

    base = [
        cells_ref[pl.ds(where_[j], ROWS, stride=stride), :]
        + cells_ref[pl.ds(species + where_[j], ROWS, stride=stride), :]
        for j in range(n)
    ]
    for i in range(0, n, 2):
        sums = [None, None]
        for j in range(n):
            pair = jnp.concatenate([m_ref[i * n + j], m_ref[(i + 1) * n + j]], 0).astype(jnp.bfloat16)
            factor_ref[0, j, i // 2] = pair
            wide = pair.astype(jnp.float32)
            for h in range(2):
                term = wide[h * ROWS : (h + 1) * ROWS] * base[j]
                sums[h] = term if sums[h] is None else sums[h] + term
        for h in range(2):
            all_ref[pl.ds(pl.multiple_of(where_[i + h] * ROWS, ROWS), ROWS), :] = sums[h]

    @pl.when(block == pl.num_programs(0) - 1)
    def _():
        conc_ref[...] = all_ref[pl.ds(place_ref[0], species, stride=ROWS), :]
        rows = jnp.sum(all_ref[...].reshape(species, ROWS, LANES), axis=1)
        ones = jnp.ones((ROWS, LANES), jnp.float32)
        part_ref[...] = lax.dot_general(ones, rows, (((1,), (1,)), ((), ())), precision=HIGHEST)


def apply_kernel(
    order_ref, cx, ux, cy, uy, s_ref, source_ref, from_left_ref, from_right_ref, factor_ref, out_ref, part_ref
):
    n = 16
    half = ROWS // 2
    block = pl.program_id(0)
    species = from_left_ref.shape[0]
    extra = from_right_ref[species].astype(jnp.float32)[:ROWS]
    upper = extra + shifted(extra, half, 0)
    first, up_x, down_x, own, other, before, after = coefficients(
        cx[...], ux[...], cy[...], uy[...], upper
    )
    values = [[None] * n, [None] * n]
    for j in range(n):
        k = order_ref[block * n + j]
        left = from_left_ref[k].astype(jnp.float32)
        right = from_right_ref[k].astype(jnp.float32)
        for g in range(2):
            a = left[g * ROWS : (g + 1) * ROWS]
            b = right[g * ROWS : (g + 1) * ROWS]
            inflow = up_x * a
            halo_0 = jnp.where(first, inflow, shifted(b, half, 0))
            halo_1 = jnp.where(first, up_x * (shifted(a, half, 0) - inflow), b)
            s = s_ref[g, k]
            s = moved(s, own, other, before, after) + halo_0
            s = moved(s, own, other, before, after) + halo_1
            values[g][j] = s + source_ref[g, k].astype(jnp.float32)
    for i in range(0, n, 2):
        sums = [[None, None], [None, None]]
        for j in range(n):
            wide = factor_ref[0, j, i // 2].astype(jnp.float32)
            for h in range(2):
                f = wide[h * ROWS : (h + 1) * ROWS]
                for g in range(2):
                    term = f * values[g][j]
                    sums[g][h] = term if sums[g][h] is None else sums[g][h] + term
        for h in range(2):
            k = order_ref[block * n + i + h]
            for g in range(2):
                out_ref[g, k] = sums[g][h]

    @pl.when(block == pl.num_programs(0) - 1)
    def _():
        ones = jnp.ones((ROWS, LANES), jnp.float32)
        for g in range(2):
            rows = jnp.sum(out_ref[g], axis=1)
            part_ref[g] = lax.dot_general(ones, rows, (((1,), (1,)), ((), ())), precision=HIGHEST)


def passed_along(value, by):
    devices = lax.axis_size("cols")
    pairs = [(i, i + by) for i in range(devices) if 0 <= i + by < devices]
    return lax.ppermute(value, "cols", pairs)


VMEM = pl.BlockSpec(memory_space=pltpu.VMEM)
SMEM = pl.BlockSpec(memory_space=pltpu.SMEM)


def whole(shape):
    return pl.BlockSpec(shape, lambda b: (0,) * len(shape))


def shards(
    concentration,
    emissions,
    rate_table,
    species_order,
    sensitivity,
    source_terms,
    courant_x,
    upwind_x,
    courant_y,
    upwind_y,
):
    blocks, width = rate_table.shape[:2]
    groups, species, planes, layers, across = sensitivity.shape
    cells = planes * layers * across
    members = lax.axis_size("params")
    s = sensitivity.reshape(groups, species, ROWS, LANES)
    source = source_terms.reshape(groups, species, ROWS, LANES)
    winds = [w.reshape(ROWS, LANES) for w in (courant_x, upwind_x, courant_y, upwind_y)]

    to_right, to_left = pl.pallas_call(
        message_kernel,
        out_shape=(
            jax.ShapeDtypeStruct((species, 2 * ROWS, LANES), jnp.bfloat16),
            jax.ShapeDtypeStruct((species + 1, 2 * ROWS, LANES), jnp.bfloat16),
        ),
        in_specs=[VMEM] * 5,
        out_specs=(VMEM, VMEM),
        name="messages",
    )(*winds, s)
    from_left = passed_along(to_right, 1)
    from_right = passed_along(to_left, -1)

    both = jnp.stack([concentration, emissions])
    gathered = lax.all_gather(both, "params", axis=0).reshape(members * 2 * species, LANES)
    place = lax.axis_index("params").astype(jnp.int32).reshape(1)
    factors, new_concentration, conc_part = pl.pallas_call(
        factor_kernel,
        grid=(blocks,),
        out_shape=(
            jax.ShapeDtypeStruct((blocks, width, width // 2, 2 * ROWS, LANES), jnp.bfloat16),
            jax.ShapeDtypeStruct((species, LANES), jnp.float32),
            jax.ShapeDtypeStruct((ROWS, species), jnp.float32),
        ),
        in_specs=[SMEM, SMEM, SMEM, whole(gathered.shape)],
        out_specs=(
            pl.BlockSpec((1, width, width // 2, 2 * ROWS, LANES), lambda b: (b, 0, 0, 0, 0)),
            whole((species, LANES)),
            whole((ROWS, species)),
        ),
        scratch_shapes=[
            pltpu.VMEM((width * width, ROWS, LANES), jnp.float32),
            pltpu.VMEM((species * ROWS, LANES), jnp.float32),
        ],
        name="factors",
    )(place, species_order, rate_table.reshape(-1), gathered)

    new_sens, sens_part = pl.pallas_call(
        apply_kernel,
        grid=(blocks,),
        out_shape=(
            jax.ShapeDtypeStruct((groups, species, ROWS, LANES), jnp.float32),
            jax.ShapeDtypeStruct((groups, ROWS, species), jnp.float32),
        ),
        in_specs=[SMEM]
        + [whole((ROWS, LANES))] * 4
        + [whole(v.shape) for v in (s, source, from_left, from_right)]
        + [pl.BlockSpec((1, width, width // 2, 2 * ROWS, LANES), lambda b: (b, 0, 0, 0, 0))],
        out_specs=(whole((groups, species, ROWS, LANES)), whole((groups, ROWS, species))),
        name="apply",
    )(species_order, *winds, s, source, from_left, from_right, factors)

    parts = jnp.concatenate([sens_part[:, 0], conc_part[:1]], axis=0)
    tiles = lax.axis_size("cols")
    everything = lax.all_to_all(
        jnp.broadcast_to(parts[None], (tiles, *parts.shape)), "cols", 0, 0, tiled=True
    )
    means = jnp.sum(everything, axis=0) / (cells * tiles)
    return (
        new_concentration,
        new_sens.reshape(sensitivity.shape),
        means[:groups],
        means[groups],
    )


def solution(mesh):
    in_specs = (
        P(None, ("cols", "params")),
        P(None, ("cols", "params")),
        P(),
        P(),
        P("params", None, "cols"),
        P("params", None, "cols"),
        P("cols"),
        P("cols"),
        P("cols"),
        P("cols"),
    )
    out_specs = (P(None, ("cols", "params")), P("params", None, "cols"), P("params"), P())
    return jax.shard_map(shards, mesh=mesh, in_specs=in_specs, out_specs=out_specs, check_vma=False)
```

time: 211 us -> 116 us (0.55)
  other arithmetic: 51.9 us -> 1.59 us
  blocking collectives: 71.6 us -> 26.6 us
  local copies, waits for them, and re-layouts: 46.9 us -> 4.95 us
  Pallas kernels: 0 us -> 28.3 us
  waiting for transfers between devices: 10.4 us -> 32.5 us
  starting transfers between devices: 13.9 us -> 6 us
    psum x5 -> x0, blocking collectives: 71.6 us -> none  [one_axis_at_a_time(): value = lax.psum(value, axis)]
    mul x51 -> x0, local copies, waits for them, and re-layouts: 37.1 us -> none  [the longest x49 37.1 us: apply_blocks(): factors[:, :, column_index, :].astype(jnp.float32)[None]]
    all_gather x1, waiting for transfers between devices: 0.01 us -> 32.5 us  [shards(): lax.all_gather(both, 'params', axis=0).reshape(members * 2 * species, LANES)]
    pallas_call x0 -> x3, Pallas kernels: none -> 28.3 us  [the longest x1 15.4 us: shards(): pl.pallas_call(factor_kernel, grid=(blocks,), out_shape=(jax.ShapeDtypeSt...]
    all_to_all x0 -> x1, blocking collectives: none -> 26.6 us  [shards(): lax.all_to_all(jnp.broadcast_to(parts[None], (tiles, *parts.shape)), 'col...]
    convert_element_type x8 -> x0, other arithmetic: 23.8 us -> none  [the longest x2 22.7 us: apply_blocks(): factors[:, :, column_index, :].astype(jnp.float32)[None]]
    all_to_all x1 -> x0, waiting for transfers between devices: 9.46 us -> none  [from_everyone(): lax.all_to_all(jnp.broadcast_to(value[None], (devices, *value.shape)), ax...]
    add x6 -> x0, other arithmetic: 8.29 us -> none  [the longest x2 5.73 us: apply_blocks(): result + factors[:, :, column_index, :].astype(jnp.float32)[None] * value...]
  transfers between devices with their start and end apart: 6 -> 3, of which waited for: 2 -> 1; matrix products, arithmetic and copies ran while one was open for 26% -> 2% of each run, Pallas kernels for 0% -> 17%
where the time goes in v1:
time: 116 us; the launch traced here: 114 us
  waiting for transfers between devices  32.5 us (28%)
  Pallas kernels  28.3 us (24%)
  blocking collectives  26.6 us (23%)
  between operations  14.1 us (12%)
  starting transfers between devices  6 us (5%)
  local copies, waits for them, and re-layouts  4.95 us (4%)
  other arithmetic  1.59 us (1%)
    all_gather x1, waiting for transfers between devices, shards(): lax.all_gather(both, 'params', axis=0).reshape(members * 2 * species, LANES)  32.5 us
    all_to_all x1, blocking collectives, shards(): lax.all_to_all(jnp.broadcast_to(parts[None], (tiles, *parts.shape)), 'col...  26.6 us
    pallas_call x1, Pallas kernels, shards(): pl.pallas_call(factor_kernel, grid=(blocks,), out_shape=(jax.ShapeDtypeSt...  15.4 us
    pallas_call x1, Pallas kernels, shards(): pl.pallas_call(apply_kernel, grid=(blocks,), out_shape=(jax.ShapeDtypeStr...  8.84 us
    ppermute x2, starting transfers between devices, passed_along(): return lax.ppermute(value, 'cols', pairs)  5.96 us
    pallas_call x1, Pallas kernels, shards(): pl.pallas_call(message_kernel, out_shape=(jax.ShapeDtypeStruct((species,...  4.1 us
  transfers between devices with their start and end apart: 3, of which 1 were waited for; matrix products, arithmetic and copies ran while one was open for 2% of the time, Pallas kernels for 17%

profile of v1, /device:TPU:1, one launch (start us, length us, event | category | flops | bytes accessed | tf_op | source)
XLA Modules:
  0.0 114.1 jit_solution(10757316974762167664)
XLA Ops:
  7.2 0.0 all-gather.3.cloned.1.call-start
  7.2 1.5 %pad_maximum_fusion = f32[2,128,128]{2,1,0:T(8,128)} fusion(f32[1,128,128]{2,1,0:T(8,128)} %bitcast.18, f32[1,128,128]{2,1,0:T(8,128)} %bitcast.19), kind=kLoop, calls=%fused_computation | loop fusion | flops 32768 | bytes 262144 | tf_op jit(solution)/shard_map/stack | solution.py:232
  8.7 0.0 all-gather.3.cloned.1.call-update
  8.8 4.1 %messages.1 = (bf16[128,16,128]{2,1,0:T(8,128)(2,1)}, bf16[129,16,128]{2,1,0:T(8,128)(2,1)}) custom-call(f32[8,128]{1,0:T(8,128)} %bitcast.20, s32[8,128]{1,0:T(8,128)} %bitcast.22, f32[8,128]{1,0:T(8,128)} %bitcast.24, s32[8,128]{1,0:T(8,128)} %bitcast.26, f32[2,128,8,128]{3,2,1,0:T(8,128)} %bitcast.14), custom_call_target="tpu_custom_call" | custom-call | tf_op jit(solution)/shard_map/messages/pallas_call | solution.py:219
  12.9 1.3 %collective-permute-start.1 = (bf16[129,16,128]{2,1,0:T(8,128)(2,1)}, bf16[129,16,128]{2,1,0:T(8,128)(2,1)S(1)}, u32[]{:S(2)}, u32[]{:S(2)}) collective-permute-start(bf16[129,16,128]{2,1,0:T(8,128)(2,1)} %get-tuple-element.13), channel_id=1, source_target_pairs={{8,0},{16,8},{24,16},{32,24},{40,32},{48,40},{56,48},{64,56},{72,6... | collective-permute-start | bytes 1585160 | tf_op jit(solution)/shard_map/ppermute | solution.py:188
  14.2 4.7 %collective-permute-start = (bf16[128,16,128]{2,1,0:T(8,128)(2,1)}, bf16[128,16,128]{2,1,0:T(8,128)(2,1)S(1)}, u32[]{:S(2)}, u32[]{:S(2)}) collective-permute-start(bf16[128,16,128]{2,1,0:T(8,128)(2,1)} %get-tuple-element.12), channel_id=1, source_target_pairs={{0,8},{8,16},{16,24},{24,32},{32,40},{40,48},{48,56},{56,64},{64,7... | collective-permute-start | bytes 1572872 | tf_op jit(solution)/shard_map/ppermute | solution.py:188
  18.9 1.5 %reshape.40.rate_ref = f32[2048]{0:T(1024)} reshape(f32[8,16,16]{2,1,0:T(8,128)} %param.12) | data formatting | bytes 16384 | tf_op jit(solution)/shard_map/reshape | solution.py:254
  20.4 32.5 %all-gather.3.cloned.1.call-done = f32[16,128,128]{2,1,0:T(8,128)} async-done(((f32[2,128,128]{2,1,0:T(8,128)}), f32[16,128,128]{2,1,0:T(8,128)}) %all-gather.3.cloned.1.call-update) | async-done | bytes 1048592 | tf_op jit(solution)/shard_map/all_gather | solution.py:233
  52.8 15.4 %factors.1 = (bf16[8,16,8,16,128]{4,3,2,1,0:T(8,128)(2,1)}, f32[128,128]{1,0:T(8,128)}, f32[8,128]{1,0:T(8,128)}) custom-call(s32[1]{0:T(128)} %bitcast.place_ref, s32[128]{0:T(128)} %order_ref.3, f32[2048]{0:T(1024)} %reshape.40.rate_ref, f32[2048,128]{1,0:T(8,128)} %bitcast.16), custom_call_target="tpu_custom_call" | custom-call | tf_op jit(solution)/shard_map/factors/pallas_call | solution.py:235
  68.2 0.7 slice.13
  68.9 0.0 collective-permute-done.from_left_ref
  68.9 0.0 copy-start.1
  68.9 0.0 collective-permute-done.1.from_right_ref
  68.9 0.0 copy-start
  68.9 0.8 copy-done.1
  69.7 0.2 copy-done
  69.9 8.8 %apply.1 = (f32[2,128,8,128]{3,2,1,0:T(8,128)}, f32[2,8,128]{2,1,0:T(8,128)}) custom-call(s32[128]{0:T(128)} %order_ref.3, f32[8,128]{1,0:T(8,128)} %bitcast.21, s32[8,128]{1,0:T(8,128)} %bitcast.23, f32[8,128]{1,0:T(8,128)} %bitcast.25, s32[8,128]{1,0:T(8,128)} %bitcast.27, f32[2,128,8,128]{3,2,1,0:T(8,128)} %bitcast.15, bf16[2,128,8,128]{3,2,1,0:T(8,128)(2,1)} %bitcast.17, ...), custom_call_target="tpu_custom_call" | custom-call | tf_op jit(solution)/shard_map/apply/pallas_call | solution.py:256
  78.7 0.7 slice.12
  79.5 26.6 %all_to_all.5 = f32[32,3,128]{2,1,0:T(4,128)S(1)} all-to-all(f32[32,3,128]{2,1,0:T(4,128)S(1)} %broadcast_in_dim.2), channel_id=1, replica_groups=mesh['cols'=32,'params'=8] {'cols'}, dimensions={0} | all-to-all | bytes 98304 | tf_op jit(solution)/shard_map/all_to_all | solution.py:273
  106.1 0.6 slice.14
  106.7 0.5 slice_bitcast_fusion
  (4 shorter events, 0.1 us)
Async XLA Ops:
  7.2 45.7 %all-gather.3.cloned.1.call-start = ((), (), s32[]{:S(2)}) async-start(), calls=%async_computation.1 | async-start | bytes 1179648 | tf_op jit(solution)/shard_map/all_gather | solution.py:233
  12.9 56.0 %collective-permute-start.1 = (bf16[129,16,128]{2,1,0:T(8,128)(2,1)}, bf16[129,16,128]{2,1,0:T(8,128)(2,1)S(1)}, u32[]{:S(2)}, u32[]{:S(2)}) collective-permute-start(bf16[129,16,128]{2,1,0:T(8,128)(2,1)} %get-tuple-element.13), channel_id=1, source_target_pairs={{8,0},{16,8},{24,16},{32,24},{40,32},{48,40},{56,48},{64,56},{72,6... | collective-permute-start | bytes 1585160 | tf_op jit(solution)/shard_map/ppermute | solution.py:188
  14.2 54.8 %collective-permute-start = (bf16[128,16,128]{2,1,0:T(8,128)(2,1)}, bf16[128,16,128]{2,1,0:T(8,128)(2,1)S(1)}, u32[]{:S(2)}, u32[]{:S(2)}) collective-permute-start(bf16[128,16,128]{2,1,0:T(8,128)(2,1)} %get-tuple-element.12), channel_id=1, source_target_pairs={{0,8},{8,16},{16,24},{24,32},{32,40},{40,48},{48,56},{56,64},{64,7... | collective-permute-start | bytes 1572872 | tf_op jit(solution)/shard_map/ppermute | solution.py:188
  68.9 0.8 copy-start.1
  68.9 1.0 copy-start
Sparse Core Ops, SparseCore 0:
  9.8 43.0 all-gather.2

commit v2 on v1

v2 whole, which is shorter than its diff:
```python
import functools

import jax
import jax.numpy as jnp
from jax import lax
from jax.experimental import pallas as pl
from jax.experimental.pallas import tpu as pltpu
from jax.sharding import PartitionSpec as P

ROWS, LANES = 8, 128
HALF = ROWS // 2
N = 16
CHUNKS = 4
HIGHEST = lax.Precision.HIGHEST
VMEM = pl.BlockSpec(memory_space=pltpu.VMEM)
SMEM = pl.BlockSpec(memory_space=pltpu.SMEM)
ANY = pl.BlockSpec(memory_space=pl.ANY)
SMALL = pltpu.CompilerParams(vmem_limit_bytes=16 << 20)


def shifted(value, by, axis):
    return pltpu.roll(value, by % value.shape[axis], axis)


def coefficients(cx, ux, cy, uy):
    row = lax.broadcasted_iota(jnp.int32, (ROWS, LANES), 0)
    lane = lax.broadcasted_iota(jnp.int32, (ROWS, LANES), 1)
    first = row < HALF
    up_x = jnp.where(ux == 1, cx, 0.0)
    down_x = jnp.where(ux == 1, 0.0, cx)
    up_y = jnp.where(uy == 1, cy, 0.0)
    down_y = jnp.where(uy == 1, 0.0, cy)
    before = jnp.where(lane == 0, 0.0, up_y)
    leave = jnp.where(lane == LANES - 1, 0.0, shifted(up_y, -1, 1))
    after = jnp.where(lane == LANES - 1, 0.0, shifted(down_y, -1, 1))
    other = jnp.where(first, shifted(down_x, HALF, 0), up_x)
    leave_x = jnp.where(first, shifted(up_x, HALF, 0), 0.0)
    own = 1.0 - down_y - leave - down_x - leave_x
    return first, up_x, down_x, (own, other, before, after)


def moved(s, weights):
    own, other, before, after = weights
    return (
        own * s
        + other * shifted(s, HALF, 0)
        + before * shifted(s, 1, 1)
        + after * shifted(s, -1, 1)
    )


def inverted(m_ref):
    for k in range(0, N, 2):
        x = [m_ref[k * N + j] for j in range(N)]
        y = [m_ref[(k + 1) * N + j] for j in range(N)]
        p = 1.0 / x[k]
        x = [p if j == k else x[j] * p for j in range(N)]
        e = y[k]
        y = [e * -x[j] if j == k else y[j] - e * x[j] for j in range(N)]
        p = 1.0 / y[k + 1]
        y = [p if j == k + 1 else y[j] * p for j in range(N)]
        e = x[k + 1]
        x = [e * -y[j] if j == k + 1 else x[j] - e * y[j] for j in range(N)]
        minus_x = {j: -x[j] for j in (k, k + 1)}
        minus_y = {j: -y[j] for j in (k, k + 1)}
        for i in range(N):
            if i in (k, k + 1):
                continue
            a = m_ref[i * N + k]
            b = m_ref[i * N + k + 1]
            for j in range(N):
                if j in (k, k + 1):
                    m_ref[i * N + j] = a * minus_x[j] + b * minus_y[j]
                else:
                    m_ref[i * N + j] = m_ref[i * N + j] - (a * x[j] + b * y[j])
        for j in range(N):
            m_ref[k * N + j] = x[j]
            m_ref[(k + 1) * N + j] = y[j]


def minus_system(m_ref, conc, rate):
    for i in range(N):
        row = [rate(i, j) * conc[j] for j in range(N)]
        total = row[0]
        for j in range(1, N):
            total = total + row[j]
        for j in range(N):
            m_ref[i * N + j] = row[j] - (1.0 + total) if i == j else row[j]


def lane_sums(rows):
    ones = jnp.ones((ROWS, LANES), jnp.float32)
    return lax.dot_general(ones, rows, (((1,), (1,)), ((), ())), precision=HIGHEST)


def message_kernel(cx, ux, cy, uy, s_hbm, a_ref, b_ref, s_ref, weights_ref, sems):
    species = s_ref.shape[1]
    size = species // CHUNKS

    def copy(c):
        part = (slice(None), pl.ds(c * size, size))
        return pltpu.make_async_copy(s_hbm.at[part], s_ref.at[part], sems.at[c])

    for c in range(CHUNKS):
        copy(c).start()
    first, up_x, down_x, weights = coefficients(cx[...], ux[...], cy[...], uy[...])
    down = jnp.where(first, down_x, 0.0)
    for at, weight in enumerate((up_x, *weights)):
        weights_ref[at] = weight
    high = up_x.astype(jnp.bfloat16).astype(jnp.float32)
    low = up_x - high
    both = jnp.where(first, high, shifted(low, HALF, 0))
    extra = jnp.concatenate([both, jnp.zeros_like(both)], 0).astype(jnp.bfloat16)
    odd = lax.axis_index("cols") % 2 == 1

    def work(right_ref, left_ref, c):
        def one(k, carry):
            rights, lefts = [], []
            for g in range(2):
                s = s_ref[g, k]
                t = moved(s, weights)
                rights.append(jnp.where(first, shifted(s, HALF, 0), t))
                lefts.append(jnp.where(first, down * s, shifted(down * t, HALF, 0)))
            right_ref[k] = jnp.concatenate(rights, 0).astype(jnp.bfloat16)
            left_ref[k] = jnp.concatenate(lefts, 0).astype(jnp.bfloat16)
            return carry

        lax.fori_loop(c * size, (c + 1) * size, one, 0, unroll=8)

    a_ref[species] = extra
    b_ref[species] = extra
    for c in range(CHUNKS):
        copy(c).wait()

        @pl.when(odd)
        def _():
            work(a_ref, b_ref, c)

        @pl.when(jnp.logical_not(odd))
        def _():
            work(b_ref, a_ref, c)


def base_kernel(order_ref, rate_ref, conc_ref, emis_ref, packet_ref, new_ref, m_ref, c_ref, e_ref, r_ref):
    species = conc_ref.shape[0]
    blocks = species // N
    for b in range(blocks):
        for j in range(N):
            k = order_ref[b * N + j]
            c_ref[pl.ds(j * ROWS + b, 1), :] = conc_ref[pl.ds(k, 1), :]
            e_ref[pl.ds(j * ROWS + b, 1), :] = emis_ref[pl.ds(k, 1), :]
    conc = [c_ref[pl.ds(j * ROWS, ROWS), :] for j in range(N)]

    for b in range(blocks):
        for i in range(N):
            r_ref[pl.ds(i * ROWS + b, 1), :] = rate_ref[b, pl.ds(i, 1), :]

    def rate(i, j):
        return jnp.broadcast_to(r_ref[pl.ds(i * ROWS, ROWS), j : j + 1], (ROWS, LANES))

    minus_system(m_ref, conc, rate)
    inverted(m_ref)
    values = [
        -(c_ref[pl.ds(j * ROWS, ROWS), :] + e_ref[pl.ds(j * ROWS, ROWS), :]) for j in range(N)
    ]
    for i in range(N):
        total = None
        for j in range(N):
            term = m_ref[i * N + j].astype(jnp.bfloat16).astype(jnp.float32) * values[j]
            total = term if total is None else total + term
        e_ref[pl.ds(i * ROWS, ROWS), :] = total
    for b in range(blocks):
        for i in range(N):
            k = order_ref[b * N + i]
            new_ref[pl.ds(k, 1), :] = e_ref[pl.ds(i * ROWS + b, 1), :]
    packet_ref[:species, :] = conc_ref[...]
    packet_ref[species:, :] = lane_sums(new_ref[...])


def factor_kernel(order_ref, rate_ref, cells_ref, source_hbm, factor_ref, part_ref, source_ref, m_ref, sem):
    stride = cells_ref.shape[0] // ROWS
    species = stride - ROWS
    blocks = species // N
    copy = pltpu.make_async_copy(source_hbm, source_ref, sem)
    copy.start()

    def one(block, carry):
        conc = [
            cells_ref[pl.ds(order_ref[block * N + j], ROWS, stride=stride), :] for j in range(N)
        ]
        minus_system(m_ref, conc, lambda i, j: rate_ref[block, i, j])
        inverted(m_ref)
        for i in range(0, N, 2):
            for j in range(N):
                pair = jnp.concatenate([m_ref[i * N + j], m_ref[(i + 1) * N + j]], 0)
                factor_ref[block, j, i // 2] = pair.astype(jnp.bfloat16)
        return carry

    lax.fori_loop(0, blocks, one, 0)
    members = cells_ref[pl.ds(species, ROWS, stride=stride), :]
    part_ref[...] = jnp.sum(members, axis=0, keepdims=True)
    copy.wait()


def apply_kernel(
    order_ref, weights_ref, s_ref, source_ref, a_ref, b_ref, factor_ref, conc_part_ref, out_ref, part_ref
):
    species = s_ref.shape[1]
    odd = lax.axis_index("cols") % 2 == 1
    extra = jnp.where(odd, a_ref[species].astype(jnp.float32), b_ref[species].astype(jnp.float32))
    extra = extra[:ROWS]
    upper = extra + shifted(extra, HALF, 0)
    first = lax.broadcasted_iota(jnp.int32, (ROWS, LANES), 0) < HALF
    up_x = weights_ref[0]
    own = weights_ref[1] - jnp.where(first, 0.0, upper)
    weights = (own, weights_ref[2], weights_ref[3], weights_ref[4])
    minus = tuple(-w for w in weights)

    def one(block, carry):
        values = [[None] * N, [None] * N]
        for j in range(N):
            k = order_ref[block * N + j]
            wide_a = a_ref[k].astype(jnp.float32)
            wide_b = b_ref[k].astype(jnp.float32)
            left = jnp.where(odd, wide_b, wide_a)
            right = jnp.where(odd, wide_a, wide_b)
            for g in range(2):
                a = left[g * ROWS : (g + 1) * ROWS]
                b = right[g * ROWS : (g + 1) * ROWS]
                inflow = up_x * a
                halo_0 = jnp.where(first, inflow, shifted(b, HALF, 0))
                halo_1 = jnp.where(first, up_x * (shifted(a, HALF, 0) - inflow), b)
                s = moved(s_ref[g, k], weights) + halo_0
                s = moved(s, minus) - halo_1
                values[g][j] = s - source_ref[g, k].astype(jnp.float32)
        for i in range(0, N, 2):
            sums = [[None, None], [None, None]]
            for j in range(N):
                wide = factor_ref[block, j, i // 2].astype(jnp.float32)
                for h in range(2):
                    f = wide[h * ROWS : (h + 1) * ROWS]
                    for g in range(2):
                        term = f * values[g][j]
                        sums[g][h] = term if sums[g][h] is None else sums[g][h] + term
            for h in range(2):
                k = order_ref[block * N + i + h]
                for g in range(2):
                    out_ref[g, k] = sums[g][h]
        return carry

    lax.fori_loop(0, species // N, one, 0)
    tiles = part_ref.shape[0]
    for g in range(2):
        row = lane_sums(jnp.sum(out_ref[g], axis=1))[:1]
        part_ref[:, g, :] = jnp.broadcast_to(row, (tiles, LANES))
    part_ref[:, 2, :] = jnp.broadcast_to(conc_part_ref[...], (tiles, LANES))


def means_kernel(scale, parts_ref, sens_ref, conc_ref):
    totals = jnp.sum(parts_ref[...], axis=0) * scale
    sens_ref[...] = totals[:2]
    conc_ref[...] = totals[2:3]


def near(value):
    return pltpu.with_memory_space_constraint(value, pltpu.VMEM)


def far(value):
    return pltpu.with_memory_space_constraint(value, pltpu.HBM)


def swapped(value, first):
    devices = lax.axis_size("cols")
    pairs = [(i, i + 1) for i in range(first, devices - 1, 2)]
    return lax.ppermute(value, "cols", pairs + [(b, a) for a, b in pairs])


def shards(
    concentration,
    emissions,
    rate_table,
    species_order,
    sensitivity,
    source_terms,
    courant_x,
    upwind_x,
    courant_y,
    upwind_y,
):
    blocks = rate_table.shape[0]
    groups, species, planes, layers, across = sensitivity.shape
    cells = planes * layers * across
    tiles = lax.axis_size("cols")
    s = sensitivity.reshape(groups, species, ROWS, LANES)
    source = source_terms.reshape(groups, species, ROWS, LANES)
    winds = [w.reshape(ROWS, LANES) for w in (courant_x, upwind_x, courant_y, upwind_y)]

    message = pltpu.VMEM((species + 1, 2 * ROWS, LANES), jnp.bfloat16)
    a, b, s_near, weights = pl.pallas_call(
        message_kernel,
        out_shape=(
            message,
            message,
            pltpu.VMEM(s.shape, jnp.float32),
            pltpu.VMEM((5, ROWS, LANES), jnp.float32),
        ),
        in_specs=[VMEM] * 4 + [ANY],
        out_specs=(VMEM,) * 4,
        scratch_shapes=[pltpu.SemaphoreType.DMA((CHUNKS,))],
        compiler_params=SMALL,
        name="messages",
    )(*map(far, winds), far(s))
    a = swapped(a, 1)
    b = swapped(b, 0)

    packet, new_concentration = pl.pallas_call(
        base_kernel,
        out_shape=(
            pltpu.VMEM((species + ROWS, LANES), jnp.float32),
            jax.ShapeDtypeStruct((species, LANES), jnp.float32),
        ),
        in_specs=[SMEM, VMEM, VMEM, VMEM],
        out_specs=(VMEM, VMEM),
        scratch_shapes=[
            pltpu.VMEM((N * N, ROWS, LANES), jnp.float32),
            pltpu.VMEM((species, LANES), jnp.float32),
            pltpu.VMEM((species, LANES), jnp.float32),
            pltpu.VMEM((N * ROWS, N), jnp.float32),
        ],
        compiler_params=SMALL,
        name="base",
    )(far(species_order), far(rate_table), far(concentration), far(emissions))
    gathered = lax.all_gather(packet, "params", axis=0, tiled=True)

    factors, conc_part, source_near = pl.pallas_call(
        factor_kernel,
        out_shape=(
            pltpu.VMEM((blocks, N, N // 2, 2 * ROWS, LANES), jnp.bfloat16),
            pltpu.VMEM((1, LANES), jnp.float32),
            pltpu.VMEM(source.shape, source.dtype),
        ),
        in_specs=[SMEM, SMEM, VMEM, ANY],
        out_specs=(VMEM,) * 3,
        scratch_shapes=[
            pltpu.VMEM((N * N, ROWS, LANES), jnp.float32),
            pltpu.SemaphoreType.DMA,
        ],
        compiler_params=SMALL,
        name="factors",
    )(far(species_order), far(rate_table), near(gathered), far(source))

    new_sens, parts = pl.pallas_call(
        apply_kernel,
        out_shape=(
            pltpu.VMEM(s.shape, jnp.float32),
            pltpu.VMEM((tiles, 3, LANES), jnp.float32),
        ),
        in_specs=[SMEM] + [VMEM] * 7,
        out_specs=(VMEM, VMEM),
        compiler_params=SMALL,
        name="apply",
    )(
        far(species_order),
        near(weights),
        near(s_near),
        near(source_near),
        near(a),
        near(b),
        near(factors),
        near(conc_part),
    )

    everything = lax.all_to_all(parts, "cols", 0, 0, tiled=True)
    sens_mean, conc_mean = pl.pallas_call(
        functools.partial(means_kernel, 1.0 / (cells * tiles)),
        out_shape=(
            jax.ShapeDtypeStruct((groups, species), jnp.float32),
            jax.ShapeDtypeStruct((1, species), jnp.float32),
        ),
        in_specs=[VMEM],
        out_specs=(VMEM, VMEM),
        compiler_params=SMALL,
        name="means",
    )(near(everything))
    return (
        new_concentration,
        new_sens.reshape(sensitivity.shape),
        sens_mean,
        conc_mean.reshape(species),
    )


def solution(mesh):
    in_specs = (
        P(None, ("cols", "params")),
        P(None, ("cols", "params")),
        P(),
        P(),
        P("params", None, "cols"),
        P("params", None, "cols"),
        P("cols"),
        P("cols"),
        P("cols"),
        P("cols"),
    )
    out_specs = (P(None, ("cols", "params")), P("params", None, "cols"), P("params"), P())
    return jax.shard_map(shards, mesh=mesh, in_specs=in_specs, out_specs=out_specs, check_vma=False)
```

time: 116 us -> 85.6 us (0.74); the launches traced: 114 us -> 85.2 us
  starting transfers between devices: 6 us -> 32.1 us
  waiting for transfers between devices: 32.5 us -> 10.3 us
  between operations: 14.1 us -> 0.68 us
  blocking collectives: 26.6 us -> 17.1 us
  Pallas kernels: 28.3 us -> 24.1 us
  local copies, waits for them, and re-layouts: 4.95 us -> 0.97 us
  other arithmetic: 1.59 us -> 0 us
    all_gather x1 -> x0, waiting for transfers between devices: 32.5 us -> none  [shards(): lax.all_gather(both, 'params', axis=0).reshape(members * 2 * species, LANES)]
    all_to_all x0 -> x1, starting transfers between devices: none -> 26.7 us  [shards(): everything = lax.all_to_all(parts, 'cols', 0, 0, tiled=True)]
    all_to_all x1 -> x0, blocking collectives: 26.6 us -> none  [shards(): lax.all_to_all(jnp.broadcast_to(parts[None], (tiles, *parts.shape)), 'col...]
    all_gather x0 -> x1, blocking collectives: none -> 17.1 us  [shards(): gathered = lax.all_gather(packet, 'params', axis=0, tiled=True)]
    all_to_all x0 -> x1, waiting for transfers between devices: none -> 10.3 us  [shards(): everything = lax.all_to_all(parts, 'cols', 0, 0, tiled=True)]
    pallas_call x3 -> x5, Pallas kernels: 28.3 us -> 24.1 us  [the longest x1 11.7 us: shards(): pl.pallas_call(factor_kernel, out_shape=(pltpu.VMEM((blocks, N, N // 2, 2...]
    slice x3 -> x0, local copies, waits for them, and re-layouts: 1.94 us -> none  [the longest x2 1.37 us: shards(): parts = jnp.concatenate([sens_part[:, 0], conc_part[:1]], axis=0)]
    another operation x1 -> x0, other arithmetic: 1.53 us -> none  [shards(): both = jnp.stack([concentration, emissions])]
  transfers between devices with their start and end apart: 3 -> 3, of which waited for: 1 -> 1; matrix products, arithmetic and copies ran while one was open for 2% -> 1% of each run, Pallas kernels for 17% -> 17%
where the time goes in v2:
time: 85.6 us; the launch traced here: 85.2 us
  starting transfers between devices  32.1 us (38%)
  Pallas kernels  24.1 us (28%)
  blocking collectives  17.1 us (20%)
  waiting for transfers between devices  10.3 us (12%)
  local copies, waits for them, and re-layouts  0.97 us (1%)
    all_to_all x1, starting transfers between devices, shards(): everything = lax.all_to_all(parts, 'cols', 0, 0, tiled=True)  26.7 us
    all_gather x1, blocking collectives, shards(): gathered = lax.all_gather(packet, 'params', axis=0, tiled=True)  17.1 us
    pallas_call x1, Pallas kernels, shards(): pl.pallas_call(factor_kernel, out_shape=(pltpu.VMEM((blocks, N, N // 2, 2...  11.7 us
    all_to_all x1, waiting for transfers between devices, shards(): everything = lax.all_to_all(parts, 'cols', 0, 0, tiled=True)  10.3 us
    ppermute x2, starting transfers between devices, swapped(): return lax.ppermute(value, 'cols', pairs + [(b, a) for a, b in pairs])  5.41 us
    pallas_call x1, Pallas kernels, shards(): pl.pallas_call(apply_kernel, out_shape=(pltpu.VMEM(s.shape, jnp.float32),...  5.15 us
    pallas_call x1, Pallas kernels, shards(): pl.pallas_call(message_kernel, out_shape=(message, message, pltpu.VMEM(s....  3.48 us
    pallas_call x1, Pallas kernels, shards(): pl.pallas_call(base_kernel, out_shape=(pltpu.VMEM((species + ROWS, LANES)...  3.16 us
  transfers between devices with their start and end apart: 3, of which 1 were waited for; matrix products, arithmetic and copies ran while one was open for 1% of the time, Pallas kernels for 17%

profile of v2, /device:TPU:1, one launch (start us, length us, event | category | flops | bytes accessed | tf_op | source)
XLA Modules:
  0.0 85.2 jit_solution(17406665188118491371)
XLA Ops:
  0.6 3.5 %messages.1 = (bf16[129,16,128]{2,1,0:T(8,128)(2,1)S(1)}, bf16[129,16,128]{2,1,0:T(8,128)(2,1)S(1)}, f32[2,128,8,128]{3,2,1,0:T(8,128)S(1)}, f32[5,8,128]{2,1,0:T(8,128)S(1)}) custom-call(f32[8,128]{1,0:T(8,128)} %bitcast.11, s32[8,128]{1,0:T(8,128)} %bitcast.12, f32[8,128]{1,0:T(8,128)} %bitcast.13, s32[8,128]{1,0:T(8,128)} %bitcast.14, ...), custom_call_target="tpu_custom_call" | custom-call | tf_op jit(solution)/shard_map/messages/pallas_call | solution.py:300
  4.1 0.7 collective-permute-start
  4.8 4.7 %collective-permute-start.1 = (bf16[129,16,128]{2,1,0:T(8,128)(2,1)S(1)}, bf16[129,16,128]{2,1,0:T(8,128)(2,1)S(1)}, u32[]{:S(2)}, u32[]{:S(2)}) collective-permute-start(bf16[129,16,128]{2,1,0:T(8,128)(2,1)S(1)} %get-tuple-element.23), channel_id=1, source_target_pairs={{0,8},{16,24},{32,40},{48,56},{64,72},{80,88},{96,104},{112,120},{... | collective-permute-start | bytes 1585160 | tf_op jit(solution)/shard_map/ppermute | solution.py:276
  9.5 3.2 %base.1 = (f32[136,128]{1,0:T(8,128)S(1)}, f32[128,128]{1,0:T(8,128)}) custom-call(s32[128]{0:T(128)} %order_ref.5, f32[8,16,16]{2,1,0:T(8,128)} %rate_ref.3, f32[128,128]{1,0:T(8,128)} %conc_ref.1, f32[128,128]{1,0:T(8,128)} %emis_ref.1), custom_call_target="tpu_custom_call" | custom-call | tf_op jit(solution)/shard_map/base/pallas_call | solution.py:317
  12.7 17.1 %all_gather.3.cells_ref = f32[1088,128]{1,0:T(8,128)S(1)} all-gather(f32[136,128]{1,0:T(8,128)S(1)} %get-tuple-element.20), channel_id=1, replica_groups=mesh['cols'=32,'params'=8] {'params'}, dimensions={0}, use_global_device_ids=true | all-gather | bytes 626688 | tf_op jit(solution)/shard_map/all_gather | solution.py:334
  29.8 11.7 %factors.1 = (bf16[8,16,8,16,128]{4,3,2,1,0:T(8,128)(2,1)S(1)}, f32[1,128]{1,0:T(1,128)S(1)}, bf16[2,128,8,128]{3,2,1,0:T(8,128)(2,1)S(1)}) custom-call(s32[128]{0:T(128)} %order_ref.5, f32[8,16,16]{2,1,0:T(8,128)} %rate_ref.3, f32[1088,128]{1,0:T(8,128)S(1)} %all_gather.3.cells_ref, bf16[2,128,8,128]{3,2,1,0:T(8,128)(2,1)} %bitcast.10), custom_call_target="tpu_custom_call" | custom-call | tf_op jit(solution)/shard_map/factors/pallas_call | solution.py:336
  41.5 0.0 collective-permute-done.a_ref
  41.5 0.0 collective-permute-done.1.b_ref
  41.5 5.1 %apply.1 = (f32[2,128,8,128]{3,2,1,0:T(8,128)S(1)}, f32[32,3,128]{2,1,0:T(4,128)}) custom-call(s32[128]{0:T(128)} %order_ref.5, f32[5,8,128]{2,1,0:T(8,128)S(1)} %get-tuple-element.18.weights_ref, f32[2,128,8,128]{3,2,1,0:T(8,128)S(1)} %get-tuple-element.19.s_ref, bf16[2,128,8,128]{3,2,1,0:T(8,128)(2,1)S(1)} %get-tuple-element.21.source_ref, ...), custom_call_target="tpu_custom_call" | custom-call | tf_op jit(solution)/shard_map/apply/pallas_call | solution.py:353
  46.7 26.7 %all-to-all-start = ((f32[32,3,128]{2,1,0:T(4,128)}), f32[32,3,128]{2,1,0:T(4,128)S(1)}, u32[]{:S(2)}, u32[]{:S(2)}) async-start(f32[32,3,128]{2,1,0:T(4,128)} %get-tuple-element.27), calls=%async_computation | async-start | bytes 131072 | tf_op jit(solution)/shard_map/all_to_all | solution.py:374
  73.4 1.0 %copy.14 = f32[2,128,2,4,128]{4,3,2,1,0:T(4,128)} copy(f32[2,128,2,4,128]{4,3,2,1,0:T(4,128)S(1)} %bitcast.8) | data formatting | bytes 2097152
  74.3 10.3 %all-to-all-done.parts_ref = f32[32,3,128]{2,1,0:T(4,128)S(1)} async-done(((f32[32,3,128]{2,1,0:T(4,128)}), f32[32,3,128]{2,1,0:T(4,128)S(1)}, u32[]{:S(2)}, u32[]{:S(2)}) %all-to-all-start) | async-done | bytes 49184 | tf_op jit(solution)/shard_map/all_to_all | solution.py:374
  84.6 0.6 means.1
Async XLA Ops:
  4.1 37.4 %collective-permute-start = (bf16[129,16,128]{2,1,0:T(8,128)(2,1)S(1)}, bf16[129,16,128]{2,1,0:T(8,128)(2,1)S(1)}, u32[]{:S(2)}, u32[]{:S(2)}) collective-permute-start(bf16[129,16,128]{2,1,0:T(8,128)(2,1)S(1)} %get-tuple-element.22), channel_id=1, source_target_pairs={{8,16},{24,32},{40,48},{56,64},{72,80},{88,96},{104,112},{120,128}... | collective-permute-start | bytes 1585160 | tf_op jit(solution)/shard_map/ppermute | solution.py:276
  4.8 36.7 %collective-permute-start.1 = (bf16[129,16,128]{2,1,0:T(8,128)(2,1)S(1)}, bf16[129,16,128]{2,1,0:T(8,128)(2,1)S(1)}, u32[]{:S(2)}, u32[]{:S(2)}) collective-permute-start(bf16[129,16,128]{2,1,0:T(8,128)(2,1)S(1)} %get-tuple-element.23), channel_id=1, source_target_pairs={{0,8},{16,24},{32,40},{48,56},{64,72},{80,88},{96,104},{112,120},{... | collective-permute-start | bytes 1585160 | tf_op jit(solution)/shard_map/ppermute | solution.py:276
  46.7 37.9 %all-to-all-start = ((f32[32,3,128]{2,1,0:T(4,128)}), f32[32,3,128]{2,1,0:T(4,128)S(1)}, u32[]{:S(2)}, u32[]{:S(2)}) async-start(f32[32,3,128]{2,1,0:T(4,128)} %get-tuple-element.27), calls=%async_computation | async-start | bytes 131072 | tf_op jit(solution)/shard_map/all_to_all | solution.py:374

commit v3 on v2

--- a/solution.py
+++ b/solution.py
@@ -6,6 +6,7 @@
 from jax.experimental import pallas as pl
 from jax.experimental.pallas import tpu as pltpu
 from jax.sharding import PartitionSpec as P
+
 
 ROWS, LANES = 8, 128
 HALF = ROWS // 2
@@ -141,7 +142,7 @@
             work(b_ref, a_ref, c)
 
 
-def base_kernel(order_ref, rate_ref, conc_ref, emis_ref, packet_ref, new_ref, m_ref, c_ref, e_ref, r_ref):
+def base_kernel(order_ref, rate_ref, conc_ref, emis_ref, part_ref, new_ref, m_ref, c_ref, e_ref, r_ref):
     species = conc_ref.shape[0]
     blocks = species // N
     for b in range(blocks):
@@ -173,20 +174,25 @@
         for i in range(N):
             k = order_ref[b * N + i]
             new_ref[pl.ds(k, 1), :] = e_ref[pl.ds(i * ROWS + b, 1), :]
-    packet_ref[:species, :] = conc_ref[...]
-    packet_ref[species:, :] = lane_sums(new_ref[...])
-
-
-def factor_kernel(order_ref, rate_ref, cells_ref, source_hbm, factor_ref, part_ref, source_ref, m_ref, sem):
-    stride = cells_ref.shape[0] // ROWS
-    species = stride - ROWS
+    part_ref[...] = lane_sums(new_ref[...])
+
+
+def factor_kernel(
+    order_ref, rate_ref, mine_ref, other_ref, source_hbm, factor_ref, source_ref, cells_ref, m_ref, sem
+):
+    links, species = mine_ref.shape[:2]
     blocks = species // N
     copy = pltpu.make_async_copy(source_hbm, source_ref, sem)
     copy.start()
+    place = lax.axis_index("params")
+    for k in range(links):
+        for core, ref in enumerate((mine_ref, other_ref)):
+            cells_ref[pl.ds(place ^ (2 * k + core), species, stride=ROWS), :] = ref[k]
 
     def one(block, carry):
         conc = [
-            cells_ref[pl.ds(order_ref[block * N + j], ROWS, stride=stride), :] for j in range(N)
+            cells_ref[pl.ds(pl.multiple_of(order_ref[block * N + j] * ROWS, ROWS), ROWS), :]
+            for j in range(N)
         ]
         minus_system(m_ref, conc, lambda i, j: rate_ref[block, i, j])
         inverted(m_ref)
@@ -197,8 +203,6 @@
         return carry
 
     lax.fori_loop(0, blocks, one, 0)
-    members = cells_ref[pl.ds(species, ROWS, stride=stride), :]
-    part_ref[...] = jnp.sum(members, axis=0, keepdims=True)
     copy.wait()
 
 
@@ -253,7 +257,7 @@
     for g in range(2):
         row = lane_sums(jnp.sum(out_ref[g], axis=1))[:1]
         part_ref[:, g, :] = jnp.broadcast_to(row, (tiles, LANES))
-    part_ref[:, 2, :] = jnp.broadcast_to(conc_part_ref[...], (tiles, LANES))
+    part_ref[:, 2, :] = jnp.broadcast_to(conc_part_ref[:1], (tiles, LANES))
 
 
 def means_kernel(scale, parts_ref, sens_ref, conc_ref):
@@ -270,13 +274,19 @@
     return pltpu.with_memory_space_constraint(value, pltpu.HBM)
 
 
+def crossed(value, bits):
+    return lax.ppermute(
+        value, "params", [(i, i ^ bits) for i in range(lax.axis_size("params"))]
+    )
+
+
 def swapped(value, first):
     devices = lax.axis_size("cols")
     pairs = [(i, i + 1) for i in range(first, devices - 1, 2)]
     return lax.ppermute(value, "cols", pairs + [(b, a) for a, b in pairs])
 
 
-def shards(
+def step(
     concentration,
     emissions,
     rate_table,
@@ -296,6 +306,10 @@
     source = source_terms.reshape(groups, species, ROWS, LANES)
     winds = [w.reshape(ROWS, LANES) for w in (courant_x, upwind_x, courant_y, upwind_y)]
 
+    links = lax.axis_size("params") // 2
+    mine = [concentration]
+    for k in range(1, links):
+        mine.append(crossed(concentration, 2 * k))
     message = pltpu.VMEM((species + 1, 2 * ROWS, LANES), jnp.bfloat16)
     a, b, s_near, weights = pl.pallas_call(
         message_kernel,
@@ -313,11 +327,13 @@
     )(*map(far, winds), far(s))
     a = swapped(a, 1)
     b = swapped(b, 0)
-
-    packet, new_concentration = pl.pallas_call(
+    mine = jnp.stack(mine)
+    other = crossed(mine, 1)
+
+    conc_part, new_concentration = pl.pallas_call(
         base_kernel,
         out_shape=(
-            pltpu.VMEM((species + ROWS, LANES), jnp.float32),
+            pltpu.VMEM((ROWS, LANES), jnp.float32),
             jax.ShapeDtypeStruct((species, LANES), jnp.float32),
         ),
         in_specs=[SMEM, VMEM, VMEM, VMEM],
@@ -331,24 +347,28 @@
         compiler_params=SMALL,
         name="base",
     )(far(species_order), far(rate_table), far(concentration), far(emissions))
-    gathered = lax.all_gather(packet, "params", axis=0, tiled=True)
-
-    factors, conc_part, source_near = pl.pallas_call(
+    conc_part = conc_part + crossed(conc_part, 1)
+    others = []
+    for k in range(1, links):
+        others.append(crossed(conc_part, 2 * k))
+    conc_part = sum(others, conc_part)
+
+    factors, source_near = pl.pallas_call(
         factor_kernel,
         out_shape=(
             pltpu.VMEM((blocks, N, N // 2, 2 * ROWS, LANES), jnp.bfloat16),
-            pltpu.VMEM((1, LANES), jnp.float32),
             pltpu.VMEM(source.shape, source.dtype),
         ),
-        in_specs=[SMEM, SMEM, VMEM, ANY],
-        out_specs=(VMEM,) * 3,
+        in_specs=[SMEM, SMEM, VMEM, VMEM, ANY],
+        out_specs=(VMEM,) * 2,
         scratch_shapes=[
+            pltpu.VMEM((species * ROWS, LANES), jnp.float32),
             pltpu.VMEM((N * N, ROWS, LANES), jnp.float32),
             pltpu.SemaphoreType.DMA,
         ],
         compiler_params=SMALL,
         name="factors",
-    )(far(species_order), far(rate_table), near(gathered), far(source))
+    )(far(species_order), far(rate_table), near(mine), near(other), far(source))
 
     new_sens, parts = pl.pallas_call(
         apply_kernel,
@@ -405,4 +425,4 @@
         P("cols"),
     )
     out_specs = (P(None, ("cols", "params")), P("params", None, "cols"), P("params"), P())
-    return jax.shard_map(shards, mesh=mesh, in_specs=in_specs, out_specs=out_specs, check_vma=False)
+    return jax.shard_map(step, mesh=mesh, in_specs=in_specs, out_specs=out_specs, check_vma=False)

time: 85.6 us -> 96.2 us (1.12)
  the two profiles are of different devices: /device:TPU:1 before, /device:TPU:2 now
where the time goes in v3:
time: 96.2 us; the launch traced here: 95.8 us
  waiting for transfers between devices  41.5 us (43%)
  starting transfers between devices  27.4 us (28%)
  Pallas kernels  24.3 us (25%)
  local copies, waits for them, and re-layouts  0.97 us (1%)
    ppermute x8, waiting for transfers between devices, crossed(): lax.ppermute(value, 'params', [(i, i ^ bits) for i in range(lax.axis_size...  31.3 us
    pallas_call x1, Pallas kernels, step(): pl.pallas_call(factor_kernel, out_shape=(pltpu.VMEM((blocks, N, N // 2, 2...  11.9 us
    ppermute x2, starting transfers between devices, swapped(): return lax.ppermute(value, 'cols', pairs + [(b, a) for a, b in pairs])  11.6 us
    all_to_all x1, waiting for transfers between devices, step(): everything = lax.all_to_all(parts, 'cols', 0, 0, tiled=True)  10.2 us
    all_to_all x1, starting transfers between devices, step(): everything = lax.all_to_all(parts, 'cols', 0, 0, tiled=True)  7.98 us
    ppermute x8, starting transfers between devices, crossed(): lax.ppermute(value, 'params', [(i, i ^ bits) for i in range(lax.axis_size...  7.82 us
    pallas_call x1, Pallas kernels, step(): pl.pallas_call(apply_kernel, out_shape=(pltpu.VMEM(s.shape, jnp.float32),...  5.14 us
    pallas_call x1, Pallas kernels, step(): pl.pallas_call(message_kernel, out_shape=(message, message, pltpu.VMEM(s....  3.48 us
  transfers between devices with their start and end apart: 11, of which 7 were waited for; matrix products, arithmetic and copies ran while one was open for 2% of the time, Pallas kernels for 16%

profile of v3, /device:TPU:2, one launch (start us, length us, event | category | flops | bytes accessed | tf_op | source)
XLA Modules:
  0.0 95.8 jit_solution(8268461282394434516)
XLA Ops:
  0.6 3.5 %messages.1 = (bf16[129,16,128]{2,1,0:T(8,128)(2,1)S(1)}, bf16[129,16,128]{2,1,0:T(8,128)(2,1)S(1)}, f32[2,128,8,128]{3,2,1,0:T(8,128)S(1)}, f32[5,8,128]{2,1,0:T(8,128)S(1)}) custom-call(f32[8,128]{1,0:T(8,128)} %bitcast.19, s32[8,128]{1,0:T(8,128)} %bitcast.20, f32[8,128]{1,0:T(8,128)} %bitcast.21, s32[8,128]{1,0:T(8,128)} %bitcast.22, ...), custom_call_target="tpu_custom_call" | custom-call | tf_op jit(solution)/shard_map/messages/pallas_call | solution.py:314
  4.1 11.5 %collective-permute-start.4 = (bf16[129,16,128]{2,1,0:T(8,128)(2,1)S(1)}, bf16[129,16,128]{2,1,0:T(8,128)(2,1)S(1)}, u32[]{:S(2)}, u32[]{:S(2)}) collective-permute-start(bf16[129,16,128]{2,1,0:T(8,128)(2,1)S(1)} %get-tuple-element.20), channel_id=1, source_target_pairs={{8,16},{24,32},{40,48},{56,64},{72,80},{88,96},{104,112},{120,128}... | collective-permute-start | bytes 1585160 | tf_op jit(solution)/shard_map/ppermute | solution.py:286
  15.7 0.1 collective-permute-start.5
  15.8 1.1 %collective-permute-start = (f32[128,128]{1,0:T(8,128)}, f32[128,128]{1,0:T(8,128)S(1)}, u32[]{:S(2)}, u32[]{:S(2)}) collective-permute-start(f32[128,128]{1,0:T(8,128)} %conc_ref.1), channel_id=1, source_target_pairs={{0,2},{1,3},{2,0},{3,1},{4,6},{5,7},{6,4},{7,5},{8,10},{9,11},{10,... | collective-permute-start | bytes 196616 | tf_op jit(solution)/shard_map/ppermute | solution.py:278
  16.9 1.9 %collective-permute-start.2 = (f32[128,128]{1,0:T(8,128)}, f32[128,128]{1,0:T(8,128)S(1)}, u32[]{:S(2)}, u32[]{:S(2)}) collective-permute-start(f32[128,128]{1,0:T(8,128)} %conc_ref.1), channel_id=1, source_target_pairs={{0,6},{1,7},{2,4},{3,5},{4,2},{5,3},{6,0},{7,1},{8,14},{9,15},{10,... | collective-permute-start | bytes 196616 | tf_op jit(solution)/shard_map/ppermute | solution.py:278
  18.8 0.6 collective-permute-start.1
  19.3 23.2 %collective-permute-done = f32[128,128]{1,0:T(8,128)S(1)} collective-permute-done((f32[128,128]{1,0:T(8,128)}, f32[128,128]{1,0:T(8,128)S(1)}, u32[]{:S(2)}, u32[]{:S(2)}) %collective-permute-start) | collective-permute-done | bytes 65568 | tf_op jit(solution)/shard_map/ppermute | solution.py:278
  42.6 1.8 %collective-permute-done.1 = f32[128,128]{1,0:T(8,128)S(1)} collective-permute-done((f32[128,128]{1,0:T(8,128)}, f32[128,128]{1,0:T(8,128)S(1)}, u32[]{:S(2)}, u32[]{:S(2)}) %collective-permute-start.1) | collective-permute-done | bytes 65568 | tf_op jit(solution)/shard_map/ppermute | solution.py:278
  44.4 0.9 pad_maximum_fusion.mine_ref
  45.3 0.1 collective-permute-start.3
  45.4 3.2 %base.1 = (f32[8,128]{1,0:T(8,128)S(1)}, f32[128,128]{1,0:T(8,128)}) custom-call(s32[128]{0:T(128)} %order_ref.5, f32[8,16,16]{2,1,0:T(8,128)} %rate_ref.3, f32[128,128]{1,0:T(8,128)} %conc_ref.1, f32[128,128]{1,0:T(8,128)} %emis_ref.1), custom_call_target="tpu_custom_call" | custom-call | tf_op jit(solution)/shard_map/base/pallas_call | solution.py:333
  48.6 0.5 collective-permute-start.6
  49.0 0.8 collective-permute-done.6
  49.9 3.6 %collective-permute-start.9 = (f32[8,128]{1,0:T(8,128)S(1)}, f32[8,128]{1,0:T(8,128)S(1)}, u32[]{:S(2)}, u32[]{:S(2)}) collective-permute-start(f32[8,128]{1,0:T(8,128)S(1)} %add.12), channel_id=1, source_target_pairs={{0,6},{1,7},{2,4},{3,5},{4,2},{5,3},{6,0},{7,1},{8,14},{9,15},{10,... | collective-permute-start | bytes 12296 | tf_op jit(solution)/shard_map/ppermute | solution.py:278
  53.5 0.0 collective-permute-start.8
  53.5 1.8 %collective-permute-done.9 = f32[8,128]{1,0:T(8,128)S(1)} collective-permute-done((f32[8,128]{1,0:T(8,128)S(1)}, f32[8,128]{1,0:T(8,128)S(1)}, u32[]{:S(2)}, u32[]{:S(2)}) %collective-permute-start.9) | collective-permute-done | bytes 4128 | tf_op jit(solution)/shard_map/ppermute | solution.py:278
  55.3 2.7 %collective-permute-done.8 = f32[8,128]{1,0:T(8,128)S(1)} collective-permute-done((f32[8,128]{1,0:T(8,128)S(1)}, f32[8,128]{1,0:T(8,128)S(1)}, u32[]{:S(2)}, u32[]{:S(2)}) %collective-permute-start.8) | collective-permute-done | bytes 4128 | tf_op jit(solution)/shard_map/ppermute | solution.py:278
  58.0 0.9 collective-permute-done.7
  58.9 11.9 %factors.1 = (bf16[8,16,8,16,128]{4,3,2,1,0:T(8,128)(2,1)S(1)}, bf16[2,128,8,128]{3,2,1,0:T(8,128)(2,1)S(1)}) custom-call(s32[128]{0:T(128)} %order_ref.5, f32[8,16,16]{2,1,0:T(8,128)} %rate_ref.3, f32[4,128,128]{2,1,0:T(8,128)S(1)} %pad_maximum_fusion.mine_ref, f32[4,128,128]{2,1,0:T(8,128)S(1)} %collective-permute-done.3.other_ref, ...), custom_call_target="tpu_custom_call" | custom-call | tf_op jit(solution)/shard_map/factors/pallas_call | solution.py:356
  70.9 5.1 %apply.1 = (f32[2,128,8,128]{3,2,1,0:T(8,128)S(1)}, f32[32,3,128]{2,1,0:T(4,128)}) custom-call(s32[128]{0:T(128)} %order_ref.5, f32[5,8,128]{2,1,0:T(8,128)S(1)} %get-tuple-element.17.weights_ref, f32[2,128,8,128]{3,2,1,0:T(8,128)S(1)} %get-tuple-element.18.s_ref, bf16[2,128,8,128]{3,2,1,0:T(8,128)(2,1)S(1)} %get-tuple-element.19.source_ref, ...), custom_call_target="tpu_custom_call" | custom-call | tf_op jit(solution)/shard_map/apply/pallas_call | solution.py:373
  76.0 8.0 %all-to-all-start = ((f32[32,3,128]{2,1,0:T(4,128)}), f32[32,3,128]{2,1,0:T(4,128)S(1)}, u32[]{:S(2)}, u32[]{:S(2)}) async-start(f32[32,3,128]{2,1,0:T(4,128)} %get-tuple-element.25), calls=%async_computation | async-start | bytes 131072 | tf_op jit(solution)/shard_map/all_to_all | solution.py:394
  84.0 1.0 %copy.14 = f32[2,128,2,4,128]{4,3,2,1,0:T(4,128)} copy(f32[2,128,2,4,128]{4,3,2,1,0:T(4,128)S(1)} %bitcast.12) | data formatting | bytes 2097152
  85.0 10.2 %all-to-all-done.parts_ref = f32[32,3,128]{2,1,0:T(4,128)S(1)} async-done(((f32[32,3,128]{2,1,0:T(4,128)}), f32[32,3,128]{2,1,0:T(4,128)S(1)}, u32[]{:S(2)}, u32[]{:S(2)}) %all-to-all-start) | async-done | bytes 49184 | tf_op jit(solution)/shard_map/all_to_all | solution.py:394
  95.2 0.6 means.1
  (7 shorter events, 0.0 us)
Async XLA Ops:
  4.1 66.7 %collective-permute-start.4 = (bf16[129,16,128]{2,1,0:T(8,128)(2,1)S(1)}, bf16[129,16,128]{2,1,0:T(8,128)(2,1)S(1)}, u32[]{:S(2)}, u32[]{:S(2)}) collective-permute-start(bf16[129,16,128]{2,1,0:T(8,128)(2,1)S(1)} %get-tuple-element.20), channel_id=1, source_target_pairs={{8,16},{24,32},{40,48},{56,64},{72,80},{88,96},{104,112},{120,128}... | collective-permute-start | bytes 1585160 | tf_op jit(solution)/shard_map/ppermute | solution.py:286
  15.7 55.2 %collective-permute-start.5 = (bf16[129,16,128]{2,1,0:T(8,128)(2,1)S(1)}, bf16[129,16,128]{2,1,0:T(8,128)(2,1)S(1)}, u32[]{:S(2)}, u32[]{:S(2)}) collective-permute-start(bf16[129,16,128]{2,1,0:T(8,128)(2,1)S(1)} %get-tuple-element.21), channel_id=1, source_target_pairs={{0,8},{16,24},{32,40},{48,56},{64,72},{80,88},{96,104},{112,120},{... | collective-permute-start | bytes 1585160 | tf_op jit(solution)/shard_map/ppermute | solution.py:286
  15.8 26.8 %collective-permute-start = (f32[128,128]{1,0:T(8,128)}, f32[128,128]{1,0:T(8,128)S(1)}, u32[]{:S(2)}, u32[]{:S(2)}) collective-permute-start(f32[128,128]{1,0:T(8,128)} %conc_ref.1), channel_id=1, source_target_pairs={{0,2},{1,3},{2,0},{3,1},{4,6},{5,7},{6,4},{7,5},{8,10},{9,11},{10,... | collective-permute-start | bytes 196616 | tf_op jit(solution)/shard_map/ppermute | solution.py:278
  16.9 25.7 %collective-permute-start.2 = (f32[128,128]{1,0:T(8,128)}, f32[128,128]{1,0:T(8,128)S(1)}, u32[]{:S(2)}, u32[]{:S(2)}) collective-permute-start(f32[128,128]{1,0:T(8,128)} %conc_ref.1), channel_id=1, source_target_pairs={{0,6},{1,7},{2,4},{3,5},{4,2},{5,3},{6,0},{7,1},{8,14},{9,15},{10,... | collective-permute-start | bytes 196616 | tf_op jit(solution)/shard_map/ppermute | solution.py:278
  18.8 25.6 %collective-permute-start.1 = (f32[128,128]{1,0:T(8,128)}, f32[128,128]{1,0:T(8,128)S(1)}, u32[]{:S(2)}, u32[]{:S(2)}) collective-permute-start(f32[128,128]{1,0:T(8,128)} %conc_ref.1), channel_id=1, source_target_pairs={{0,4},{1,5},{2,6},{3,7},{4,0},{5,1},{6,2},{7,3},{8,12},{9,13},{10,... | collective-permute-start | bytes 196616 | tf_op jit(solution)/shard_map/ppermute | solution.py:278
  45.3 13.6 %collective-permute-start.3 = (f32[4,128,128]{2,1,0:T(8,128)S(1)}, f32[4,128,128]{2,1,0:T(8,128)S(1)}, u32[]{:S(2)}, u32[]{:S(2)}) collective-permute-start(f32[4,128,128]{2,1,0:T(8,128)S(1)} %pad_maximum_fusion.mine_ref), channel_id=1, source_target_pairs={{0,1},{1,0},{2,3},{3,2},{4,5},{5,4},{6,7},{7,6},{8,9},{9,8},{10,11... | collective-permute-start | bytes 786440 | tf_op jit(solution)/shard_map/ppermute | solution.py:278
  48.6 1.3 %collective-permute-start.6 = (f32[8,128]{1,0:T(8,128)S(1)}, f32[8,128]{1,0:T(8,128)S(1)}, u32[]{:S(2)}, u32[]{:S(2)}) collective-permute-start(f32[8,128]{1,0:T(8,128)S(1)} %get-tuple-element.23), channel_id=1, source_target_pairs={{0,1},{1,0},{2,3},{3,2},{4,5},{5,4},{6,7},{7,6},{8,9},{9,8},{10,11... | collective-permute-start | bytes 12296 | tf_op jit(solution)/shard_map/ppermute | solution.py:278
  49.9 5.4 %collective-permute-start.9 = (f32[8,128]{1,0:T(8,128)S(1)}, f32[8,128]{1,0:T(8,128)S(1)}, u32[]{:S(2)}, u32[]{:S(2)}) collective-permute-start(f32[8,128]{1,0:T(8,128)S(1)} %add.12), channel_id=1, source_target_pairs={{0,6},{1,7},{2,4},{3,5},{4,2},{5,3},{6,0},{7,1},{8,14},{9,15},{10,... | collective-permute-start | bytes 12296 | tf_op jit(solution)/shard_map/ppermute | solution.py:278
  53.5 4.5 %collective-permute-start.8 = (f32[8,128]{1,0:T(8,128)S(1)}, f32[8,128]{1,0:T(8,128)S(1)}, u32[]{:S(2)}, u32[]{:S(2)}) collective-permute-start(f32[8,128]{1,0:T(8,128)S(1)} %add.12), channel_id=1, source_target_pairs={{0,4},{1,5},{2,6},{3,7},{4,0},{5,1},{6,2},{7,3},{8,12},{9,13},{10,... | collective-permute-start | bytes 12296 | tf_op jit(solution)/shard_map/ppermute | solution.py:278
  55.3 3.6 %collective-permute-start.7 = (f32[8,128]{1,0:T(8,128)S(1)}, f32[8,128]{1,0:T(8,128)S(1)}, u32[]{:S(2)}, u32[]{:S(2)}) collective-permute-start(f32[8,128]{1,0:T(8,128)S(1)} %add.12), channel_id=1, source_target_pairs={{0,2},{1,3},{2,0},{3,1},{4,6},{5,7},{6,4},{7,5},{8,10},{9,11},{10,... | collective-permute-start | bytes 12296 | tf_op jit(solution)/shard_map/ppermute | solution.py:278
  76.0 19.2 %all-to-all-start = ((f32[32,3,128]{2,1,0:T(4,128)}), f32[32,3,128]{2,1,0:T(4,128)S(1)}, u32[]{:S(2)}, u32[]{:S(2)}) async-start(f32[32,3,128]{2,1,0:T(4,128)} %get-tuple-element.25), calls=%async_computation | async-start | bytes 131072 | tf_op jit(solution)/shard_map/all_to_all | solution.py:394

commit v4 on v3

--- a/solution.py
+++ b/solution.py
@@ -11,7 +11,7 @@
 ROWS, LANES = 8, 128
 HALF = ROWS // 2
 N = 16
-CHUNKS = 4
+CHUNKS = 8
 HIGHEST = lax.Precision.HIGHEST
 VMEM = pl.BlockSpec(memory_space=pltpu.VMEM)
 SMEM = pl.BlockSpec(memory_space=pltpu.SMEM)
@@ -94,7 +94,9 @@
     return lax.dot_general(ones, rows, (((1,), (1,)), ((), ())), precision=HIGHEST)
 
 
-def message_kernel(cx, ux, cy, uy, s_hbm, a_ref, b_ref, s_ref, weights_ref, sems):
+def message_kernel(
+    cx_hbm, ux_hbm, cy_hbm, uy_hbm, s_hbm, a_ref, b_ref, s_ref, t_ref, weights_ref, reals_ref, flags_ref, wind_sem, sems
+):
     species = s_ref.shape[1]
     size = species // CHUNKS
 
@@ -102,9 +104,26 @@
         part = (slice(None), pl.ds(c * size, size))
         return pltpu.make_async_copy(s_hbm.at[part], s_ref.at[part], sems.at[c])
 
+    winds = [
+        pltpu.make_async_copy(source, target, wind_sem.at[at])
+        for at, (source, target) in enumerate(
+            (
+                (cx_hbm, reals_ref.at[0]),
+                (ux_hbm, flags_ref.at[0]),
+                (cy_hbm, reals_ref.at[1]),
+                (uy_hbm, flags_ref.at[1]),
+            )
+        )
+    ]
+    for wind in winds:
+        wind.start()
     for c in range(CHUNKS):
         copy(c).start()
-    first, up_x, down_x, weights = coefficients(cx[...], ux[...], cy[...], uy[...])
+    for wind in winds:
+        wind.wait()
+    first, up_x, down_x, weights = coefficients(
+        reals_ref[0], flags_ref[0], reals_ref[1], flags_ref[1]
+    )
     down = jnp.where(first, down_x, 0.0)
     for at, weight in enumerate((up_x, *weights)):
         weights_ref[at] = weight
@@ -113,33 +132,34 @@
     both = jnp.where(first, high, shifted(low, HALF, 0))
     extra = jnp.concatenate([both, jnp.zeros_like(both)], 0).astype(jnp.bfloat16)
     odd = lax.axis_index("cols") % 2 == 1
-
-    def work(right_ref, left_ref, c):
-        def one(k, carry):
-            rights, lefts = [], []
-            for g in range(2):
-                s = s_ref[g, k]
-                t = moved(s, weights)
-                rights.append(jnp.where(first, shifted(s, HALF, 0), t))
-                lefts.append(jnp.where(first, down * s, shifted(down * t, HALF, 0)))
-            right_ref[k] = jnp.concatenate(rights, 0).astype(jnp.bfloat16)
-            left_ref[k] = jnp.concatenate(lefts, 0).astype(jnp.bfloat16)
-            return carry
-
-        lax.fori_loop(c * size, (c + 1) * size, one, 0, unroll=8)
-
     a_ref[species] = extra
     b_ref[species] = extra
-    for c in range(CHUNKS):
-        copy(c).wait()
-
-        @pl.when(odd)
-        def _():
-            work(a_ref, b_ref, c)
-
-        @pl.when(jnp.logical_not(odd))
-        def _():
-            work(b_ref, a_ref, c)
+
+    def work(right_ref, left_ref):
+        def chunk(c, carry):
+            copy(c).wait()
+            for at in range(size):
+                k = c * size + at
+                rights, lefts = [], []
+                for g in range(2):
+                    s = s_ref[g, k]
+                    t = moved(s, weights)
+                    t_ref[g, k] = t
+                    rights.append(jnp.where(first, shifted(s, HALF, 0), t))
+                    lefts.append(jnp.where(first, down * s, shifted(down * t, HALF, 0)))
+                right_ref[k] = jnp.concatenate(rights, 0).astype(jnp.bfloat16)
+                left_ref[k] = jnp.concatenate(lefts, 0).astype(jnp.bfloat16)
+            return carry
+
+        lax.fori_loop(0, CHUNKS, chunk, 0)
+
+    @pl.when(odd)
+    def _():
+        work(a_ref, b_ref)
+
+    @pl.when(jnp.logical_not(odd))
+    def _():
+        work(b_ref, a_ref)
 
 
 def base_kernel(order_ref, rate_ref, conc_ref, emis_ref, part_ref, new_ref, m_ref, c_ref, e_ref, r_ref):
@@ -199,7 +219,7 @@
         for i in range(0, N, 2):
             for j in range(N):
                 pair = jnp.concatenate([m_ref[i * N + j], m_ref[(i + 1) * N + j]], 0)
-                factor_ref[block, j, i // 2] = pair.astype(jnp.bfloat16)
+                factor_ref[block, j, i // 2] = pair.astype(jnp.bfloat16).astype(jnp.float32)
         return carry
 
     lax.fori_loop(0, blocks, one, 0)
@@ -207,52 +227,76 @@
 
 
 def apply_kernel(
-    order_ref, weights_ref, s_ref, source_ref, a_ref, b_ref, factor_ref, conc_part_ref, out_ref, part_ref
+    order_ref,
+    weights_ref,
+    s_ref,
+    t_ref,
+    source_ref,
+    a_ref,
+    b_ref,
+    factor_ref,
+    conc_part_ref,
+    out_ref,
+    part_ref,
+    even_ref,
+    odd_ref,
 ):
     species = s_ref.shape[1]
+    blocks = species // N
     odd = lax.axis_index("cols") % 2 == 1
     extra = jnp.where(odd, a_ref[species].astype(jnp.float32), b_ref[species].astype(jnp.float32))
     extra = extra[:ROWS]
-    upper = extra + shifted(extra, HALF, 0)
     first = lax.broadcasted_iota(jnp.int32, (ROWS, LANES), 0) < HALF
+    upper = jnp.where(first, 0.0, extra + shifted(extra, HALF, 0))
     up_x = weights_ref[0]
-    own = weights_ref[1] - jnp.where(first, 0.0, upper)
-    weights = (own, weights_ref[2], weights_ref[3], weights_ref[4])
-    minus = tuple(-w for w in weights)
-
-    def one(block, carry):
-        values = [[None] * N, [None] * N]
+    minus = (upper - weights_ref[1],) + tuple(-weights_ref[at] for at in range(2, 5))
+
+    def values(block, j, ref):
+        k = order_ref[block * N + j]
+        wide_a = a_ref[k].astype(jnp.float32)
+        wide_b = b_ref[k].astype(jnp.float32)
+        left = jnp.where(odd, wide_b, wide_a)
+        right = jnp.where(odd, wide_a, wide_b)
+        for g in range(2):
+            a = left[g * ROWS : (g + 1) * ROWS]
+            b = right[g * ROWS : (g + 1) * ROWS]
+            inflow = up_x * a
+            halo_0 = jnp.where(first, inflow, shifted(b, HALF, 0))
+            halo_1 = jnp.where(first, up_x * (shifted(a, HALF, 0) - inflow), b)
+            s = (t_ref[g, k] - upper * s_ref[g, k]) + halo_0
+            s = moved(s, minus) - halo_1
+            ref[j * 2 + g] = s - source_ref[g, k].astype(jnp.float32)
+
+    def products(block, i, ref):
+        sums = [[None, None], [None, None]]
         for j in range(N):
-            k = order_ref[block * N + j]
-            wide_a = a_ref[k].astype(jnp.float32)
-            wide_b = b_ref[k].astype(jnp.float32)
-            left = jnp.where(odd, wide_b, wide_a)
-            right = jnp.where(odd, wide_a, wide_b)
+            wide = factor_ref[block, j, i]
+            for h in range(2):
+                f = wide[h * ROWS : (h + 1) * ROWS]
+                for g in range(2):
+                    term = f * ref[j * 2 + g]
+                    sums[g][h] = term if sums[g][h] is None else sums[g][h] + term
+        for h in range(2):
+            k = order_ref[block * N + 2 * i + h]
             for g in range(2):
-                a = left[g * ROWS : (g + 1) * ROWS]
-                b = right[g * ROWS : (g + 1) * ROWS]
-                inflow = up_x * a
-                halo_0 = jnp.where(first, inflow, shifted(b, HALF, 0))
-                halo_1 = jnp.where(first, up_x * (shifted(a, HALF, 0) - inflow), b)
-                s = moved(s_ref[g, k], weights) + halo_0
-                s = moved(s, minus) - halo_1
-                values[g][j] = s - source_ref[g, k].astype(jnp.float32)
-        for i in range(0, N, 2):
-            sums = [[None, None], [None, None]]
-            for j in range(N):
-                wide = factor_ref[block, j, i // 2].astype(jnp.float32)
-                for h in range(2):
-                    f = wide[h * ROWS : (h + 1) * ROWS]
-                    for g in range(2):
-                        term = f * values[g][j]
-                        sums[g][h] = term if sums[g][h] is None else sums[g][h] + term
-            for h in range(2):
-                k = order_ref[block * N + i + h]
-                for g in range(2):
-                    out_ref[g, k] = sums[g][h]
+                out_ref[g, k] = sums[g][h]
+
+    for j in range(N):
+        values(0, j, even_ref)
+
+    def two(pair, carry):
+        block = 2 * pair
+        for now, later, ref, other in (
+            (block, block + 1, even_ref, odd_ref),
+            (block + 1, lax.rem(block + 2, blocks), odd_ref, even_ref),
+        ):
+            for i in range(N // 2):
+                products(now, i, ref)
+                values(later, 2 * i, other)
+                values(later, 2 * i + 1, other)
         return carry
 
-    lax.fori_loop(0, species // N, one, 0)
+    lax.fori_loop(0, blocks // 2, two, 0)
     tiles = part_ref.shape[0]
     for g in range(2):
         row = lane_sums(jnp.sum(out_ref[g], axis=1))[:1]
@@ -311,17 +355,23 @@
     for k in range(1, links):
         mine.append(crossed(concentration, 2 * k))
     message = pltpu.VMEM((species + 1, 2 * ROWS, LANES), jnp.bfloat16)
-    a, b, s_near, weights = pl.pallas_call(
+    a, b, s_near, t_near, weights = pl.pallas_call(
         message_kernel,
         out_shape=(
             message,
             message,
             pltpu.VMEM(s.shape, jnp.float32),
+            pltpu.VMEM(s.shape, jnp.float32),
             pltpu.VMEM((5, ROWS, LANES), jnp.float32),
         ),
-        in_specs=[VMEM] * 4 + [ANY],
-        out_specs=(VMEM,) * 4,
-        scratch_shapes=[pltpu.SemaphoreType.DMA((CHUNKS,))],
+        in_specs=[ANY] * 5,
+        out_specs=(VMEM,) * 5,
+        scratch_shapes=[
+            pltpu.VMEM((2, ROWS, LANES), jnp.float32),
+            pltpu.VMEM((2, ROWS, LANES), jnp.int32),
+            pltpu.SemaphoreType.DMA((4,)),
+            pltpu.SemaphoreType.DMA((CHUNKS,)),
+        ],
         compiler_params=SMALL,
         name="messages",
     )(*map(far, winds), far(s))
@@ -356,7 +406,7 @@
     factors, source_near = pl.pallas_call(
         factor_kernel,
         out_shape=(
-            pltpu.VMEM((blocks, N, N // 2, 2 * ROWS, LANES), jnp.bfloat16),
+            pltpu.VMEM((blocks, N, N // 2, 2 * ROWS, LANES), jnp.float32),
             pltpu.VMEM(source.shape, source.dtype),
         ),
         in_specs=[SMEM, SMEM, VMEM, VMEM, ANY],
@@ -376,14 +426,16 @@
             pltpu.VMEM(s.shape, jnp.float32),
             pltpu.VMEM((tiles, 3, LANES), jnp.float32),
         ),
-        in_specs=[SMEM] + [VMEM] * 7,
+        in_specs=[SMEM] + [VMEM] * 8,
         out_specs=(VMEM, VMEM),
+        scratch_shapes=[pltpu.VMEM((2 * N, ROWS, LANES), jnp.float32)] * 2,
         compiler_params=SMALL,
         name="apply",
     )(
         far(species_order),
         near(weights),
         near(s_near),
+        near(t_near),
         near(source_near),
         near(a),
         near(b),

time: 96.2 us -> 94.6 us (0.983)
  Pallas kernels: 24.3 us -> 22.7 us
    pallas_call x1, Pallas kernels: 3.48 us -> 2.46 us  [step(): pl.pallas_call(message_kernel, out_shape=(message, message, pltpu.VMEM(s....]
    pallas_call x1, Pallas kernels: 5.14 us -> 4.14 us  [step(): pl.pallas_call(apply_kernel, out_shape=(pltpu.VMEM(s.shape, jnp.float32),...]
where the time goes in v4:
time: 94.6 us; the launch traced here: 94.2 us
  waiting for transfers between devices  41.5 us (44%)
  starting transfers between devices  27.4 us (29%)
  Pallas kernels  22.7 us (24%)
  local copies, waits for them, and re-layouts  0.97 us (1%)
    ppermute x8, waiting for transfers between devices, crossed(): lax.ppermute(value, 'params', [(i, i ^ bits) for i in range(lax.axis_size...  31.3 us
    pallas_call x1, Pallas kernels, step(): pl.pallas_call(factor_kernel, out_shape=(pltpu.VMEM((blocks, N, N // 2, 2...  12.3 us
    ppermute x2, starting transfers between devices, swapped(): return lax.ppermute(value, 'cols', pairs + [(b, a) for a, b in pairs])  11.6 us
    all_to_all x1, waiting for transfers between devices, step(): everything = lax.all_to_all(parts, 'cols', 0, 0, tiled=True)  10.2 us
    all_to_all x1, starting transfers between devices, step(): everything = lax.all_to_all(parts, 'cols', 0, 0, tiled=True)  7.98 us
    ppermute x8, starting transfers between devices, crossed(): lax.ppermute(value, 'params', [(i, i ^ bits) for i in range(lax.axis_size...  7.82 us
    pallas_call x1, Pallas kernels, step(): pl.pallas_call(apply_kernel, out_shape=(pltpu.VMEM(s.shape, jnp.float32),...  4.14 us
    pallas_call x1, Pallas kernels, step(): pl.pallas_call(base_kernel, out_shape=(pltpu.VMEM((ROWS, LANES), jnp.floa...  3.16 us
  transfers between devices with their start and end apart: 11, of which 7 were waited for; matrix products, arithmetic and copies ran while one was open for 2% of the time, Pallas kernels for 16%

profile of v4, /device:TPU:2, one launch (start us, length us, event | category | flops | bytes accessed | tf_op | source)
XLA Modules:
  0.0 94.2 jit_solution(12513272661957257147)
XLA Ops:
  0.6 2.5 %messages.1 = (bf16[129,16,128]{2,1,0:T(8,128)(2,1)S(1)}, bf16[129,16,128]{2,1,0:T(8,128)(2,1)S(1)}, f32[2,128,8,128]{3,2,1,0:T(8,128)S(1)}, f32[2,128,8,128]{3,2,1,0:T(8,128)S(1)}, f32[5,8,128]{2,1,0:T(8,128)S(1)}) custom-call(f32[8,128]{1,0:T(8,128)} %bitcast.19, s32[8,128]{1,0:T(8,128)} %bitcast.20, f32[8,128]{1,0:T(8,128)} %bitcast.21, ...), custom_call_target="tpu_custom_call" | custom-call | tf_op jit(solution)/shard_map/messages/pallas_call | solution.py:358
  3.1 11.5 %collective-permute-start.4 = (bf16[129,16,128]{2,1,0:T(8,128)(2,1)S(1)}, bf16[129,16,128]{2,1,0:T(8,128)(2,1)S(1)}, u32[]{:S(2)}, u32[]{:S(2)}) collective-permute-start(bf16[129,16,128]{2,1,0:T(8,128)(2,1)S(1)} %get-tuple-element.22), channel_id=1, source_target_pairs={{8,16},{24,32},{40,48},{56,64},{72,80},{88,96},{104,112},{120,128}... | collective-permute-start | bytes 1585160 | tf_op jit(solution)/shard_map/ppermute | solution.py:330
  14.6 0.1 collective-permute-start.5
  14.7 1.1 %collective-permute-start = (f32[128,128]{1,0:T(8,128)}, f32[128,128]{1,0:T(8,128)S(1)}, u32[]{:S(2)}, u32[]{:S(2)}) collective-permute-start(f32[128,128]{1,0:T(8,128)} %conc_ref.1), channel_id=1, source_target_pairs={{0,2},{1,3},{2,0},{3,1},{4,6},{5,7},{6,4},{7,5},{8,10},{9,11},{10,... | collective-permute-start | bytes 196616 | tf_op jit(solution)/shard_map/ppermute | solution.py:322
  15.8 1.9 %collective-permute-start.2 = (f32[128,128]{1,0:T(8,128)}, f32[128,128]{1,0:T(8,128)S(1)}, u32[]{:S(2)}, u32[]{:S(2)}) collective-permute-start(f32[128,128]{1,0:T(8,128)} %conc_ref.1), channel_id=1, source_target_pairs={{0,6},{1,7},{2,4},{3,5},{4,2},{5,3},{6,0},{7,1},{8,14},{9,15},{10,... | collective-permute-start | bytes 196616 | tf_op jit(solution)/shard_map/ppermute | solution.py:322
  17.8 0.6 collective-permute-start.1
  18.3 23.2 %collective-permute-done = f32[128,128]{1,0:T(8,128)S(1)} collective-permute-done((f32[128,128]{1,0:T(8,128)}, f32[128,128]{1,0:T(8,128)S(1)}, u32[]{:S(2)}, u32[]{:S(2)}) %collective-permute-start) | collective-permute-done | bytes 65568 | tf_op jit(solution)/shard_map/ppermute | solution.py:322
  41.6 0.0 collective-permute-done.2
  41.6 1.8 %collective-permute-done.1 = f32[128,128]{1,0:T(8,128)S(1)} collective-permute-done((f32[128,128]{1,0:T(8,128)}, f32[128,128]{1,0:T(8,128)S(1)}, u32[]{:S(2)}, u32[]{:S(2)}) %collective-permute-start.1) | collective-permute-done | bytes 65568 | tf_op jit(solution)/shard_map/ppermute | solution.py:322
  43.4 0.9 pad_maximum_fusion.mine_ref
  44.3 0.1 collective-permute-start.3
  44.4 3.2 %base.1 = (f32[8,128]{1,0:T(8,128)S(1)}, f32[128,128]{1,0:T(8,128)}) custom-call(s32[128]{0:T(128)} %order_ref.5, f32[8,16,16]{2,1,0:T(8,128)} %rate_ref.3, f32[128,128]{1,0:T(8,128)} %conc_ref.1, f32[128,128]{1,0:T(8,128)} %emis_ref.1), custom_call_target="tpu_custom_call" | custom-call | tf_op jit(solution)/shard_map/base/pallas_call | solution.py:383
  47.5 0.5 collective-permute-start.6
  48.0 0.8 collective-permute-done.6
  48.9 3.6 %collective-permute-start.9 = (f32[8,128]{1,0:T(8,128)S(1)}, f32[8,128]{1,0:T(8,128)S(1)}, u32[]{:S(2)}, u32[]{:S(2)}) collective-permute-start(f32[8,128]{1,0:T(8,128)S(1)} %add.12), channel_id=1, source_target_pairs={{0,6},{1,7},{2,4},{3,5},{4,2},{5,3},{6,0},{7,1},{8,14},{9,15},{10,... | collective-permute-start | bytes 12296 | tf_op jit(solution)/shard_map/ppermute | solution.py:322
  52.5 1.8 %collective-permute-done.9 = f32[8,128]{1,0:T(8,128)S(1)} collective-permute-done((f32[8,128]{1,0:T(8,128)S(1)}, f32[8,128]{1,0:T(8,128)S(1)}, u32[]{:S(2)}, u32[]{:S(2)}) %collective-permute-start.9) | collective-permute-done | bytes 4128 | tf_op jit(solution)/shard_map/ppermute | solution.py:322
  54.3 2.7 %collective-permute-done.8 = f32[8,128]{1,0:T(8,128)S(1)} collective-permute-done((f32[8,128]{1,0:T(8,128)S(1)}, f32[8,128]{1,0:T(8,128)S(1)}, u32[]{:S(2)}, u32[]{:S(2)}) %collective-permute-start.8) | collective-permute-done | bytes 4128 | tf_op jit(solution)/shard_map/ppermute | solution.py:322
  57.0 0.9 collective-permute-done.7
  57.9 12.3 %factors.1 = (f32[8,16,8,16,128]{4,3,2,1,0:T(8,128)S(1)}, bf16[2,128,8,128]{3,2,1,0:T(8,128)(2,1)S(1)}) custom-call(s32[128]{0:T(128)} %order_ref.5, f32[8,16,16]{2,1,0:T(8,128)} %rate_ref.3, f32[4,128,128]{2,1,0:T(8,128)S(1)} %pad_maximum_fusion.mine_ref, f32[4,128,128]{2,1,0:T(8,128)S(1)} %collective-permute-done.3.other_ref, bf16[2,128,8,128]{3,2,1,0:T(8,128)(2,1)} %bitcast.14), custom_call_target="tpu_custom_call" | custom-call | tf_op jit(solution)/shard_map/factors/pallas_call | solution.py:406
  70.2 4.1 %apply.1 = (f32[2,128,8,128]{3,2,1,0:T(8,128)S(1)}, f32[32,3,128]{2,1,0:T(4,128)}) custom-call(s32[128]{0:T(128)} %order_ref.5, f32[5,8,128]{2,1,0:T(8,128)S(1)} %get-tuple-element.18.weights_ref, f32[2,128,8,128]{3,2,1,0:T(8,128)S(1)} %get-tuple-element.19.s_ref, f32[2,128,8,128]{3,2,1,0:T(8,128)S(1)} %get-tuple-element.20.t_ref, ...), custom_call_target="tpu_custom_call" | custom-call | tf_op jit(solution)/shard_map/apply/pallas_call | solution.py:423
  74.4 8.0 %all-to-all-start = ((f32[32,3,128]{2,1,0:T(4,128)}), f32[32,3,128]{2,1,0:T(4,128)S(1)}, u32[]{:S(2)}, u32[]{:S(2)}) async-start(f32[32,3,128]{2,1,0:T(4,128)} %get-tuple-element.27), calls=%async_computation | async-start | bytes 131072 | tf_op jit(solution)/shard_map/all_to_all | solution.py:446
  82.4 1.0 %copy.14 = f32[2,128,2,4,128]{4,3,2,1,0:T(4,128)} copy(f32[2,128,2,4,128]{4,3,2,1,0:T(4,128)S(1)} %bitcast.12) | data formatting | bytes 2097152
  83.3 10.2 %all-to-all-done.parts_ref = f32[32,3,128]{2,1,0:T(4,128)S(1)} async-done(((f32[32,3,128]{2,1,0:T(4,128)}), f32[32,3,128]{2,1,0:T(4,128)S(1)}, u32[]{:S(2)}, u32[]{:S(2)}) %all-to-all-start) | async-done | bytes 49184 | tf_op jit(solution)/shard_map/all_to_all | solution.py:446
  93.6 0.6 means.1
  (7 shorter events, 0.0 us)
Async XLA Ops:
  3.1 67.1 %collective-permute-start.4 = (bf16[129,16,128]{2,1,0:T(8,128)(2,1)S(1)}, bf16[129,16,128]{2,1,0:T(8,128)(2,1)S(1)}, u32[]{:S(2)}, u32[]{:S(2)}) collective-permute-start(bf16[129,16,128]{2,1,0:T(8,128)(2,1)S(1)} %get-tuple-element.22), channel_id=1, source_target_pairs={{8,16},{24,32},{40,48},{56,64},{72,80},{88,96},{104,112},{120,128}... | collective-permute-start | bytes 1585160 | tf_op jit(solution)/shard_map/ppermute | solution.py:330
  14.6 55.6 %collective-permute-start.5 = (bf16[129,16,128]{2,1,0:T(8,128)(2,1)S(1)}, bf16[129,16,128]{2,1,0:T(8,128)(2,1)S(1)}, u32[]{:S(2)}, u32[]{:S(2)}) collective-permute-start(bf16[129,16,128]{2,1,0:T(8,128)(2,1)S(1)} %get-tuple-element.23), channel_id=1, source_target_pairs={{0,8},{16,24},{32,40},{48,56},{64,72},{80,88},{96,104},{112,120},{... | collective-permute-start | bytes 1585160 | tf_op jit(solution)/shard_map/ppermute | solution.py:330
  14.7 26.8 %collective-permute-start = (f32[128,128]{1,0:T(8,128)}, f32[128,128]{1,0:T(8,128)S(1)}, u32[]{:S(2)}, u32[]{:S(2)}) collective-permute-start(f32[128,128]{1,0:T(8,128)} %conc_ref.1), channel_id=1, source_target_pairs={{0,2},{1,3},{2,0},{3,1},{4,6},{5,7},{6,4},{7,5},{8,10},{9,11},{10,... | collective-permute-start | bytes 196616 | tf_op jit(solution)/shard_map/ppermute | solution.py:322
  15.8 25.7 %collective-permute-start.2 = (f32[128,128]{1,0:T(8,128)}, f32[128,128]{1,0:T(8,128)S(1)}, u32[]{:S(2)}, u32[]{:S(2)}) collective-permute-start(f32[128,128]{1,0:T(8,128)} %conc_ref.1), channel_id=1, source_target_pairs={{0,6},{1,7},{2,4},{3,5},{4,2},{5,3},{6,0},{7,1},{8,14},{9,15},{10,... | collective-permute-start | bytes 196616 | tf_op jit(solution)/shard_map/ppermute | solution.py:322
  17.8 25.6 %collective-permute-start.1 = (f32[128,128]{1,0:T(8,128)}, f32[128,128]{1,0:T(8,128)S(1)}, u32[]{:S(2)}, u32[]{:S(2)}) collective-permute-start(f32[128,128]{1,0:T(8,128)} %conc_ref.1), channel_id=1, source_target_pairs={{0,4},{1,5},{2,6},{3,7},{4,0},{5,1},{6,2},{7,3},{8,12},{9,13},{10,... | collective-permute-start | bytes 196616 | tf_op jit(solution)/shard_map/ppermute | solution.py:322
  44.3 13.6 %collective-permute-start.3 = (f32[4,128,128]{2,1,0:T(8,128)S(1)}, f32[4,128,128]{2,1,0:T(8,128)S(1)}, u32[]{:S(2)}, u32[]{:S(2)}) collective-permute-start(f32[4,128,128]{2,1,0:T(8,128)S(1)} %pad_maximum_fusion.mine_ref), channel_id=1, source_target_pairs={{0,1},{1,0},{2,3},{3,2},{4,5},{5,4},{6,7},{7,6},{8,9},{9,8},{10,11... | collective-permute-start | bytes 786440 | tf_op jit(solution)/shard_map/ppermute | solution.py:322
  47.5 1.3 %collective-permute-start.6 = (f32[8,128]{1,0:T(8,128)S(1)}, f32[8,128]{1,0:T(8,128)S(1)}, u32[]{:S(2)}, u32[]{:S(2)}) collective-permute-start(f32[8,128]{1,0:T(8,128)S(1)} %get-tuple-element.25), channel_id=1, source_target_pairs={{0,1},{1,0},{2,3},{3,2},{4,5},{5,4},{6,7},{7,6},{8,9},{9,8},{10,11... | collective-permute-start | bytes 12296 | tf_op jit(solution)/shard_map/ppermute | solution.py:322
  48.9 5.4 %collective-permute-start.9 = (f32[8,128]{1,0:T(8,128)S(1)}, f32[8,128]{1,0:T(8,128)S(1)}, u32[]{:S(2)}, u32[]{:S(2)}) collective-permute-start(f32[8,128]{1,0:T(8,128)S(1)} %add.12), channel_id=1, source_target_pairs={{0,6},{1,7},{2,4},{3,5},{4,2},{5,3},{6,0},{7,1},{8,14},{9,15},{10,... | collective-permute-start | bytes 12296 | tf_op jit(solution)/shard_map/ppermute | solution.py:322
  52.5 4.5 %collective-permute-start.8 = (f32[8,128]{1,0:T(8,128)S(1)}, f32[8,128]{1,0:T(8,128)S(1)}, u32[]{:S(2)}, u32[]{:S(2)}) collective-permute-start(f32[8,128]{1,0:T(8,128)S(1)} %add.12), channel_id=1, source_target_pairs={{0,4},{1,5},{2,6},{3,7},{4,0},{5,1},{6,2},{7,3},{8,12},{9,13},{10,... | collective-permute-start | bytes 12296 | tf_op jit(solution)/shard_map/ppermute | solution.py:322
  54.3 3.6 %collective-permute-start.7 = (f32[8,128]{1,0:T(8,128)S(1)}, f32[8,128]{1,0:T(8,128)S(1)}, u32[]{:S(2)}, u32[]{:S(2)}) collective-permute-start(f32[8,128]{1,0:T(8,128)S(1)} %add.12), channel_id=1, source_target_pairs={{0,2},{1,3},{2,0},{3,1},{4,6},{5,7},{6,4},{7,5},{8,10},{9,11},{10,... | collective-permute-start | bytes 12296 | tf_op jit(solution)/shard_map/ppermute | solution.py:322
  74.4 19.2 %all-to-all-start = ((f32[32,3,128]{2,1,0:T(4,128)}), f32[32,3,128]{2,1,0:T(4,128)S(1)}, u32[]{:S(2)}, u32[]{:S(2)}) async-start(f32[32,3,128]{2,1,0:T(4,128)} %get-tuple-element.27), calls=%async_computation | async-start | bytes 131072 | tf_op jit(solution)/shard_map/all_to_all | solution.py:446

commit v5 on v4

--- a/solution.py
+++ b/solution.py
@@ -1,4 +1,5 @@
 import functools
+import math
 
 import jax
 import jax.numpy as jnp
@@ -12,6 +13,9 @@
 HALF = ROWS // 2
 N = 16
 CHUNKS = 8
+RUN = 4
+LEAST, SPAN = 0.2, math.log(25.0)
+TOP, CENTRE = 65535.0, 32768.0
 HIGHEST = lax.Precision.HIGHEST
 VMEM = pl.BlockSpec(memory_space=pltpu.VMEM)
 SMEM = pl.BlockSpec(memory_space=pltpu.SMEM)
@@ -94,8 +98,37 @@
     return lax.dot_general(ones, rows, (((1,), (1,)), ((), ())), precision=HIGHEST)
 
 
+def coded(unit):
+    steps = jnp.clip(jnp.floor(unit * TOP + 0.5), 0.0, TOP) - CENTRE
+    return steps.astype(jnp.int32).astype(jnp.int16)
+
+
+def decoded(code):
+    return (code.astype(jnp.int32).astype(jnp.float32) + CENTRE) * (1.0 / TOP)
+
+
+def packet_kernel(conc_ref, emis_ref, packet_ref):
+    packet_ref[0] = coded(jnp.log(conc_ref[...] * (1.0 / LEAST)) * (1.0 / SPAN))
+    packet_ref[1] = coded(emis_ref[...])
+
+
 def message_kernel(
-    cx_hbm, ux_hbm, cy_hbm, uy_hbm, s_hbm, a_ref, b_ref, s_ref, t_ref, weights_ref, reals_ref, flags_ref, wind_sem, sems
+    cx_hbm,
+    ux_hbm,
+    cy_hbm,
+    uy_hbm,
+    s_hbm,
+    a_ref,
+    b_ref,
+    half_0_ref,
+    half_1_ref,
+    s_ref,
+    t_ref,
+    weights_ref,
+    reals_ref,
+    flags_ref,
+    wind_sem,
+    sems,
 ):
     species = s_ref.shape[1]
     size = species // CHUNKS
@@ -134,8 +167,9 @@
     odd = lax.axis_index("cols") % 2 == 1
     a_ref[species] = extra
     b_ref[species] = extra
-
-    def work(right_ref, left_ref):
+    half_0_ref[species] = extra[:ROWS]
+
+    def work(right_ref, left_ref, to_right):
         def chunk(c, carry):
             copy(c).wait()
             for at in range(size):
@@ -149,80 +183,79 @@
                     lefts.append(jnp.where(first, down * s, shifted(down * t, HALF, 0)))
                 right_ref[k] = jnp.concatenate(rights, 0).astype(jnp.bfloat16)
                 left_ref[k] = jnp.concatenate(lefts, 0).astype(jnp.bfloat16)
+                halves = rights if to_right else lefts
+                half_0_ref[k] = halves[0].astype(jnp.bfloat16)
+                half_1_ref[k] = halves[1].astype(jnp.bfloat16)
             return carry
 
         lax.fori_loop(0, CHUNKS, chunk, 0)
 
     @pl.when(odd)
     def _():
-        work(a_ref, b_ref)
+        work(a_ref, b_ref, True)
 
     @pl.when(jnp.logical_not(odd))
     def _():
-        work(b_ref, a_ref)
-
-
-def base_kernel(order_ref, rate_ref, conc_ref, emis_ref, part_ref, new_ref, m_ref, c_ref, e_ref, r_ref):
-    species = conc_ref.shape[0]
-    blocks = species // N
-    for b in range(blocks):
-        for j in range(N):
-            k = order_ref[b * N + j]
-            c_ref[pl.ds(j * ROWS + b, 1), :] = conc_ref[pl.ds(k, 1), :]
-            e_ref[pl.ds(j * ROWS + b, 1), :] = emis_ref[pl.ds(k, 1), :]
-    conc = [c_ref[pl.ds(j * ROWS, ROWS), :] for j in range(N)]
-
-    for b in range(blocks):
-        for i in range(N):
-            r_ref[pl.ds(i * ROWS + b, 1), :] = rate_ref[b, pl.ds(i, 1), :]
-
-    def rate(i, j):
-        return jnp.broadcast_to(r_ref[pl.ds(i * ROWS, ROWS), j : j + 1], (ROWS, LANES))
-
-    minus_system(m_ref, conc, rate)
-    inverted(m_ref)
-    values = [
-        -(c_ref[pl.ds(j * ROWS, ROWS), :] + e_ref[pl.ds(j * ROWS, ROWS), :]) for j in range(N)
-    ]
-    for i in range(N):
-        total = None
-        for j in range(N):
-            term = m_ref[i * N + j].astype(jnp.bfloat16).astype(jnp.float32) * values[j]
-            total = term if total is None else total + term
-        e_ref[pl.ds(i * ROWS, ROWS), :] = total
-    for b in range(blocks):
-        for i in range(N):
-            k = order_ref[b * N + i]
-            new_ref[pl.ds(k, 1), :] = e_ref[pl.ds(i * ROWS + b, 1), :]
-    part_ref[...] = lane_sums(new_ref[...])
+        work(b_ref, a_ref, False)
 
 
 def factor_kernel(
-    order_ref, rate_ref, mine_ref, other_ref, source_hbm, factor_ref, source_ref, cells_ref, m_ref, sem
+    order_ref,
+    rate_ref,
+    mine_ref,
+    other_ref,
+    conc_ref,
+    emis_ref,
+    source_hbm,
+    factor_ref,
+    new_ref,
+    part_ref,
+    source_ref,
+    cells_ref,
+    added_ref,
+    all_ref,
+    m_ref,
+    sem,
 ):
-    links, species = mine_ref.shape[:2]
+    links, _, species = mine_ref.shape[:3]
     blocks = species // N
     copy = pltpu.make_async_copy(source_hbm, source_ref, sem)
     copy.start()
     place = lax.axis_index("params")
     for k in range(links):
         for core, ref in enumerate((mine_ref, other_ref)):
-            cells_ref[pl.ds(place ^ (2 * k + core), species, stride=ROWS), :] = ref[k]
+            rows = pl.ds(place ^ (2 * k + core), species, stride=ROWS)
+            if k == 0 and core == 0:
+                cells_ref[rows, :] = conc_ref[...]
+                added_ref[rows, :] = emis_ref[...]
+            else:
+                cells_ref[rows, :] = LEAST * jnp.exp(SPAN * decoded(ref[k, 0]))
+                added_ref[rows, :] = decoded(ref[k, 1])
 
     def one(block, carry):
-        conc = [
-            cells_ref[pl.ds(pl.multiple_of(order_ref[block * N + j] * ROWS, ROWS), ROWS), :]
-            for j in range(N)
+        tiles = [
+            pl.ds(pl.multiple_of(order_ref[block * N + j] * ROWS, ROWS), ROWS) for j in range(N)
         ]
+        conc = [cells_ref[tile, :] for tile in tiles]
         minus_system(m_ref, conc, lambda i, j: rate_ref[block, i, j])
         inverted(m_ref)
+        values = [-(cells_ref[tile, :] + added_ref[tile, :]) for tile in tiles]
         for i in range(0, N, 2):
+            sums = [None, None]
             for j in range(N):
                 pair = jnp.concatenate([m_ref[i * N + j], m_ref[(i + 1) * N + j]], 0)
-                factor_ref[block, j, i // 2] = pair.astype(jnp.bfloat16).astype(jnp.float32)
+                wide = pair.astype(jnp.bfloat16).astype(jnp.float32)
+                factor_ref[block, j, i // 2] = wide
+                for h in range(2):
+                    term = wide[h * ROWS : (h + 1) * ROWS] * values[j]
+                    sums[h] = term if sums[h] is None else sums[h] + term
+            for h in range(2):
+                all_ref[tiles[i + h], :] = sums[h]
         return carry
 
     lax.fori_loop(0, blocks, one, 0)
+    new_ref[...] = all_ref[pl.ds(place, species, stride=ROWS), :]
+    part_ref[...] = lane_sums(jnp.sum(all_ref[...].reshape(species, ROWS, LANES), axis=1))
     copy.wait()
 
 
@@ -234,6 +267,8 @@
     source_ref,
     a_ref,
     b_ref,
+    half_0_ref,
+    half_1_ref,
     factor_ref,
     conc_part_ref,
     out_ref,
@@ -243,9 +278,15 @@
 ):
     species = s_ref.shape[1]
     blocks = species // N
-    odd = lax.axis_index("cols") % 2 == 1
-    extra = jnp.where(odd, a_ref[species].astype(jnp.float32), b_ref[species].astype(jnp.float32))
-    extra = extra[:ROWS]
+    tile = lax.axis_index("cols")
+    odd = tile % 2 == 1
+    relayed = is_late(tile) & ((tile % RUN == 0) | (tile % RUN == RUN - 1))
+    extra_a = jnp.where(
+        relayed,
+        half_0_ref[species].astype(jnp.float32),
+        a_ref[species].astype(jnp.float32)[:ROWS],
+    )
+    extra = jnp.where(odd, extra_a, b_ref[species].astype(jnp.float32)[:ROWS])
     first = lax.broadcasted_iota(jnp.int32, (ROWS, LANES), 0) < HALF
     upper = jnp.where(first, 0.0, extra + shifted(extra, HALF, 0))
     up_x = weights_ref[0]
@@ -255,11 +296,13 @@
         k = order_ref[block * N + j]
         wide_a = a_ref[k].astype(jnp.float32)
         wide_b = b_ref[k].astype(jnp.float32)
-        left = jnp.where(odd, wide_b, wide_a)
-        right = jnp.where(odd, wide_a, wide_b)
-        for g in range(2):
-            a = left[g * ROWS : (g + 1) * ROWS]
-            b = right[g * ROWS : (g + 1) * ROWS]
+        for g, half_ref in enumerate((half_0_ref, half_1_ref)):
+            from_a = jnp.where(
+                relayed, half_ref[k].astype(jnp.float32), wide_a[g * ROWS : (g + 1) * ROWS]
+            )
+            from_b = wide_b[g * ROWS : (g + 1) * ROWS]
+            a = jnp.where(odd, from_b, from_a)
+            b = jnp.where(odd, from_a, from_b)
             inflow = up_x * a
             halo_0 = jnp.where(first, inflow, shifted(b, HALF, 0))
             halo_1 = jnp.where(first, up_x * (shifted(a, HALF, 0) - inflow), b)
@@ -324,10 +367,25 @@
     )
 
 
-def swapped(value, first):
-    devices = lax.axis_size("cols")
-    pairs = [(i, i + 1) for i in range(first, devices - 1, 2)]
-    return lax.ppermute(value, "cols", pairs + [(b, a) for a, b in pairs])
+def is_late(tile):
+    return (tile // RUN) % 2 == 1
+
+
+def edges(first):
+    pairs = [(i, i + 1) for i in range(first, lax.axis_size("cols") - 1, 2)]
+    return pairs + [(b, a) for a, b in pairs]
+
+
+def leaps():
+    return [
+        (a, a - 1 if a < b else a + 1, b)
+        for a, b in edges(1)
+        if a // RUN != b // RUN and not is_late(a)
+    ]
+
+
+def passed(value, pairs):
+    return lax.ppermute(value, "cols", pairs)
 
 
 def step(
@@ -351,21 +409,31 @@
     winds = [w.reshape(ROWS, LANES) for w in (courant_x, upwind_x, courant_y, upwind_y)]
 
     links = lax.axis_size("params") // 2
-    mine = [concentration]
+    message = pltpu.VMEM((species + 1, 2 * ROWS, LANES), jnp.bfloat16)
+    packet = pl.pallas_call(
+        packet_kernel,
+        out_shape=pltpu.VMEM((2, species, LANES), jnp.int16),
+        in_specs=[VMEM, VMEM],
+        out_specs=VMEM,
+        compiler_params=SMALL,
+        name="packet",
+    )(far(concentration), far(emissions))
+    mine = [packet]
     for k in range(1, links):
-        mine.append(crossed(concentration, 2 * k))
-    message = pltpu.VMEM((species + 1, 2 * ROWS, LANES), jnp.bfloat16)
-    a, b, s_near, t_near, weights = pl.pallas_call(
+        mine.append(crossed(packet, 2 * k))
+    a, b, half_0, half_1, s_near, t_near, weights = pl.pallas_call(
         message_kernel,
         out_shape=(
             message,
             message,
+            pltpu.VMEM((species + 1, ROWS, LANES), jnp.bfloat16),
+            pltpu.VMEM((species, ROWS, LANES), jnp.bfloat16),
             pltpu.VMEM(s.shape, jnp.float32),
             pltpu.VMEM(s.shape, jnp.float32),
             pltpu.VMEM((5, ROWS, LANES), jnp.float32),
         ),
         in_specs=[ANY] * 5,
-        out_specs=(VMEM,) * 5,
+        out_specs=(VMEM,) * 7,
         scratch_shapes=[
             pltpu.VMEM((2, ROWS, LANES), jnp.float32),
             pltpu.VMEM((2, ROWS, LANES), jnp.int32),
@@ -375,50 +443,44 @@
         compiler_params=SMALL,
         name="messages",
     )(*map(far, winds), far(s))
-    a = swapped(a, 1)
-    b = swapped(b, 0)
+    far_edges = leaps()
+    direct = [(u, v) for u, _, v in far_edges]
+    a = passed(a, [edge for edge in edges(1) if edge not in direct])
+    half_1 = passed(half_1, [(u, w) for u, w, _ in far_edges])
+    half_0 = passed(half_0, direct)
+    half_1 = passed(half_1, [(w, v) for _, w, v in far_edges])
+    b = passed(b, edges(0))
     mine = jnp.stack(mine)
     other = crossed(mine, 1)
 
-    conc_part, new_concentration = pl.pallas_call(
-        base_kernel,
-        out_shape=(
-            pltpu.VMEM((ROWS, LANES), jnp.float32),
-            jax.ShapeDtypeStruct((species, LANES), jnp.float32),
-        ),
-        in_specs=[SMEM, VMEM, VMEM, VMEM],
-        out_specs=(VMEM, VMEM),
-        scratch_shapes=[
-            pltpu.VMEM((N * N, ROWS, LANES), jnp.float32),
-            pltpu.VMEM((species, LANES), jnp.float32),
-            pltpu.VMEM((species, LANES), jnp.float32),
-            pltpu.VMEM((N * ROWS, N), jnp.float32),
-        ],
-        compiler_params=SMALL,
-        name="base",
-    )(far(species_order), far(rate_table), far(concentration), far(emissions))
-    conc_part = conc_part + crossed(conc_part, 1)
-    others = []
-    for k in range(1, links):
-        others.append(crossed(conc_part, 2 * k))
-    conc_part = sum(others, conc_part)
-
-    factors, source_near = pl.pallas_call(
+    factors, new_concentration, conc_part, source_near = pl.pallas_call(
         factor_kernel,
         out_shape=(
             pltpu.VMEM((blocks, N, N // 2, 2 * ROWS, LANES), jnp.float32),
+            jax.ShapeDtypeStruct((species, LANES), jnp.float32),
+            pltpu.VMEM((ROWS, LANES), jnp.float32),
             pltpu.VMEM(source.shape, source.dtype),
         ),
-        in_specs=[SMEM, SMEM, VMEM, VMEM, ANY],
-        out_specs=(VMEM,) * 2,
+        in_specs=[SMEM, SMEM, VMEM, VMEM, VMEM, VMEM, ANY],
+        out_specs=(VMEM,) * 4,
         scratch_shapes=[
+            pltpu.VMEM((species * ROWS, LANES), jnp.float32),
+            pltpu.VMEM((species * ROWS, LANES), jnp.float32),
             pltpu.VMEM((species * ROWS, LANES), jnp.float32),
             pltpu.VMEM((N * N, ROWS, LANES), jnp.float32),
             pltpu.SemaphoreType.DMA,
         ],
         compiler_params=SMALL,
         name="factors",
-    )(far(species_order), far(rate_table), near(mine), near(other), far(source))
+    )(
+        far(species_order),
+        far(rate_table),
+        near(mine),
+        near(other),
+        far(concentration),
+        far(emissions),
+        far(source),
+    )
 
     new_sens, parts = pl.pallas_call(
         apply_kernel,
@@ -426,7 +488,7 @@
             pltpu.VMEM(s.shape, jnp.float32),
             pltpu.VMEM((tiles, 3, LANES), jnp.float32),
         ),
-        in_specs=[SMEM] + [VMEM] * 8,
+        in_specs=[SMEM] + [VMEM] * 10,
         out_specs=(VMEM, VMEM),
         scratch_shapes=[pltpu.VMEM((2 * N, ROWS, LANES), jnp.float32)] * 2,
         compiler_params=SMALL,
@@ -439,6 +501,8 @@
         near(source_near),
         near(a),
         near(b),
+        near(half_0),
+        near(half_1),
         near(factors),
         near(conc_part),
     )

time: 94.6 us -> 86 us (0.909)
  the two profiles are of different devices: /device:TPU:2 before, /device:TPU:32 now
where the time goes in v5:
time: 86 us; the launch traced here: 85.6 us
  starting transfers between devices  37.8 us (44%)
  Pallas kernels  23.3 us (27%)
  waiting for transfers between devices  22.8 us (27%)
  local copies, waits for them, and re-layouts  0.97 us (1%)
    all_to_all x1, starting transfers between devices, step(): everything = lax.all_to_all(parts, 'cols', 0, 0, tiled=True)  27.1 us
    pallas_call x1, Pallas kernels, step(): pl.pallas_call(factor_kernel, out_shape=(pltpu.VMEM((blocks, N, N // 2, 2...  14.8 us
    all_to_all x1, waiting for transfers between devices, step(): everything = lax.all_to_all(parts, 'cols', 0, 0, tiled=True)  11.4 us
    ppermute x4, waiting for transfers between devices, crossed(): lax.ppermute(value, 'params', [(i, i ^ bits) for i in range(lax.axis_size...  11.4 us
    ppermute x5, starting transfers between devices, passed(): return lax.ppermute(value, 'cols', pairs)  7.16 us
    pallas_call x1, Pallas kernels, step(): pl.pallas_call(apply_kernel, out_shape=(pltpu.VMEM(s.shape, jnp.float32),...  4.45 us
    ppermute x4, starting transfers between devices, crossed(): lax.ppermute(value, 'params', [(i, i ^ bits) for i in range(lax.axis_size...  3.55 us
    pallas_call x1, Pallas kernels, step(): pl.pallas_call(message_kernel, out_shape=(message, message, pltpu.VMEM((s...  2.5 us
  transfers between devices with their start and end apart: 10, of which 4 were waited for; matrix products, arithmetic and copies ran while one was open for 1% of the time, Pallas kernels for 18%

profile of v5, /device:TPU:32, one launch (start us, length us, event | category | flops | bytes accessed | tf_op | source)
XLA Modules:
  0.0 85.6 jit_solution(7241381781519056401)
XLA Ops:
  0.6 2.5 %messages.1 = (bf16[129,16,128]{2,1,0:T(8,128)(2,1)S(1)}, bf16[129,16,128]{2,1,0:T(8,128)(2,1)S(1)}, bf16[129,8,128]{2,1,0:T(8,128)(2,1)S(1)}, bf16[128,8,128]{2...) custom-call(f32[8,128]{1,0:T(8,128)} %bitcast.19, ...), custom_call_target="tpu_custom_call" | custom-call | tf_op jit(solution)/shard_map/messages/pallas_call | solution.py:424
  3.1 0.7 collective-permute-start.4
  3.8 4.5 %collective-permute-start.5 = (bf16[129,16,128]{2,1,0:T(8,128)(2,1)S(1)}, bf16[129,16,128]{2,1,0:T(8,128)(2,1)S(1)}, u32[]{:S(2)}, u32[]{:S(2)}) collective-permute-start(bf16[129,16,128]{2,1,0:T(8,128)(2,1)S(1)} %get-tuple-element.25), channel_id=1, source_target_pairs={{0,8},{16,24},{32,40},{48,56},{64,72},{80,88},{96,104},{112,120},{... | collective-permute-start | bytes 1585160 | tf_op jit(solution)/shard_map/ppermute | solution.py:388
  8.3 0.7 collective-permute-start.7
  9.0 0.9 %packet.1 = s16[2,128,128]{2,1,0:T(8,128)(2,1)S(1)} custom-call(f32[128,128]{1,0:T(8,128)} %conc_ref.3, f32[128,128]{1,0:T(8,128)} %emis_ref.3), custom_call_target="tpu_custom_call" | custom-call | tf_op jit(solution)/shard_map/packet/pallas_call | solution.py:413
  9.9 2.0 %collective-permute-start.2 = (s16[2,128,128]{2,1,0:T(8,128)(2,1)S(1)}, s16[2,128,128]{2,1,0:T(8,128)(2,1)S(1)}, u32[]{:S(2)}, u32[]{:S(2)}) collective-permute-start(s16[2,128,128]{2,1,0:T(8,128)(2,1)S(1)} %packet.1), channel_id=1, source_target_pairs={{0,6},{1,7},{2,4},{3,5},{4,2},{5,3},{6,0},{7,1},{8,14},{9,15},{10,... | collective-permute-start | bytes 196616 | tf_op jit(solution)/shard_map/ppermute | solution.py:365
  11.9 1.5 %collective-permute-start.1 = (s16[2,128,128]{2,1,0:T(8,128)(2,1)S(1)}, s16[2,128,128]{2,1,0:T(8,128)(2,1)S(1)}, u32[]{:S(2)}, u32[]{:S(2)}) collective-permute-start(s16[2,128,128]{2,1,0:T(8,128)(2,1)S(1)} %packet.1), channel_id=1, source_target_pairs={{0,4},{1,5},{2,6},{3,7},{4,0},{5,1},{6,2},{7,3},{8,12},{9,13},{10,... | collective-permute-start | bytes 196616 | tf_op jit(solution)/shard_map/ppermute | solution.py:365
  13.4 7.0 %collective-permute-done.2 = s16[2,128,128]{2,1,0:T(8,128)(2,1)S(1)} collective-permute-done((s16[2,128,128]{2,1,0:T(8,128)(2,1)S(1)}, s16[2,128,128]{2,1,0:T(8,128)(2,1)S(1)}, u32[]{:S(2)}, u32[]{:S(2)}) %collective-permute-start.2) | collective-permute-done | bytes 65568 | tf_op jit(solution)/shard_map/ppermute | solution.py:365
  20.4 0.0 collective-permute-start
  20.4 0.0 collective-permute-done.1
  20.4 0.7 collective-permute-start.6
  21.0 3.6 %collective-permute-done = s16[2,128,128]{2,1,0:T(8,128)(2,1)S(1)} collective-permute-done((s16[2,128,128]{2,1,0:T(8,128)(2,1)S(1)}, s16[2,128,128]{2,1,0:T(8,128)(2,1)S(1)}, u32[]{:S(2)}, u32[]{:S(2)}) %collective-permute-start) | collective-permute-done | bytes 65568 | tf_op jit(solution)/shard_map/ppermute | solution.py:365
  24.6 0.1 collective-permute-start.3
  24.7 0.0 collective-permute-done.7
  24.8 0.7 collective-permute-start.8
  25.4 0.8 collective-permute-done.3.other_ref
  26.3 14.8 %factors.1 = (f32[8,16,8,16,128]{4,3,2,1,0:T(8,128)S(1)}, f32[128,128]{1,0:T(8,128)}, f32[8,128]{1,0:T(8,128)S(1)}, bf16[2,128,8,128]{3,2,1,0:T(8,128)(2,1)S(1)}) custom-call(s32[128]{0:T(128)} %order_ref.3, f32[8,16,16]{2,1,0:T(8,128)} %rate_ref.1, s16[4,2,128,128]{3,2,1,0:T(8,128)(2,1)S(1)} %pad_add_fusion.mine_ref, ...), custom_call_target="tpu_custom_call" | custom-call | tf_op jit(solution)/shard_map/factors/pallas_call | solution.py:456
  41.1 0.0 collective-permute-done.6.half_0_ref
  41.1 0.0 collective-permute-done.8.half_1_ref
  41.1 4.5 %apply.1 = (f32[2,128,8,128]{3,2,1,0:T(8,128)S(1)}, f32[32,3,128]{2,1,0:T(4,128)}) custom-call(s32[128]{0:T(128)} %order_ref.3, f32[5,8,128]{2,1,0:T(8,128)S(1)} %get-tuple-element.20.weights_ref, f32[2,128,8,128]{3,2,1,0:T(8,128)S(1)} %get-tuple-element.21.s_ref, f32[2,128,8,128]{3,2,1,0:T(8,128)S(1)} %get-tuple-element.22.t_ref, ...), custom_call_target="tpu_custom_call" | custom-call | tf_op jit(solution)/shard_map/apply/pallas_call | solution.py:485
  45.6 27.1 %all-to-all-start = ((f32[32,3,128]{2,1,0:T(4,128)}), f32[32,3,128]{2,1,0:T(4,128)S(1)}, u32[]{:S(2)}, u32[]{:S(2)}) async-start(f32[32,3,128]{2,1,0:T(4,128)} %get-tuple-element.31), calls=%async_computation | async-start | bytes 131072 | tf_op jit(solution)/shard_map/all_to_all | solution.py:510
  72.6 1.0 %copy.14 = f32[2,128,2,4,128]{4,3,2,1,0:T(4,128)} copy(f32[2,128,2,4,128]{4,3,2,1,0:T(4,128)S(1)} %bitcast.12) | data formatting | bytes 2097152
  73.6 11.4 %all-to-all-done.parts_ref = f32[32,3,128]{2,1,0:T(4,128)S(1)} async-done(((f32[32,3,128]{2,1,0:T(4,128)}), f32[32,3,128]{2,1,0:T(4,128)S(1)}, u32[]{:S(2)}, u32[]{:S(2)}) %all-to-all-start) | async-done | bytes 49184 | tf_op jit(solution)/shard_map/all_to_all | solution.py:510
  85.0 0.6 means.1
  (3 shorter events, 0.0 us)
Async XLA Ops:
  3.1 38.0 %collective-permute-start.4 = (bf16[129,16,128]{2,1,0:T(8,128)(2,1)S(1)}, bf16[129,16,128]{2,1,0:T(8,128)(2,1)S(1)}, u32[]{:S(2)}, u32[]{:S(2)}) collective-permute-start(bf16[129,16,128]{2,1,0:T(8,128)(2,1)S(1)} %get-tuple-element.24), channel_id=1, source_target_pairs={{8,16},{40,48},{56,64},{72,80},{104,112},{120,128},{136,144},{168,... | collective-permute-start | bytes 1585160 | tf_op jit(solution)/shard_map/ppermute | solution.py:388
  3.8 37.3 %collective-permute-start.5 = (bf16[129,16,128]{2,1,0:T(8,128)(2,1)S(1)}, bf16[129,16,128]{2,1,0:T(8,128)(2,1)S(1)}, u32[]{:S(2)}, u32[]{:S(2)}) collective-permute-start(bf16[129,16,128]{2,1,0:T(8,128)(2,1)S(1)} %get-tuple-element.25), channel_id=1, source_target_pairs={{0,8},{16,24},{32,40},{48,56},{64,72},{80,88},{96,104},{112,120},{... | collective-permute-start | bytes 1585160 | tf_op jit(solution)/shard_map/ppermute | solution.py:388
  8.3 16.4 %collective-permute-start.7 = (bf16[128,8,128]{2,1,0:T(8,128)(2,1)S(1)}, bf16[128,8,128]{2,1,0:T(8,128)(2,1)S(1)}, u32[]{:S(2)}, u32[]{:S(2)}) collective-permute-start(bf16[128,8,128]{2,1,0:T(8,128)(2,1)S(1)} %get-tuple-element.27), channel_id=1, source_target_pairs={{24,16},{88,80},{152,144},{216,208},{64,72},{128,136},{192,200},{2... | collective-permute-start | bytes 786440 | tf_op jit(solution)/shard_map/ppermute | solution.py:388
  9.9 10.5 %collective-permute-start.2 = (s16[2,128,128]{2,1,0:T(8,128)(2,1)S(1)}, s16[2,128,128]{2,1,0:T(8,128)(2,1)S(1)}, u32[]{:S(2)}, u32[]{:S(2)}) collective-permute-start(s16[2,128,128]{2,1,0:T(8,128)(2,1)S(1)} %packet.1), channel_id=1, source_target_pairs={{0,6},{1,7},{2,4},{3,5},{4,2},{5,3},{6,0},{7,1},{8,14},{9,15},{10,... | collective-permute-start | bytes 196616 | tf_op jit(solution)/shard_map/ppermute | solution.py:365
  11.9 8.5 %collective-permute-start.1 = (s16[2,128,128]{2,1,0:T(8,128)(2,1)S(1)}, s16[2,128,128]{2,1,0:T(8,128)(2,1)S(1)}, u32[]{:S(2)}, u32[]{:S(2)}) collective-permute-start(s16[2,128,128]{2,1,0:T(8,128)(2,1)S(1)} %packet.1), channel_id=1, source_target_pairs={{0,4},{1,5},{2,6},{3,7},{4,0},{5,1},{6,2},{7,3},{8,12},{9,13},{10,... | collective-permute-start | bytes 196616 | tf_op jit(solution)/shard_map/ppermute | solution.py:365
  20.4 4.3 %collective-permute-start = (s16[2,128,128]{2,1,0:T(8,128)(2,1)S(1)}, s16[2,128,128]{2,1,0:T(8,128)(2,1)S(1)}, u32[]{:S(2)}, u32[]{:S(2)}) collective-permute-start(s16[2,128,128]{2,1,0:T(8,128)(2,1)S(1)} %packet.1), channel_id=1, source_target_pairs={{0,2},{1,3},{2,0},{3,1},{4,6},{5,7},{6,4},{7,5},{8,10},{9,11},{10,... | collective-permute-start | bytes 196616 | tf_op jit(solution)/shard_map/ppermute | solution.py:365
  20.4 20.7 %collective-permute-start.6 = (bf16[129,8,128]{2,1,0:T(8,128)(2,1)S(1)}, bf16[129,8,128]{2,1,0:T(8,128)(2,1)S(1)}, u32[]{:S(2)}, u32[]{:S(2)}) collective-permute-start(bf16[129,8,128]{2,1,0:T(8,128)(2,1)S(1)} %get-tuple-element.26), channel_id=1, source_target_pairs={{24,32},{88,96},{152,160},{216,224},{64,56},{128,120},{192,184},{2... | collective-permute-start | bytes 792584 | tf_op jit(solution)/shard_map/ppermute | solution.py:388
  24.6 1.6 %collective-permute-start.3 = (s16[4,2,128,128]{3,2,1,0:T(8,128)(2,1)S(1)}, s16[4,2,128,128]{3,2,1,0:T(8,128)(2,1)S(1)}, u32[]{:S(2)}, u32[]{:S(2)}) collective-permute-start(s16[4,2,128,128]{3,2,1,0:T(8,128)(2,1)S(1)} %pad_add_fusion.mine_ref), channel_id=1, source_target_pairs={{0,1},{1,0},{2,3},{3,2},{4,5},{5,4},{6,7},{7,6},{8,9},{9,8},{10,11... | collective-permute-start | bytes 786440 | tf_op jit(solution)/shard_map/ppermute | solution.py:365
  24.8 16.3 %collective-permute-start.8 = (bf16[128,8,128]{2,1,0:T(8,128)(2,1)S(1)}, bf16[128,8,128]{2,1,0:T(8,128)(2,1)S(1)}, u32[]{:S(2)}, u32[]{:S(2)}) collective-permute-start(bf16[128,8,128]{2,1,0:T(8,128)(2,1)S(1)} %collective-permute-done.7), channel_id=1, source_target_pairs={{16,32},{80,96},{144,160},{208,224},{72,56},{136,120},{200,184},{1... | collective-permute-start | bytes 786440 | tf_op jit(solution)/shard_map/ppermute | solution.py:388
  45.6 39.5 %all-to-all-start = ((f32[32,3,128]{2,1,0:T(4,128)}), f32[32,3,128]{2,1,0:T(4,128)S(1)}, u32[]{:S(2)}, u32[]{:S(2)}) async-start(f32[32,3,128]{2,1,0:T(4,128)} %get-tuple-element.31), calls=%async_computation | async-start | bytes 131072 | tf_op jit(solution)/shard_map/all_to_all | solution.py:510

commit v6 on v5

--- a/solution.py
+++ b/solution.py
@@ -211,6 +211,7 @@
     new_ref,
     part_ref,
     source_ref,
+    kept_ref,
     cells_ref,
     added_ref,
     all_ref,
@@ -236,6 +237,8 @@
         tiles = [
             pl.ds(pl.multiple_of(order_ref[block * N + j] * ROWS, ROWS), ROWS) for j in range(N)
         ]
+        for j in range(N):
+            kept_ref[block * N + j] = order_ref[block * N + j]
         conc = [cells_ref[tile, :] for tile in tiles]
         minus_system(m_ref, conc, lambda i, j: rate_ref[block, i, j])
         inverted(m_ref)
@@ -453,16 +456,17 @@
     mine = jnp.stack(mine)
     other = crossed(mine, 1)
 
-    factors, new_concentration, conc_part, source_near = pl.pallas_call(
+    factors, new_concentration, conc_part, source_near, order_near = pl.pallas_call(
         factor_kernel,
         out_shape=(
             pltpu.VMEM((blocks, N, N // 2, 2 * ROWS, LANES), jnp.float32),
-            jax.ShapeDtypeStruct((species, LANES), jnp.float32),
+            pltpu.VMEM((species, LANES), jnp.float32),
             pltpu.VMEM((ROWS, LANES), jnp.float32),
             pltpu.VMEM(source.shape, source.dtype),
+            pltpu.SMEM(species_order.shape, jnp.int32),
         ),
         in_specs=[SMEM, SMEM, VMEM, VMEM, VMEM, VMEM, ANY],
-        out_specs=(VMEM,) * 4,
+        out_specs=(VMEM,) * 4 + (SMEM,),
         scratch_shapes=[
             pltpu.VMEM((species * ROWS, LANES), jnp.float32),
             pltpu.VMEM((species * ROWS, LANES), jnp.float32),
@@ -494,7 +498,7 @@
         compiler_params=SMALL,
         name="apply",
     )(
-        far(species_order),
+        pltpu.with_memory_space_constraint(order_near, pltpu.SMEM),
         near(weights),
         near(s_near),
         near(t_near),

time: 86 us -> 85.4 us (level)
  Pallas kernels: 23.3 us -> 22.1 us
  transfers between devices with their start and end apart: 10 -> 10, of which waited for: 4 -> 4; matrix products, arithmetic and copies ran while one was open for 1% -> 2% of each run, Pallas kernels for 18% -> 18%
where the time goes in v6:
time: 85.4 us; the launch traced here: 85 us
  starting transfers between devices  38.3 us (45%)
  waiting for transfers between devices  22.2 us (26%)
  Pallas kernels  22.1 us (26%)
  local copies, waits for them, and re-layouts  1.6 us (2%)
    all_to_all x1, starting transfers between devices, step(): everything = lax.all_to_all(parts, 'cols', 0, 0, tiled=True)  27.6 us
    pallas_call x1, Pallas kernels, step(): pl.pallas_call(factor_kernel, out_shape=(pltpu.VMEM((blocks, N, N // 2, 2...  14.3 us
    ppermute x4, waiting for transfers between devices, crossed(): lax.ppermute(value, 'params', [(i, i ^ bits) for i in range(lax.axis_size...  11.4 us
    all_to_all x1, waiting for transfers between devices, step(): everything = lax.all_to_all(parts, 'cols', 0, 0, tiled=True)  10.8 us
    ppermute x5, starting transfers between devices, passed(): return lax.ppermute(value, 'cols', pairs)  7.16 us
    pallas_call x1, Pallas kernels, step(): pl.pallas_call(apply_kernel, out_shape=(pltpu.VMEM(s.shape, jnp.float32),...  3.8 us
    ppermute x4, starting transfers between devices, crossed(): lax.ppermute(value, 'params', [(i, i ^ bits) for i in range(lax.axis_size...  3.55 us
    pallas_call x1, Pallas kernels, step(): pl.pallas_call(message_kernel, out_shape=(message, message, pltpu.VMEM((s...  2.5 us
  transfers between devices with their start and end apart: 10, of which 4 were waited for; matrix products, arithmetic and copies ran while one was open for 2% of the time, Pallas kernels for 18%

profile of v6, /device:TPU:32, one launch (start us, length us, event | category | flops | bytes accessed | tf_op | source)
XLA Modules:
  0.0 85.0 jit_solution(10354427421466558438)
XLA Ops:
  0.6 2.5 %messages.1 = (bf16[129,16,128]{2,1,0:T(8,128)(2,1)S(1)}, bf16[129,16,128]{2,1,0:T(8,128)(2,1)S(1)}, bf16[129,8,128]{2,1,0:T(8,128)(2,1)S(1)}, bf16[128,8,128]{2...) custom-call(f32[8,128]{1,0:T(8,128)} %bitcast.19, ...), custom_call_target="tpu_custom_call" | custom-call | tf_op jit(solution)/shard_map/messages/pallas_call | solution.py:427
  3.1 0.7 collective-permute-start.4
  3.8 4.5 %collective-permute-start.5 = (bf16[129,16,128]{2,1,0:T(8,128)(2,1)S(1)}, bf16[129,16,128]{2,1,0:T(8,128)(2,1)S(1)}, u32[]{:S(2)}, u32[]{:S(2)}) collective-permute-start(bf16[129,16,128]{2,1,0:T(8,128)(2,1)S(1)} %get-tuple-element.27), channel_id=1, source_target_pairs={{0,8},{16,24},{32,40},{48,56},{64,72},{80,88},{96,104},{112,120},{... | collective-permute-start | bytes 1585160 | tf_op jit(solution)/shard_map/ppermute | solution.py:391
  8.3 0.7 collective-permute-start.7
  9.0 0.9 %packet.1 = s16[2,128,128]{2,1,0:T(8,128)(2,1)S(1)} custom-call(f32[128,128]{1,0:T(8,128)} %conc_ref.3, f32[128,128]{1,0:T(8,128)} %emis_ref.3), custom_call_target="tpu_custom_call" | custom-call | tf_op jit(solution)/shard_map/packet/pallas_call | solution.py:416
  9.9 2.0 %collective-permute-start.2 = (s16[2,128,128]{2,1,0:T(8,128)(2,1)S(1)}, s16[2,128,128]{2,1,0:T(8,128)(2,1)S(1)}, u32[]{:S(2)}, u32[]{:S(2)}) collective-permute-start(s16[2,128,128]{2,1,0:T(8,128)(2,1)S(1)} %packet.1), channel_id=1, source_target_pairs={{0,6},{1,7},{2,4},{3,5},{4,2},{5,3},{6,0},{7,1},{8,14},{9,15},{10,... | collective-permute-start | bytes 196616 | tf_op jit(solution)/shard_map/ppermute | solution.py:368
  11.9 1.5 %collective-permute-start.1 = (s16[2,128,128]{2,1,0:T(8,128)(2,1)S(1)}, s16[2,128,128]{2,1,0:T(8,128)(2,1)S(1)}, u32[]{:S(2)}, u32[]{:S(2)}) collective-permute-start(s16[2,128,128]{2,1,0:T(8,128)(2,1)S(1)} %packet.1), channel_id=1, source_target_pairs={{0,4},{1,5},{2,6},{3,7},{4,0},{5,1},{6,2},{7,3},{8,12},{9,13},{10,... | collective-permute-start | bytes 196616 | tf_op jit(solution)/shard_map/ppermute | solution.py:368
  13.4 7.0 %collective-permute-done.2 = s16[2,128,128]{2,1,0:T(8,128)(2,1)S(1)} collective-permute-done((s16[2,128,128]{2,1,0:T(8,128)(2,1)S(1)}, s16[2,128,128]{2,1,0:T(8,128)(2,1)S(1)}, u32[]{:S(2)}, u32[]{:S(2)}) %collective-permute-start.2) | collective-permute-done | bytes 65568 | tf_op jit(solution)/shard_map/ppermute | solution.py:368
  20.4 0.0 collective-permute-start
  20.4 0.0 collective-permute-done.1
  20.4 0.7 collective-permute-start.6
  21.0 3.6 %collective-permute-done = s16[2,128,128]{2,1,0:T(8,128)(2,1)S(1)} collective-permute-done((s16[2,128,128]{2,1,0:T(8,128)(2,1)S(1)}, s16[2,128,128]{2,1,0:T(8,128)(2,1)S(1)}, u32[]{:S(2)}, u32[]{:S(2)}) %collective-permute-start) | collective-permute-done | bytes 65568 | tf_op jit(solution)/shard_map/ppermute | solution.py:368
  24.6 0.1 collective-permute-start.3
  24.7 0.0 collective-permute-done.7
  24.8 0.7 collective-permute-start.8
  25.4 0.8 collective-permute-done.3.other_ref
  26.3 14.3 %factors.1 = (f32[8,16,8,16,128]{4,3,2,1,0:T(8,128)S(1)}, f32[128,128]{1,0:T(8,128)S(1)}, f32[8,128]{1,0:T(8,128)S(1)}, bf16[2,128,8,128]{3,2,1,0:T(8,128)(2,1)S(1)}, s32[128]{0:T(128)S(4)}) custom-call(s32[128]{0:T(128)} %order_ref.1, f32[8,16,16]{2,1,0:T(8,128)} %rate_ref.1, s16[4,2,128,128]{3,2,1,0:T(8,128)(2,1)S(1)} %pad_add_fusion.mine_ref, ...), custom_call_target="tpu_custom_call" | custom-call | tf_op jit(solution)/shard_map/factors/pallas_call | solution.py:459
  40.6 0.0 collective-permute-done.8.half_1_ref
  40.6 3.8 %apply.1 = (f32[2,128,8,128]{3,2,1,0:T(8,128)S(1)}, f32[32,3,128]{2,1,0:T(4,128)}) custom-call(s32[128]{0:T(128)S(4)} %get-tuple-element.21.order_ref, f32[5,8,128]{2,1,0:T(8,128)S(1)} %get-tuple-element.22.weights_ref, f32[2,128,8,128]{3,2,1,0:T(8,128)S(1)} %get-tuple-element.23.s_ref, f32[2,128,8,128]{3,2,1,0:T(8,128)S(1)} %get-tuple-element.24.t_ref, ...), custom_call_target="tpu_custom_call" | custom-call | tf_op jit(solution)/shard_map/apply/pallas_call | solution.py:489
  44.4 27.6 %all-to-all-start = ((f32[32,3,128]{2,1,0:T(4,128)}), f32[32,3,128]{2,1,0:T(4,128)S(1)}, u32[]{:S(2)}, u32[]{:S(2)}) async-start(f32[32,3,128]{2,1,0:T(4,128)} %get-tuple-element.33), calls=%async_computation | async-start | bytes 131072 | tf_op jit(solution)/shard_map/all_to_all | solution.py:514
  72.0 0.6 copy.14
  72.6 1.0 %copy.15 = f32[2,128,2,4,128]{4,3,2,1,0:T(4,128)} copy(f32[2,128,2,4,128]{4,3,2,1,0:T(4,128)S(1)} %bitcast.12) | data formatting | bytes 2097152
  73.6 10.8 %all-to-all-done.parts_ref = f32[32,3,128]{2,1,0:T(4,128)S(1)} async-done(((f32[32,3,128]{2,1,0:T(4,128)}), f32[32,3,128]{2,1,0:T(4,128)S(1)}, u32[]{:S(2)}, u32[]{:S(2)}) %all-to-all-start) | async-done | bytes 49184 | tf_op jit(solution)/shard_map/all_to_all | solution.py:514
  84.4 0.6 means.1
  (4 shorter events, 0.0 us)
Async XLA Ops:
  3.1 37.4 %collective-permute-start.4 = (bf16[129,16,128]{2,1,0:T(8,128)(2,1)S(1)}, bf16[129,16,128]{2,1,0:T(8,128)(2,1)S(1)}, u32[]{:S(2)}, u32[]{:S(2)}) collective-permute-start(bf16[129,16,128]{2,1,0:T(8,128)(2,1)S(1)} %get-tuple-element.26), channel_id=1, source_target_pairs={{8,16},{40,48},{56,64},{72,80},{104,112},{120,128},{136,144},{168,... | collective-permute-start | bytes 1585160 | tf_op jit(solution)/shard_map/ppermute | solution.py:391
  3.8 36.7 %collective-permute-start.5 = (bf16[129,16,128]{2,1,0:T(8,128)(2,1)S(1)}, bf16[129,16,128]{2,1,0:T(8,128)(2,1)S(1)}, u32[]{:S(2)}, u32[]{:S(2)}) collective-permute-start(bf16[129,16,128]{2,1,0:T(8,128)(2,1)S(1)} %get-tuple-element.27), channel_id=1, source_target_pairs={{0,8},{16,24},{32,40},{48,56},{64,72},{80,88},{96,104},{112,120},{... | collective-permute-start | bytes 1585160 | tf_op jit(solution)/shard_map/ppermute | solution.py:391
  8.3 16.4 %collective-permute-start.7 = (bf16[128,8,128]{2,1,0:T(8,128)(2,1)S(1)}, bf16[128,8,128]{2,1,0:T(8,128)(2,1)S(1)}, u32[]{:S(2)}, u32[]{:S(2)}) collective-permute-start(bf16[128,8,128]{2,1,0:T(8,128)(2,1)S(1)} %get-tuple-element.29), channel_id=1, source_target_pairs={{24,16},{88,80},{152,144},{216,208},{64,72},{128,136},{192,200},{2... | collective-permute-start | bytes 786440 | tf_op jit(solution)/shard_map/ppermute | solution.py:391
  9.9 10.5 %collective-permute-start.2 = (s16[2,128,128]{2,1,0:T(8,128)(2,1)S(1)}, s16[2,128,128]{2,1,0:T(8,128)(2,1)S(1)}, u32[]{:S(2)}, u32[]{:S(2)}) collective-permute-start(s16[2,128,128]{2,1,0:T(8,128)(2,1)S(1)} %packet.1), channel_id=1, source_target_pairs={{0,6},{1,7},{2,4},{3,5},{4,2},{5,3},{6,0},{7,1},{8,14},{9,15},{10,... | collective-permute-start | bytes 196616 | tf_op jit(solution)/shard_map/ppermute | solution.py:368
  11.9 8.5 %collective-permute-start.1 = (s16[2,128,128]{2,1,0:T(8,128)(2,1)S(1)}, s16[2,128,128]{2,1,0:T(8,128)(2,1)S(1)}, u32[]{:S(2)}, u32[]{:S(2)}) collective-permute-start(s16[2,128,128]{2,1,0:T(8,128)(2,1)S(1)} %packet.1), channel_id=1, source_target_pairs={{0,4},{1,5},{2,6},{3,7},{4,0},{5,1},{6,2},{7,3},{8,12},{9,13},{10,... | collective-permute-start | bytes 196616 | tf_op jit(solution)/shard_map/ppermute | solution.py:368
  20.4 4.3 %collective-permute-start = (s16[2,128,128]{2,1,0:T(8,128)(2,1)S(1)}, s16[2,128,128]{2,1,0:T(8,128)(2,1)S(1)}, u32[]{:S(2)}, u32[]{:S(2)}) collective-permute-start(s16[2,128,128]{2,1,0:T(8,128)(2,1)S(1)} %packet.1), channel_id=1, source_target_pairs={{0,2},{1,3},{2,0},{3,1},{4,6},{5,7},{6,4},{7,5},{8,10},{9,11},{10,... | collective-permute-start | bytes 196616 | tf_op jit(solution)/shard_map/ppermute | solution.py:368
  20.4 20.2 %collective-permute-start.6 = (bf16[129,8,128]{2,1,0:T(8,128)(2,1)S(1)}, bf16[129,8,128]{2,1,0:T(8,128)(2,1)S(1)}, u32[]{:S(2)}, u32[]{:S(2)}) collective-permute-start(bf16[129,8,128]{2,1,0:T(8,128)(2,1)S(1)} %get-tuple-element.28), channel_id=1, source_target_pairs={{24,32},{88,96},{152,160},{216,224},{64,56},{128,120},{192,184},{2... | collective-permute-start | bytes 792584 | tf_op jit(solution)/shard_map/ppermute | solution.py:391
  24.6 1.6 %collective-permute-start.3 = (s16[4,2,128,128]{3,2,1,0:T(8,128)(2,1)S(1)}, s16[4,2,128,128]{3,2,1,0:T(8,128)(2,1)S(1)}, u32[]{:S(2)}, u32[]{:S(2)}) collective-permute-start(s16[4,2,128,128]{3,2,1,0:T(8,128)(2,1)S(1)} %pad_add_fusion.mine_ref), channel_id=1, source_target_pairs={{0,1},{1,0},{2,3},{3,2},{4,5},{5,4},{6,7},{7,6},{8,9},{9,8},{10,11... | collective-permute-start | bytes 786440 | tf_op jit(solution)/shard_map/ppermute | solution.py:368
  24.8 15.8 %collective-permute-start.8 = (bf16[128,8,128]{2,1,0:T(8,128)(2,1)S(1)}, bf16[128,8,128]{2,1,0:T(8,128)(2,1)S(1)}, u32[]{:S(2)}, u32[]{:S(2)}) collective-permute-start(bf16[128,8,128]{2,1,0:T(8,128)(2,1)S(1)} %collective-permute-done.7), channel_id=1, source_target_pairs={{16,32},{80,96},{144,160},{208,224},{72,56},{136,120},{200,184},{1... | collective-permute-start | bytes 786440 | tf_op jit(solution)/shard_map/ppermute | solution.py:391
  44.4 40.0 %all-to-all-start = ((f32[32,3,128]{2,1,0:T(4,128)}), f32[32,3,128]{2,1,0:T(4,128)S(1)}, u32[]{:S(2)}, u32[]{:S(2)}) async-start(f32[32,3,128]{2,1,0:T(4,128)} %get-tuple-element.33), calls=%async_computation | async-start | bytes 131072 | tf_op jit(solution)/shard_map/all_to_all | solution.py:514

commit v7 on v5

--- a/solution.py
+++ b/solution.py
@@ -107,7 +107,9 @@
     return (code.astype(jnp.int32).astype(jnp.float32) + CENTRE) * (1.0 / TOP)
 
 
-def packet_kernel(conc_ref, emis_ref, packet_ref):
+def packet_kernel(conc_ref, emis_ref, packet_ref, near_ref):
+    near_ref[0] = conc_ref[...]
+    near_ref[1] = emis_ref[...]
     packet_ref[0] = coded(jnp.log(conc_ref[...] * (1.0 / LEAST)) * (1.0 / SPAN))
     packet_ref[1] = coded(emis_ref[...])
 
@@ -118,6 +120,8 @@
     cy_hbm,
     uy_hbm,
     s_hbm,
+    order_hbm,
+    rate_hbm,
     a_ref,
     b_ref,
     half_0_ref,
@@ -125,10 +129,13 @@
     s_ref,
     t_ref,
     weights_ref,
+    order_ref,
+    rate_ref,
     reals_ref,
     flags_ref,
     wind_sem,
     sems,
+    table_sem,
 ):
     species = s_ref.shape[1]
     size = species // CHUNKS
@@ -148,10 +155,16 @@
             )
         )
     ]
+    tables = (
+        pltpu.make_async_copy(order_hbm, order_ref, table_sem.at[0]),
+        pltpu.make_async_copy(rate_hbm, rate_ref, table_sem.at[1]),
+    )
     for wind in winds:
         wind.start()
     for c in range(CHUNKS):
         copy(c).start()
+    for table in tables:
+        table.start()
     for wind in winds:
         wind.wait()
     first, up_x, down_x, weights = coefficients(
@@ -198,14 +211,16 @@
     def _():
         work(b_ref, a_ref, False)
 
+    for table in tables:
+        table.wait()
+
 
 def factor_kernel(
     order_ref,
     rate_ref,
     mine_ref,
     other_ref,
-    conc_ref,
-    emis_ref,
+    own_ref,
     source_hbm,
     factor_ref,
     new_ref,
@@ -226,8 +241,8 @@
         for core, ref in enumerate((mine_ref, other_ref)):
             rows = pl.ds(place ^ (2 * k + core), species, stride=ROWS)
             if k == 0 and core == 0:
-                cells_ref[rows, :] = conc_ref[...]
-                added_ref[rows, :] = emis_ref[...]
+                cells_ref[rows, :] = own_ref[0]
+                added_ref[rows, :] = own_ref[1]
             else:
                 cells_ref[rows, :] = LEAST * jnp.exp(SPAN * decoded(ref[k, 0]))
                 added_ref[rows, :] = decoded(ref[k, 1])
@@ -357,6 +372,10 @@
     return pltpu.with_memory_space_constraint(value, pltpu.VMEM)
 
 
+def scalars(value):
+    return pltpu.with_memory_space_constraint(value, pltpu.SMEM)
+
+
 def far(value):
     return pltpu.with_memory_space_constraint(value, pltpu.HBM)
 
@@ -410,18 +429,21 @@
 
     links = lax.axis_size("params") // 2
     message = pltpu.VMEM((species + 1, 2 * ROWS, LANES), jnp.bfloat16)
-    packet = pl.pallas_call(
+    packet, cells_near = pl.pallas_call(
         packet_kernel,
-        out_shape=pltpu.VMEM((2, species, LANES), jnp.int16),
+        out_shape=(
+            pltpu.VMEM((2, species, LANES), jnp.int16),
+            pltpu.VMEM((2, species, LANES), jnp.float32),
+        ),
         in_specs=[VMEM, VMEM],
-        out_specs=VMEM,
+        out_specs=(VMEM, VMEM),
         compiler_params=SMALL,
         name="packet",
     )(far(concentration), far(emissions))
     mine = [packet]
     for k in range(1, links):
         mine.append(crossed(packet, 2 * k))
-    a, b, half_0, half_1, s_near, t_near, weights = pl.pallas_call(
+    a, b, half_0, half_1, s_near, t_near, weights, order_near, rate_near = pl.pallas_call(
         message_kernel,
         out_shape=(
             message,
@@ -431,18 +453,21 @@
             pltpu.VMEM(s.shape, jnp.float32),
             pltpu.VMEM(s.shape, jnp.float32),
             pltpu.VMEM((5, ROWS, LANES), jnp.float32),
+            pltpu.SMEM(species_order.shape, jnp.int32),
+            pltpu.SMEM(rate_table.shape, jnp.float32),
         ),
-        in_specs=[ANY] * 5,
-        out_specs=(VMEM,) * 7,
+        in_specs=[ANY] * 7,
+        out_specs=(VMEM,) * 7 + (SMEM,) * 2,
         scratch_shapes=[
             pltpu.VMEM((2, ROWS, LANES), jnp.float32),
             pltpu.VMEM((2, ROWS, LANES), jnp.int32),
             pltpu.SemaphoreType.DMA((4,)),
             pltpu.SemaphoreType.DMA((CHUNKS,)),
+            pltpu.SemaphoreType.DMA((2,)),
         ],
         compiler_params=SMALL,
         name="messages",
-    )(*map(far, winds), far(s))
+    )(*map(far, winds), far(s), far(species_order), far(rate_table))
     far_edges = leaps()
     direct = [(u, v) for u, _, v in far_edges]
     a = passed(a, [edge for edge in edges(1) if edge not in direct])
@@ -457,11 +482,11 @@
         factor_kernel,
         out_shape=(
             pltpu.VMEM((blocks, N, N // 2, 2 * ROWS, LANES), jnp.float32),
-            jax.ShapeDtypeStruct((species, LANES), jnp.float32),
+            pltpu.VMEM((species, LANES), jnp.float32),
             pltpu.VMEM((ROWS, LANES), jnp.float32),
             pltpu.VMEM(source.shape, source.dtype),
         ),
-        in_specs=[SMEM, SMEM, VMEM, VMEM, VMEM, VMEM, ANY],
+        in_specs=[SMEM, SMEM, VMEM, VMEM, VMEM, ANY],
         out_specs=(VMEM,) * 4,
         scratch_shapes=[
             pltpu.VMEM((species * ROWS, LANES), jnp.float32),
@@ -473,12 +498,11 @@
         compiler_params=SMALL,
         name="factors",
     )(
-        far(species_order),
-        far(rate_table),
+        scalars(order_near),
+        scalars(rate_near),
         near(mine),
         near(other),
-        far(concentration),
-        far(emissions),
+        near(cells_near),
         far(source),
     )
 
@@ -494,7 +518,7 @@
         compiler_params=SMALL,
         name="apply",
     )(
-        far(species_order),
+        scalars(order_near),
         near(weights),
         near(s_near),
         near(t_near),

time: 86 us -> 85.3 us (level)
  Pallas kernels: 23.3 us -> 20.4 us
  starting transfers between devices: 37.8 us -> 40 us
    pallas_call x1, Pallas kernels: 14.8 us -> 12.5 us  [step(): pl.pallas_call(factor_kernel, out_shape=(pltpu.VMEM((blocks, N, N // 2, 2...]
    all_to_all x1, starting transfers between devices: 27.1 us -> 29.3 us  [step(): everything = lax.all_to_all(parts, 'cols', 0, 0, tiled=True)]
  transfers between devices with their start and end apart: 10 -> 10, of which waited for: 4 -> 4; matrix products, arithmetic and copies ran while one was open for 1% -> 2% of each run, Pallas kernels for 18% -> 16%
where the time goes in v7:
time: 85.3 us; the launch traced here: 85 us
  starting transfers between devices  40 us (47%)
  waiting for transfers between devices  22.2 us (26%)
  Pallas kernels  20.4 us (24%)
  local copies, waits for them, and re-layouts  1.6 us (2%)
    all_to_all x1, starting transfers between devices, step(): everything = lax.all_to_all(parts, 'cols', 0, 0, tiled=True)  29.3 us
    pallas_call x1, Pallas kernels, step(): pl.pallas_call(factor_kernel, out_shape=(pltpu.VMEM((blocks, N, N // 2, 2...  12.5 us
    ppermute x4, waiting for transfers between devices, crossed(): lax.ppermute(value, 'params', [(i, i ^ bits) for i in range(lax.axis_size...  11.4 us
    all_to_all x1, waiting for transfers between devices, step(): everything = lax.all_to_all(parts, 'cols', 0, 0, tiled=True)  10.8 us
    ppermute x5, starting transfers between devices, passed(): return lax.ppermute(value, 'cols', pairs)  7.16 us
    pallas_call x1, Pallas kernels, step(): pl.pallas_call(apply_kernel, out_shape=(pltpu.VMEM(s.shape, jnp.float32),...  3.8 us
    ppermute x4, starting transfers between devices, crossed(): lax.ppermute(value, 'params', [(i, i ^ bits) for i in range(lax.axis_size...  3.55 us
    pallas_call x1, Pallas kernels, step(): pl.pallas_call(message_kernel, out_shape=(message, message, pltpu.VMEM((s...  2.54 us
  transfers between devices with their start and end apart: 10, of which 4 were waited for; matrix products, arithmetic and copies ran while one was open for 2% of the time, Pallas kernels for 16%

profile of v7, /device:TPU:32, one launch (start us, length us, event | category | flops | bytes accessed | tf_op | source)
XLA Modules:
  0.0 85.0 jit_solution(16781112728136804534)
XLA Ops:
  0.6 2.5 %messages.1 = (bf16[129,16,128]{2,1,0:T(8,128)(2,1)S(1)}, bf16[129,16,128]{2,1,0:T(8,128)(2,1)S(1)}, bf16[129,8,128]{2,1,0:T(8,128)(2,1)S(1)}, bf16[128,8,128]{2...) custom-call(f32[8,128]{1,0:T(8,128)} %bitcast.19, ...), custom_call_target="tpu_custom_call" | custom-call | tf_op jit(solution)/shard_map/messages/pallas_call | solution.py:446
  3.2 0.7 collective-permute-start.4
  3.9 4.5 %collective-permute-start.5 = (bf16[129,16,128]{2,1,0:T(8,128)(2,1)S(1)}, bf16[129,16,128]{2,1,0:T(8,128)(2,1)S(1)}, u32[]{:S(2)}, u32[]{:S(2)}) collective-permute-start(bf16[129,16,128]{2,1,0:T(8,128)(2,1)S(1)} %get-tuple-element.33), channel_id=1, source_target_pairs={{0,8},{16,24},{32,40},{48,56},{64,72},{80,88},{96,104},{112,120},{... | collective-permute-start | bytes 1585160 | tf_op jit(solution)/shard_map/ppermute | solution.py:407
  8.3 0.7 collective-permute-start.7
  9.0 0.9 %packet.1 = (s16[2,128,128]{2,1,0:T(8,128)(2,1)S(1)}, f32[2,128,128]{2,1,0:T(8,128)S(1)}) custom-call(f32[128,128]{1,0:T(8,128)} %conc_ref.1, f32[128,128]{1,0:T(8,128)} %emis_ref.1), custom_call_target="tpu_custom_call" | custom-call | tf_op jit(solution)/shard_map/packet/pallas_call | solution.py:432
  9.9 2.0 %collective-permute-start.2 = (s16[2,128,128]{2,1,0:T(8,128)(2,1)S(1)}, s16[2,128,128]{2,1,0:T(8,128)(2,1)S(1)}, u32[]{:S(2)}, u32[]{:S(2)}) collective-permute-start(s16[2,128,128]{2,1,0:T(8,128)(2,1)S(1)} %get-tuple-element.25), channel_id=1, source_target_pairs={{0,6},{1,7},{2,4},{3,5},{4,2},{5,3},{6,0},{7,1},{8,14},{9,15},{10,... | collective-permute-start | bytes 196616 | tf_op jit(solution)/shard_map/ppermute | solution.py:384
  11.9 1.5 %collective-permute-start.1 = (s16[2,128,128]{2,1,0:T(8,128)(2,1)S(1)}, s16[2,128,128]{2,1,0:T(8,128)(2,1)S(1)}, u32[]{:S(2)}, u32[]{:S(2)}) collective-permute-start(s16[2,128,128]{2,1,0:T(8,128)(2,1)S(1)} %get-tuple-element.25), channel_id=1, source_target_pairs={{0,4},{1,5},{2,6},{3,7},{4,0},{5,1},{6,2},{7,3},{8,12},{9,13},{10,... | collective-permute-start | bytes 196616 | tf_op jit(solution)/shard_map/ppermute | solution.py:384
  13.4 7.0 %collective-permute-done.2 = s16[2,128,128]{2,1,0:T(8,128)(2,1)S(1)} collective-permute-done((s16[2,128,128]{2,1,0:T(8,128)(2,1)S(1)}, s16[2,128,128]{2,1,0:T(8,128)(2,1)S(1)}, u32[]{:S(2)}, u32[]{:S(2)}) %collective-permute-start.2) | collective-permute-done | bytes 65568 | tf_op jit(solution)/shard_map/ppermute | solution.py:384
  20.4 0.0 collective-permute-start
  20.4 0.0 collective-permute-done.1
  20.4 0.7 collective-permute-start.6
  21.1 3.6 %collective-permute-done = s16[2,128,128]{2,1,0:T(8,128)(2,1)S(1)} collective-permute-done((s16[2,128,128]{2,1,0:T(8,128)(2,1)S(1)}, s16[2,128,128]{2,1,0:T(8,128)(2,1)S(1)}, u32[]{:S(2)}, u32[]{:S(2)}) %collective-permute-start) | collective-permute-done | bytes 65568 | tf_op jit(solution)/shard_map/ppermute | solution.py:384
  24.7 0.1 collective-permute-start.3
  24.8 0.7 collective-permute-start.8
  25.5 0.8 collective-permute-done.3.other_ref
  26.3 12.5 %factors.1 = (f32[8,16,8,16,128]{4,3,2,1,0:T(8,128)S(1)}, f32[128,128]{1,0:T(8,128)S(1)}, f32[8,128]{1,0:T(8,128)S(1)}, bf16[2,128,8,128]{3,2,1,0:T(8,128)(2,1)S(1)}) custom-call(s32[128]{0:T(128)S(4)} %get-tuple-element.23.order_ref, f32[8,16,16]{2,1,0:T(8,128)S(4)} %get-tuple-element.24.rate_ref, s16[4,2,128,128]{3,2,1,0:T(8,128)(2,1)S(1)} %pad_add_fusion.mine_ref, ...), custom_call_target="tpu_custom_call" | custom-call | tf_op jit(solution)/shard_map/factors/pallas_call | solution.py:481
  38.9 0.0 collective-permute-done.8.half_1_ref
  38.9 0.0 collective-permute-done.4.a_ref
  38.9 3.8 %apply.1 = (f32[2,128,8,128]{3,2,1,0:T(8,128)S(1)}, f32[32,3,128]{2,1,0:T(4,128)}) custom-call(s32[128]{0:T(128)S(4)} %get-tuple-element.23.order_ref, f32[5,8,128]{2,1,0:T(8,128)S(1)} %get-tuple-element.28.weights_ref, f32[2,128,8,128]{3,2,1,0:T(8,128)S(1)} %get-tuple-element.29.s_ref, f32[2,128,8,128]{3,2,1,0:T(8,128)S(1)} %get-tuple-element.30.t_ref, ...), custom_call_target="tpu_custom_call" | custom-call | tf_op jit(solution)/shard_map/apply/pallas_call | solution.py:509
  42.7 29.3 %all-to-all-start = ((f32[32,3,128]{2,1,0:T(4,128)}), f32[32,3,128]{2,1,0:T(4,128)S(1)}, u32[]{:S(2)}, u32[]{:S(2)}) async-start(f32[32,3,128]{2,1,0:T(4,128)} %get-tuple-element.39), calls=%async_computation | async-start | bytes 131072 | tf_op jit(solution)/shard_map/all_to_all | solution.py:534
  72.0 0.6 copy.14
  72.7 1.0 %copy.15 = f32[2,128,2,4,128]{4,3,2,1,0:T(4,128)} copy(f32[2,128,2,4,128]{4,3,2,1,0:T(4,128)S(1)} %bitcast.12) | data formatting | bytes 2097152
  73.6 10.8 %all-to-all-done.parts_ref = f32[32,3,128]{2,1,0:T(4,128)S(1)} async-done(((f32[32,3,128]{2,1,0:T(4,128)}), f32[32,3,128]{2,1,0:T(4,128)S(1)}, u32[]{:S(2)}, u32[]{:S(2)}) %all-to-all-start) | async-done | bytes 49184 | tf_op jit(solution)/shard_map/all_to_all | solution.py:534
  84.4 0.6 means.1
  (4 shorter events, 0.0 us)
Async XLA Ops:
  3.2 35.7 %collective-permute-start.4 = (bf16[129,16,128]{2,1,0:T(8,128)(2,1)S(1)}, bf16[129,16,128]{2,1,0:T(8,128)(2,1)S(1)}, u32[]{:S(2)}, u32[]{:S(2)}) collective-permute-start(bf16[129,16,128]{2,1,0:T(8,128)(2,1)S(1)} %get-tuple-element.32), channel_id=1, source_target_pairs={{8,16},{40,48},{56,64},{72,80},{104,112},{120,128},{136,144},{168,... | collective-permute-start | bytes 1585160 | tf_op jit(solution)/shard_map/ppermute | solution.py:407
  3.9 35.0 %collective-permute-start.5 = (bf16[129,16,128]{2,1,0:T(8,128)(2,1)S(1)}, bf16[129,16,128]{2,1,0:T(8,128)(2,1)S(1)}, u32[]{:S(2)}, u32[]{:S(2)}) collective-permute-start(bf16[129,16,128]{2,1,0:T(8,128)(2,1)S(1)} %get-tuple-element.33), channel_id=1, source_target_pairs={{0,8},{16,24},{32,40},{48,56},{64,72},{80,88},{96,104},{112,120},{... | collective-permute-start | bytes 1585160 | tf_op jit(solution)/shard_map/ppermute | solution.py:407
  8.3 16.5 %collective-permute-start.7 = (bf16[128,8,128]{2,1,0:T(8,128)(2,1)S(1)}, bf16[128,8,128]{2,1,0:T(8,128)(2,1)S(1)}, u32[]{:S(2)}, u32[]{:S(2)}) collective-permute-start(bf16[128,8,128]{2,1,0:T(8,128)(2,1)S(1)} %get-tuple-element.35), channel_id=1, source_target_pairs={{24,16},{88,80},{152,144},{216,208},{64,72},{128,136},{192,200},{2... | collective-permute-start | bytes 786440 | tf_op jit(solution)/shard_map/ppermute | solution.py:407
  9.9 10.5 %collective-permute-start.2 = (s16[2,128,128]{2,1,0:T(8,128)(2,1)S(1)}, s16[2,128,128]{2,1,0:T(8,128)(2,1)S(1)}, u32[]{:S(2)}, u32[]{:S(2)}) collective-permute-start(s16[2,128,128]{2,1,0:T(8,128)(2,1)S(1)} %get-tuple-element.25), channel_id=1, source_target_pairs={{0,6},{1,7},{2,4},{3,5},{4,2},{5,3},{6,0},{7,1},{8,14},{9,15},{10,... | collective-permute-start | bytes 196616 | tf_op jit(solution)/shard_map/ppermute | solution.py:384
  11.9 8.5 %collective-permute-start.1 = (s16[2,128,128]{2,1,0:T(8,128)(2,1)S(1)}, s16[2,128,128]{2,1,0:T(8,128)(2,1)S(1)}, u32[]{:S(2)}, u32[]{:S(2)}) collective-permute-start(s16[2,128,128]{2,1,0:T(8,128)(2,1)S(1)} %get-tuple-element.25), channel_id=1, source_target_pairs={{0,4},{1,5},{2,6},{3,7},{4,0},{5,1},{6,2},{7,3},{8,12},{9,13},{10,... | collective-permute-start | bytes 196616 | tf_op jit(solution)/shard_map/ppermute | solution.py:384
  20.4 4.3 %collective-permute-start = (s16[2,128,128]{2,1,0:T(8,128)(2,1)S(1)}, s16[2,128,128]{2,1,0:T(8,128)(2,1)S(1)}, u32[]{:S(2)}, u32[]{:S(2)}) collective-permute-start(s16[2,128,128]{2,1,0:T(8,128)(2,1)S(1)} %get-tuple-element.25), channel_id=1, source_target_pairs={{0,2},{1,3},{2,0},{3,1},{4,6},{5,7},{6,4},{7,5},{8,10},{9,11},{10,... | collective-permute-start | bytes 196616 | tf_op jit(solution)/shard_map/ppermute | solution.py:384
  20.4 18.4 %collective-permute-start.6 = (bf16[129,8,128]{2,1,0:T(8,128)(2,1)S(1)}, bf16[129,8,128]{2,1,0:T(8,128)(2,1)S(1)}, u32[]{:S(2)}, u32[]{:S(2)}) collective-permute-start(bf16[129,8,128]{2,1,0:T(8,128)(2,1)S(1)} %get-tuple-element.34), channel_id=1, source_target_pairs={{24,32},{88,96},{152,160},{216,224},{64,56},{128,120},{192,184},{2... | collective-permute-start | bytes 792584 | tf_op jit(solution)/shard_map/ppermute | solution.py:407
  24.7 1.6 %collective-permute-start.3 = (s16[4,2,128,128]{3,2,1,0:T(8,128)(2,1)S(1)}, s16[4,2,128,128]{3,2,1,0:T(8,128)(2,1)S(1)}, u32[]{:S(2)}, u32[]{:S(2)}) collective-permute-start(s16[4,2,128,128]{3,2,1,0:T(8,128)(2,1)S(1)} %pad_add_fusion.mine_ref), channel_id=1, source_target_pairs={{0,1},{1,0},{2,3},{3,2},{4,5},{5,4},{6,7},{7,6},{8,9},{9,8},{10,11... | collective-permute-start | bytes 786440 | tf_op jit(solution)/shard_map/ppermute | solution.py:384
  24.8 14.1 %collective-permute-start.8 = (bf16[128,8,128]{2,1,0:T(8,128)(2,1)S(1)}, bf16[128,8,128]{2,1,0:T(8,128)(2,1)S(1)}, u32[]{:S(2)}, u32[]{:S(2)}) collective-permute-start(bf16[128,8,128]{2,1,0:T(8,128)(2,1)S(1)} %collective-permute-done.7), channel_id=1, source_target_pairs={{16,32},{80,96},{144,160},{208,224},{72,56},{136,120},{200,184},{1... | collective-permute-start | bytes 786440 | tf_op jit(solution)/shard_map/ppermute | solution.py:407
  42.7 41.7 %all-to-all-start = ((f32[32,3,128]{2,1,0:T(4,128)}), f32[32,3,128]{2,1,0:T(4,128)S(1)}, u32[]{:S(2)}, u32[]{:S(2)}) async-start(f32[32,3,128]{2,1,0:T(4,128)} %get-tuple-element.39), calls=%async_computation | async-start | bytes 131072 | tf_op jit(solution)/shard_map/all_to_all | solution.py:534
